TPU v7x, 32 devices: a 4x4x1 block of a 4x4x8 slice. The times are simulated.
32 devices in a mesh: dp: 1 (over z), ty: 4 (over y), tx: 8 (over x, core).
Axes of the slice: x: 4, y: 4, z: 1, core: 2. Of those that a mesh axis runs over, the one named last changes fastest.
The devices are a block of a 4x4x8 slice.
Arguments:
- x_in: bfloat16 [128, 6144], P('dp', 'tx')
- seq_lens: int32 [128], P('dp')
- k_cache: bfloat16 [128, 4096, 128], P(('dp', 'ty', 'tx'))
- v_cache: bfloat16 [128, 4096, 128], P(('dp', 'ty', 'tx'))
- ln_gamma: float32 [6144], P('tx')
- w_query: bfloat16 [6144, 6144], P('tx', 'ty')
- w_key: bfloat16 [6144, 128], P('tx')
- w_value: bfloat16 [6144, 128], P('tx')
- w_gate: bfloat16 [6144, 24576], P('tx', 'ty')
- w_up: bfloat16 [6144, 24576], P('tx', 'ty')
- w_out: bfloat16 [6144, 6144], P('ty', 'tx')
- w_down: bfloat16 [24576, 6144], P('ty', 'tx')
Outputs:
- output 1: bfloat16 [128, 6144], P('dp', 'tx')
- output 2: bfloat16 [128, 4096, 128], P(('dp', 'ty', 'tx'))
- output 3: bfloat16 [128, 4096, 128], P(('dp', 'ty', 'tx'))
All inputs are finite; a program needn't handle non-finite values.
Results may differ from a plain program's by a relative error of at most 0.0159228.
Values are sent between devices in bfloat16 or wider.
A program may use at most 768 MiB of HBM per device.

v0:
```python
import jax
import jax.numpy as jnp
from jax import lax
from jax.sharding import PartitionSpec as P

EPSILON = 1e-6
ROPE_BASE = 10000.0


def rope_tables(positions, head_dim):
    half_dim = head_dim // 2
    inv_freqs = ROPE_BASE ** (-(jnp.arange(half_dim, dtype=jnp.float32) * 2.0) / head_dim)
    angles = positions.astype(jnp.float32)[:, None] * inv_freqs[None, :]
    return jnp.cos(angles), jnp.sin(angles)


def rope_apply(vals, cosines, sines):
    half_dim = vals.shape[-1] // 2
    first = vals[..., :half_dim]
    second = vals[..., half_dim:]
    return jnp.concatenate([first * cosines - second * sines, second * cosines + first * sines], axis=-1)


def solution(mesh):
    ty_size = mesh.shape["ty"]
    tx_size = mesh.shape["tx"]
    cache_spec = P(("dp", "ty", "tx"), None, None)

    def layer_shard(x_blk, lens_part, k_blk, v_blk, gamma_blk, w_query, w_key, w_value, w_gate, w_up, w_out, w_down):
        rows = x_blk.shape[0]
        d_model = x_blk.shape[1] * tx_size
        seq_block, ctx_len, head_dim = k_blk.shape
        local_heads = w_query.shape[1] // head_dim
        row_idx = lax.axis_index("ty")
        col_idx = lax.axis_index("tx")

        x_f32 = x_blk.astype(jnp.float32)
        row_stats = jnp.stack([jnp.sum(x_f32, axis=-1), jnp.sum(x_f32 * x_f32, axis=-1)], axis=-1)
        row_stats = lax.psum(row_stats, "tx")
        row_mean = row_stats[:, 0] / d_model
        row_var = row_stats[:, 1] / d_model - row_mean * row_mean
        normed = ((x_f32 - row_mean[:, None]) * lax.rsqrt(row_var[:, None] + EPSILON) * gamma_blk[None, :]).astype(jnp.bfloat16)

        partials = tuple(jnp.dot(normed, weight, preferred_element_type=jnp.float32).astype(jnp.bfloat16) for weight in (w_query, w_key, w_value, w_gate, w_up))
        q_sum, k_sum, v_new, gate, up_proj = lax.psum(partials, "tx")

        cosines, sines = rope_tables(lens_part, head_dim)
        queries = rope_apply(q_sum.astype(jnp.float32).reshape(rows, local_heads, head_dim), cosines[:, None, :], sines[:, None, :]).astype(jnp.bfloat16)
        k_new = rope_apply(k_sum.astype(jnp.float32), cosines, sines).astype(jnp.bfloat16)

        block_start = (row_idx * tx_size + col_idx) * seq_block
        lens_own = lax.dynamic_slice_in_dim(lens_part, block_start, seq_block)
        k_own = lax.dynamic_slice_in_dim(k_new, block_start, seq_block)
        v_own = lax.dynamic_slice_in_dim(v_new, block_start, seq_block)
        positions = jnp.arange(ctx_len)
        at_slot = positions[None, :, None] == lens_own[:, None, None]
        k_out = jnp.where(at_slot, k_own[:, None, :], k_blk)
        v_out = jnp.where(at_slot, v_own[:, None, :], v_blk)

        q_column = lax.dynamic_index_in_dim(queries.reshape(ty_size, tx_size, seq_block, local_heads, head_dim), col_idx, axis=1, keepdims=False)
        q_owned = lax.all_to_all(q_column, "ty", 0, 0, tiled=True)
        scores = jnp.einsum("gbhd,btd->gbht", q_owned, k_out, preferred_element_type=jnp.float32) * (head_dim ** -0.5)
        in_range = positions[None, None, None, :] <= lens_own[None, :, None, None]
        scores = jnp.where(in_range, scores, -1e30)
        att_probs = jax.nn.softmax(scores, axis=-1).astype(jnp.bfloat16)
        att_owned = jnp.einsum("gbht,btd->gbhd", att_probs, v_out, preferred_element_type=jnp.float32).astype(jnp.bfloat16)
        att_column = lax.all_to_all(att_owned, "ty", 0, 0, tiled=True)
        att_rows = lax.all_gather(att_column, "tx", axis=1, tiled=False).reshape(rows, local_heads * head_dim)

        mlp_act = (jax.nn.silu(gate.astype(jnp.float32)) * up_proj.astype(jnp.float32)).astype(jnp.bfloat16)
        part_out = jnp.dot(att_rows, w_out, preferred_element_type=jnp.float32) + jnp.dot(mlp_act, w_down, preferred_element_type=jnp.float32)
        out_sum = lax.psum(part_out.astype(jnp.bfloat16), "ty")
        y_blk = (x_f32 + out_sum.astype(jnp.float32)).astype(jnp.bfloat16)
        return y_blk, k_out, v_out

    in_specs = (P("dp", "tx"), P("dp"), cache_spec, cache_spec, P("tx"), P("tx", "ty"), P("tx", None), P("tx", None), P("tx", "ty"), P("tx", "ty"), P("ty", "tx"), P("ty", "tx"))
    out_specs = (P("dp", "tx"), cache_spec, cache_spec)
    return jax.shard_map(layer_shard, mesh=mesh, in_specs=in_specs, out_specs=out_specs, check_vma=False)
```

profile of v0, /device:TPU:97, one launch (start us, length us, event | category | flops | bytes accessed | tf_op | source)
XLA Modules:
  0.0 260.4 jit_solution(9511444203881993326)
XLA Ops:
  7.3 1.2 convert_reduce_fusion
  8.5 13.9 %psum.49 = f32[128,2]{0,1:T(2,128)S(1)} all-reduce(f32[128,2]{0,1:T(2,128)S(1)} %pad_maximum_fusion), channel_id=1, replica_groups=mesh['dp'=1,'ty'=4,'tx'=8] {'tx'}, use_global_device_ids=true, to_apply=%region_2.0 | all-reduce | flops 256 | bytes 2048 | tf_op jit(solution)/shard_map/psum | solution.py:39
  22.4 2.0 convolution_convert_fusion.3
  24.3 1.9 convolution_convert_fusion.4
  26.4 6.5 %convolution_convert_fusion.1 = bf16[128,6144]{1,0:T(8,128)(2,1)} fusion(bf16[768,6144]{1,0:T(8,128)(2,1)} %param.20, bf16[128,768]{1,0:T(8,128)(2,1)} %param.12, f32[768]{0:T(1024)} %param.16, f32[128]{0:T(128)S(1)} %get-tuple-element.21, f32[128]{0:T(128)S(1)} %get-tuple-element.20), kind=kOutput, calls=%fused_computation.2 | convolution fusion | flops 1209237504 | bytes 11210752 | tf_op jit(solution)/shard_map/dot_general | solution.py:44
  33.0 0.1 copy-done.1
  33.1 2.6 convolution_convert_fusion
  35.7 0.5 convolution_convert_fusion.2
  36.2 0.9 copy.51
  37.4 0.7 iota_compare_fusion
  38.1 43.3 %all-reduce.8.cloned.1.call-done = (bf16[128,128]{0,1:T(8,128)(2,1)}, bf16[128,128]{1,0:T(8,128)(2,1)}) async-done(((bf16[128,128]{0,1:T(8,128)(2,1)}, bf16[128,128]{1,0:T(8,128)(2,1)}), (bf16[128,128]{0,1:T(8,128)(2,1)}, bf16[128,128]{1,0:T(8,128)(2,1)})) %all-reduce.8.cloned.1.call-update) | async-done | bytes 65552 | tf_op jit(solution)/shard_map/psum | solution.py:45
  81.4 0.8 convert_element_type.62
  82.1 0.2 multiply_cosine_fusion
  82.4 0.7 copy.50
  83.1 1.3 constant_dynamic-slice_fusion
  84.4 64.7 %all-reduce.10.cloned.1.call-done = (bf16[128,6144]{1,0:T(8,128)(2,1)}, bf16[128,6144]{1,0:T(8,128)(2,1)}, bf16[128,12,128]{0,2,1:T(8,128)(2,1)}) async-done(((bf16[128,6144]{1,0:T(8,128)(2,1)}, bf16[128,6144]{1,0:T(8,128)(2,1)}, bf16[128,12,128]{0,2,1:T(8,128)(2,1)}), (bf16[128,6144]{1,0:T(8,128)(2,1)}, bf16[128,6144]{1,0:T(8,128)(2,1)}, bf16[128,12,128]{0,2,1:T(8,128)(2,1)})) %all-reduce.10.cloned.1.call-update) | async-done | bytes 3538960 | tf_op jit(solution)/shard_map/psum | solution.py:45
  149.1 1.1 reshape.126
  150.2 0.1 add_convert_fusion
  150.3 0.2 copy.53
  150.5 0.2 copy.52
  150.8 0.7 copy_bitcast_fusion
  151.5 4.0 %all-to-all-start = ((bf16[4,4,12,128]{3,1,2,0:T(4,128)(2,1)}), bf16[4,4,12,128]{3,1,2,0:T(4,128)(2,1)S(1)}, u32[]{:S(2)}, u32[]{:S(2)}) async-start(bf16[4,4,12,128]{3,1,2,0:T(4,128)(2,1)} %copy_bitcast_fusion), calls=%async_computation | async-start | bytes 98304 | tf_op jit(solution)/shard_map/all_to_all | solution.py:61
  155.5 11.4 %broadcast_select_fusion.1 = (bf16[4,4096,128]{2,1,0:T(8,128)(2,1)}, bf16[4,4096,128]{2,1,0:T(8,128)(2,1)}) fusion(bf16[4,4096,128]{2,1,0:T(8,128)(2,1)} %param.15, pred[4,4096]{1,0:T(4,128)(4,1)S(1)} %get-tuple-element.23, bf16[4,128]{1,0:T(4,128)(2,1)} %constant_dynamic-slice_fusion, bf16[4,4096,128]{2,1,0:T(8,128)(2,1)} %param.14, bf16[4,128]{1,0:T(4,128)(2,1)} %copy.50), kind=kLoop, calls=%fused_computation.13 | loop fusion | flops 4194304 | bytes 16795648 | tf_op jit(solution)/shard_map/jit(_where)/select_n | solution.py:58
  166.9 6.2 %fusion.40 = (f32[4,4,12]{2,0,1:T(4,128)S(1)}, f32[4,4,12,4096]{3,2,0,1:T(8,128)}) fusion(bf16[4,4096,128]{2,1,0:T(8,128)(2,1)} %get-tuple-element.15, pred[4,4096]{1,0:T(4,128)(4,1)S(1)} %copy-done.4, bf16[4,4,12,128]{3,1,2,0:T(4,128)(2,1)S(1)} %all-to-all-done), kind=kOutput, calls=%fused_computation.63 | convolution fusion | flops 204476416 | bytes 7406336 | tf_op jit(solution)/shard_map/sub | solution.py:65
  173.2 4.3 %fusion.21 = bf16[4,4,12,128]{3,2,0,1:T(8,128)(2,1)S(1)} fusion(f32[4,4,12,4096]{3,2,0,1:T(8,128)} %get-tuple-element.25, f32[4,4,12]{2,0,1:T(4,128)S(1)} %get-tuple-element.24, bf16[4,4096,128]{2,1,0:T(8,128)(2,1)} %get-tuple-element.14), kind=kOutput, calls=%fused_computation.28 | convolution fusion | flops 202924032 | bytes 7389952 | tf_op jit(solution)/shard_map/gbht,btd->gbhd/dot_general | solution.py:66
  177.5 0.7 copy.56
  178.2 4.2 %all-to-all-start.1 = ((bf16[4,4,12,128]{3,1,2,0:T(4,128)(2,1)}), bf16[4,4,12,128]{3,1,2,0:T(4,128)(2,1)S(1)}, u32[]{:S(2)}, u32[]{:S(2)}) async-start(bf16[4,4,12,128]{3,1,2,0:T(4,128)(2,1)} %copy.56), calls=%async_computation.1 | async-start | bytes 98304 | tf_op jit(solution)/shard_map/all_to_all | solution.py:67
  182.4 6.6 %fusion.14 = f32[128,768]{1,0:T(8,128)S(1)} fusion(bf16[6144,768]{1,0:T(8,128)(2,1)} %param.23, bf16[128,6144]{1,0:T(8,128)(2,1)} %get-tuple-element.7, bf16[128,6144]{1,0:T(8,128)(2,1)} %get-tuple-element.8), kind=kOutput, calls=%fused_computation.23 | convolution fusion | flops 1214251008 | bytes 12976128 | tf_op jit(solution)/shard_map/dot_general | solution.py:71
  189.1 19.7 %all-gather = bf16[4,32,12,128]{3,0,2,1:T(4,128)(2,1)S(1)} all-gather(bf16[4,4,12,128]{3,0,2,1:T(4,128)(2,1)S(1)} %copy.57), channel_id=2, replica_groups=mesh['dp'=1,'ty'=4,'tx'=8] {'tx'}, dimensions={1}, use_global_device_ids=true | all-gather | bytes 442368 | tf_op jit(solution)/shard_map/all_gather | solution.py:68
  208.9 2.8 %fusion.17 = bf16[128,768]{1,0:T(8,128)(2,1)} fusion(f32[128,768]{1,0:T(8,128)S(1)} %fusion.14, bf16[1536,768]{1,0:T(8,128)(2,1)} %param.22, bf16[16,8,12,128]{3,2,1,0:T(8,128)(2,1)S(1)} %bitcast.45), kind=kOutput, calls=%fused_computation.26 | convolution fusion | flops 302186496 | bytes 3342336 | tf_op jit(solution)/shard_map/dot_general | solution.py:71
  211.8 40.5 %all-reduce.6.cloned.1.call-done = bf16[128,768]{1,0:T(8,128)(2,1)} async-done(((bf16[128,768]{1,0:T(8,128)(2,1)}), bf16[128,768]{1,0:T(8,128)(2,1)}) %all-reduce.6.cloned.1.call-update) | async-done | bytes 196624 | tf_op jit(solution)/shard_map/psum | solution.py:72
  252.2 1.6 fusion.28
  (27 shorter events, 0.6 us)
Async XLA Ops:
  7.2 28.5 %copy-start = (bf16[768,1536]{1,0:T(8,128)(2,1)S(1)}, bf16[768,1536]{1,0:T(8,128)(2,1)}, u32[]{:S(2)}) copy-start(bf16[768,1536]{1,0:T(8,128)(2,1)} %param.17) | copy-start | bytes 7077892
  7.2 74.2 %all-reduce.8.cloned.1.call-start = ((), (), s32[]{:S(2)}) async-start(), calls=%async_computation.3 | async-start | bytes 131072 | tf_op jit(solution)/shard_map/psum | solution.py:45
  26.3 6.7 %copy-start.2 = (bf16[128,768]{1,0:T(8,128)(2,1)S(1)}, bf16[128,768]{1,0:T(8,128)(2,1)}, u32[]{:S(2)}) copy-start(bf16[128,768]{1,0:T(8,128)(2,1)} %param.12) | copy-start | bytes 589828
  26.3 6.6 %copy-start.3 = (f32[768]{0:T(1024)S(1)}, f32[768]{0:T(1024)}, u32[]{:S(2)}) copy-start(f32[768]{0:T(1024)} %param.16) | copy-start | bytes 9220
  26.3 122.8 %all-reduce.10.cloned.1.call-start = ((), (), s32[]{:S(2)}) async-start(), calls=%async_computation.4 | async-start | bytes 7077888 | tf_op jit(solution)/shard_map/psum | solution.py:45
  26.4 6.7 %copy-start.1 = (bf16[768,6144]{1,0:T(8,128)(2,1)S(1)}, bf16[768,6144]{1,0:T(8,128)(2,1)}, u32[]{:S(2)}) copy-start(bf16[768,6144]{1,0:T(8,128)(2,1)} %param.21) | copy-start | bytes 28311556
  35.7 1.6 copy-start.5
  151.5 15.4 %all-to-all-start = ((bf16[4,4,12,128]{3,1,2,0:T(4,128)(2,1)}), bf16[4,4,12,128]{3,1,2,0:T(4,128)(2,1)S(1)}, u32[]{:S(2)}, u32[]{:S(2)}) async-start(bf16[4,4,12,128]{3,1,2,0:T(4,128)(2,1)} %copy_bitcast_fusion), calls=%async_computation | async-start | bytes 98304 | tf_op jit(solution)/shard_map/all_to_all | solution.py:61
  155.5 11.4 %copy-start.4 = (pred[4,4096]{1,0:T(4,128)(4,1)S(1)}, pred[4,4096]{1,0:T(4,128)(4,1)}, u32[]{:S(2)}) copy-start(pred[4,4096]{1,0:T(4,128)(4,1)} %get-tuple-element.22) | copy-start | bytes 49156
  178.2 10.8 %all-to-all-start.1 = ((bf16[4,4,12,128]{3,1,2,0:T(4,128)(2,1)}), bf16[4,4,12,128]{3,1,2,0:T(4,128)(2,1)S(1)}, u32[]{:S(2)}, u32[]{:S(2)}) async-start(bf16[4,4,12,128]{3,1,2,0:T(4,128)(2,1)} %copy.56), calls=%async_computation.1 | async-start | bytes 98304 | tf_op jit(solution)/shard_map/all_to_all | solution.py:67
  182.4 69.8 %all-reduce.6.cloned.1.call-start = ((), (), s32[]{:S(2)}) async-start(), calls=%async_computation.2 | async-start | bytes 393216 | tf_op jit(solution)/shard_map/psum | solution.py:72
Sparse Core Ops, SparseCore 0:
  26.4 54.9 all-reduce.7
  84.6 64.4 all-reduce.9
  211.9 40.2 all-reduce.5
where the time goes:
time: 262 us; the launch traced here: 260 us
  waiting for transfers between devices  149 us (57%)
  blocking collectives  33.6 us (13%)
  matrix products  33.6 us (13%)
  other arithmetic  18 us (7%)
  between operations  13.9 us (5%)
  starting transfers between devices  8.41 us (3%)
  local copies, waits for them, and re-layouts  4.33 us (2%)
    psum x2, waiting for transfers between devices, layer_shard(): q_sum, k_sum, v_new, gate, up_proj = lax.psum(partials, 'tx')  108 us
    psum x1, waiting for transfers between devices, layer_shard(): out_sum = lax.psum(part_out.astype(jnp.bfloat16), 'ty')  40.5 us
    all_gather x1, blocking collectives, layer_shard(): lax.all_gather(att_column, 'tx', axis=1, tiled=False)  19.7 us
    psum x1, blocking collectives, layer_shard(): row_stats = lax.psum(row_stats, 'tx')  13.9 us
    dot_general x5, matrix products, layer_shard(): jnp.dot(normed, weight, preferred_element_type=jnp.float32)  13.6 us
    select_n x1, other arithmetic, layer_shard(): v_out = jnp.where(at_slot, v_own[:, None, :], v_blk)  11.4 us
    dot_general x1, matrix products, layer_shard(): jnp.dot(mlp_act, w_down, preferred_element_type=jnp.float32)  6.58 us
    sub x1, matrix products, layer_shard(): att_probs = jax.nn.softmax(scores, axis=-1).astype(jnp.bfloat16)  6.24 us
  transfers between devices with their start and end apart: 5, of which 3 were waited for; matrix products, arithmetic and copies ran while one was open for 12% of the time, Pallas kernels for 0%

commit v1 on v0

v1 whole, which is shorter than its diff:
```python
import functools

import jax
import jax.numpy as jnp
import numpy as np
from jax import lax
from jax.experimental import pallas as pl
from jax.experimental.pallas import tpu as pltpu
from jax.sharding import PartitionSpec as P

EPSILON = 1e-6
ROPE_BASE = 10000.0
MESH = pl.DeviceIdType.MESH
F32 = jnp.float32
BF16 = jnp.bfloat16
VMEM = pltpu.VMEM
DMA = pltpu.SemaphoreType.DMA
SUBS = 4


def place(nx):
    row = lax.axis_index("ty")
    col = lax.axis_index("tx")
    chip = lax.div(col, 2)
    core = lax.rem(col, 2)
    step = 1 - 2 * core
    return row, col, chip, core, step


def remote(src, dst, send_sem, recv_sem, tx=None, ty=None):
    device = {}
    if tx is not None:
        device["tx"] = tx
    if ty is not None:
        device["ty"] = ty
    return pltpu.make_async_remote_copy(src_ref=src, dst_ref=dst, send_sem=send_sem, recv_sem=recv_sem, device_id=device, device_id_type=MESH)


def greet(tx_peers, ty_peers):
    barrier = pltpu.get_barrier_semaphore()
    for peer in tx_peers:
        pl.semaphore_signal(barrier, inc=1, device_id={"tx": peer}, device_id_type=MESH)
    for peer in ty_peers:
        pl.semaphore_signal(barrier, inc=1, device_id={"ty": peer}, device_id_type=MESH)
    pl.semaphore_wait(barrier, len(tx_peers) + len(ty_peers))


def proj_kernel(ny, nx, d_model, x_ref, gamma_ref, perm_ref, wq_h, wk_h, wv_h, wg_h, wu_h,
                q_out, kv_out, act_out,
                wq_v, wb_v, h_v, stat_s, stat_r, qp, qd_s, qd_r, qx_s, qx_r, qsum, qy_s, qy_r, d_s, d_r, own, r_s, r_r,
                wq_sem, wb_sem, stat_ss, stat_rs, qd_ss, qd_rs, qx_ss, qx_rs, qy_ss, qy_rs, d_ss, d_rs, r_ss, r_rs):
    row, col, chip, core, step = place(nx)
    ntx = 2 * nx
    rows = x_ref.shape[0]
    rb = rows // ntx
    sb = rb // ny
    qn = wq_h.shape[1]
    hd = wk_h.shape[1]
    fb = wb_v.shape[2] // 2
    sub = rows // SUBS

    def block_of(s, mine):
        sign = step if mine else -step
        at = lax.rem(chip - (s + 1) * sign + 2 * nx, nx)
        return 2 * at + (core if mine else 1 - core)

    def q_loads():
        return [
            pltpu.make_async_copy(wq_h, wq_v.at[:, pl.ds(0, qn)], wq_sem.at[0]),
            pltpu.make_async_copy(wk_h, wq_v.at[:, pl.ds(qn, hd)], wq_sem.at[1]),
            pltpu.make_async_copy(wv_h, wq_v.at[:, pl.ds(qn + hd, hd)], wq_sem.at[2]),
        ]

    def block_loads(n, b):
        at = pl.ds(pl.multiple_of(b * fb, fb), fb)
        return [
            pltpu.make_async_copy(wg_h.at[:, at], wb_v.at[n, :, pl.ds(0, fb)], wb_sem.at[n, 0]),
            pltpu.make_async_copy(wu_h.at[:, at], wb_v.at[n, :, pl.ds(fb, fb)], wb_sem.at[n, 1]),
        ]

    for c in q_loads():
        c.start()
    for n in range(ntx):
        for c in block_loads(n, block_of(n // 2, n % 2 == 1)):
            c.start()

    xp = jnp.dot(perm_ref[...], x_ref[...], preferred_element_type=F32)
    s1 = jnp.sum(xp, axis=1, keepdims=True)
    s2 = jnp.sum(xp * xp, axis=1, keepdims=True)
    lane = lax.broadcasted_iota(jnp.int32, (rows, rows), 1)
    both = jnp.where(lane == 0, s1, jnp.where(lane == 1, s2, 0.0))
    stat_s[...] = jnp.transpose(both)[:8]

    tx_peers = [lax.rem(col + k, ntx) for k in range(1, ntx)]
    ty_peers = [lax.rem(row + k, ny) for k in range(1, ny)]
    greet(tx_peers, ty_peers)

    stat_cp = [remote(stat_s, stat_r.at[k], stat_ss.at[k], stat_rs.at[k], tx=tx_peers[k - 1]) for k in range(1, ntx)]
    for c in stat_cp:
        c.start()
    total = stat_s[...]
    for k, c in enumerate(stat_cp):
        c.wait_recv()
        total = total + stat_r[k + 1]
    square = jnp.transpose(jnp.concatenate([total, jnp.zeros((rows - 8, rows), F32)], axis=0))
    mean = square[:, 0:1] / d_model
    var = square[:, 1:2] / d_model - mean * mean
    h_v[...] = ((xp - mean) * lax.rsqrt(var + EPSILON) * gamma_ref[...]).astype(BF16)

    for c in q_loads():
        c.wait()
    qw = qn + 2 * hd
    qp[...] = jnp.dot(h_v[...], wq_v[...], preferred_element_type=F32).reshape(ntx, rb, qw)
    for n in range(nx):
        qd_s[n] = qp[2 * n + 1 - core].astype(BF16)
    partner = lax.rem(col + 1, 2) + 2 * chip
    qd_cp = remote(qd_s, qd_r, qd_ss, qd_rs, tx=partner)
    qd_cp.start()

    qx_cp = [remote(qx_s.at[k], qx_r.at[k], qx_ss.at[k], qx_rs.at[k], tx=2 * lax.rem(chip + k, nx) + core) for k in range(1, nx)]
    qy_cp = [remote(qy_s.at[lax.rem(row + k, ny)], qy_r.at[row], qy_ss.at[k], qy_rs.at[k], ty=lax.rem(row + k, ny)) for k in range(1, ny)]
    qy_in = [remote(qy_s.at[lax.rem(row - k + ny, ny)], qy_r.at[lax.rem(row - k + ny, ny)], qy_ss.at[k], qy_rs.at[k], ty=lax.rem(row + k, ny)) for k in range(1, ny)]

    def q_pair():
        qd_cp.wait_recv()
        for k in range(1, nx):
            at = lax.rem(chip + k, nx)
            qx_s[k] = (qp[2 * at + core] + qd_r[at].astype(F32)).astype(BF16)
            qx_cp[k - 1].start()

    def q_rows():
        mine = qp[2 * chip + core] + qd_r[chip].astype(F32)
        for k in range(1, nx):
            qx_cp[k - 1].wait_recv()
            mine = mine + qx_r[k].astype(F32)
        qsum[...] = mine
        for a in range(ny):
            for n in range(qn // hd):
                qy_s[a, n * sb:(n + 1) * sb, :] = qsum[a * sb:(a + 1) * sb, n * hd:(n + 1) * hd]
        kv_out[...] = qsum[:, qn:]
        for c in qy_cp:
            c.start()

    after = 2 * lax.rem(chip + step + nx, nx) + core

    def d_copy(s):
        return remote(d_s.at[s], d_r.at[s], d_ss.at[s], d_rs.at[s], tx=partner)

    def r_copy(s, t):
        at = pl.ds(pl.multiple_of(t * sub, sub), sub)
        return remote(r_s.at[s, at], r_r.at[s, at], r_ss.at[s, t], r_rs.at[s, t], tx=after)

    def ring(s, carry):
        for c in block_loads(2 * s, 0):
            c.wait()
        own[...] = jnp.dot(h_v[...], wb_v[2 * s], preferred_element_type=F32)
        d_s[s] = own[...].astype(BF16)
        d_copy(s).start()

        @pl.when(s == 0)
        def _():
            q_pair()

        for c in block_loads(2 * s + 1, 0):
            c.wait()
        own[...] = jnp.dot(h_v[...], wb_v[2 * s + 1], preferred_element_type=F32)

        @pl.when(s == 2)
        def _():
            q_rows()

        d_copy(s).wait_recv()

        @pl.when(s == 0)
        def _():
            for t in range(SUBS):
                at = pl.ds(t * sub, sub)
                r_s[s, at] = (own[at] + d_r[s, at].astype(F32)).astype(BF16)
                r_copy(s, t).start()

        @pl.when(s > 0)
        def _():
            for t in range(SUBS):
                at = pl.ds(t * sub, sub)
                own[at] = own[at] + d_r[s, at].astype(F32)
                r_copy(s - 1, t).wait_recv()
                own[at] = own[at] + r_r[s - 1, at].astype(F32)

                @pl.when(s < nx - 1)
                def _():
                    r_s[s, at] = own[at].astype(BF16)
                    r_copy(s, t).start()

        return carry

    lax.fori_loop(0, nx, ring, 0)

    gate = own[:, :fb].astype(BF16).astype(F32)
    up = own[:, fb:].astype(BF16).astype(F32)
    act_out[...] = (gate * (1.0 / (1.0 + jnp.exp(-gate))) * up).astype(BF16)

    qy_r[row] = qy_s[row]
    for k in range(1, ny):
        qy_in[k - 1].wait_recv()
    q_out[...] = qy_r[...]

    for c in stat_cp:
        c.wait_send()
    qd_cp.wait_send()
    for c in qx_cp + qy_cp:
        c.wait_send()
    for s in range(nx):
        d_copy(s).wait_send()
    for s in range(nx - 1):
        for t in range(SUBS):
            r_copy(s, t).wait_send()


def attn_kernel(ny, ntx, chunk, lens_ref, q_ref, kv_ref, cs_ref, k_h, v_h, att_out, ko_h, vo_h, kbuf, vbuf, sbuf, qs, o32, in_sem, out_sem):
    row = lax.axis_index("ty")
    col = lax.axis_index("tx")
    sb, ctx, hd = k_h.shape
    heads = q_ref.shape[0] * q_ref.shape[1] // sb
    lh = heads // ny

    def k_in(r):
        return pltpu.make_async_copy(k_h.at[r], kbuf.at[r], in_sem.at[0, r])

    def v_in(r):
        return pltpu.make_async_copy(v_h.at[r], vbuf.at[r], in_sem.at[1, r])

    def k_put(r):
        return pltpu.make_async_copy(kbuf.at[r], ko_h.at[r], out_sem.at[0, r])

    def v_put(r):
        return pltpu.make_async_copy(vbuf.at[r], vo_h.at[r], out_sem.at[1, r])

    for r in range(sb):
        k_in(r).start()
        v_in(r).start()

    def turn(vals, r):
        return vals * cs_ref[r:r + 1, :] + pltpu.roll(vals, hd // 2, 1) * cs_ref[sb + r:sb + r + 1, :]

    def patch(buf, r, length, new):
        base = pl.multiple_of(lax.div(length, 16) * 16, 16)
        at = pl.ds(base, 16)
        old = buf[r, at, :]
        here = lax.broadcasted_iota(jnp.int32, (16, hd), 0) == length - base
        buf[r, at, :] = jnp.where(here, new, old.astype(F32)).astype(BF16)

    for r in range(sb):
        length = lens_ref[(row * ntx + col) * sb + r]
        for a in range(ny):
            part = q_ref[a, pl.ds(r, lh, stride=sb), :]
            qs[a * lh:(a + 1) * lh, :] = turn(part, r)
        q = qs[...].astype(BF16)
        new_rows = kv_ref[pl.ds(row * sb + r, 1), :]
        k_in(r).wait()
        patch(kbuf, r, length, turn(new_rows[:, :hd], r))
        k_put(r).start()
        chunks = lax.div(length, chunk) + 1

        def score(c, top):
            at = pl.ds(pl.multiple_of(c * chunk, chunk), chunk)
            s = lax.dot_general(q, kbuf[r, at, :], (((1,), (1,)), ((), ())), preferred_element_type=F32) * (hd ** -0.5)
            pos = lax.broadcasted_iota(jnp.int32, (heads, chunk), 1) + c * chunk
            s = jnp.where(pos <= length, s, -1e30)
            sbuf[:, at] = s
            return jnp.maximum(top, jnp.max(s, axis=1, keepdims=True))

        top = lax.fori_loop(0, chunks, score, jnp.full((heads, 1), -1e30, F32))

        def weigh(c, low):
            at = pl.ds(pl.multiple_of(c * chunk, chunk), chunk)
            e = jnp.exp(sbuf[:, at] - top)
            sbuf[:, at] = e
            return low + jnp.sum(e, axis=1, keepdims=True)

        low = lax.fori_loop(0, chunks, weigh, jnp.zeros((heads, 1), F32))
        share = 1.0 / low
        v_in(r).wait()
        patch(vbuf, r, length, new_rows[:, hd:])
        v_put(r).start()

        def mix(c, out):
            at = pl.ds(pl.multiple_of(c * chunk, chunk), chunk)
            p = (sbuf[:, at] * share).astype(BF16)
            return out + jnp.dot(p, vbuf[r, at, :], preferred_element_type=F32)

        out = lax.fori_loop(0, chunks, mix, jnp.zeros((heads, hd), F32))
        for a in range(ny):
            o32[a, pl.ds(r, lh, stride=sb), :] = out[a * lh:(a + 1) * lh]
    att_out[...] = o32[...].astype(BF16)
    for r in range(sb):
        k_put(r).wait()
        v_put(r).wait()


def out_kernel(ny, nx, x_ref, perm_ref, att_ref, act_ref, wo_h, wd_h, y_out,
               wo_v, wd_v, ay_r, g32, g_v, b_v, acc, y_s, y_r, yf,
               wo_sem, wd_sem, ay_ss, ay_rs, g_ss, g_rs, gp_ss, gp_rs, b_ss, b_rs, bp_ss, bp_rs, y_ss, y_rs, f_ss, f_rs):
    row, col, chip, core, step = place(nx)
    ntx = 2 * nx
    rows, fb = act_ref.shape
    lh, rb, hd = g32.shape
    sb = rb // ny
    sub = rows // SUBS
    yb = rows // ny
    dl = wo_h.shape[1]
    partner = lax.rem(col + 1, 2) + 2 * chip
    after = 2 * lax.rem(chip + step + nx, nx) + core

    def block_of(s, mine):
        sign = step if mine else -step
        return 2 * lax.rem(chip - s * sign + 2 * nx, nx) + (core if mine else 1 - core)

    def wo_load():
        return pltpu.make_async_copy(wo_h, wo_v, wo_sem)

    def wd_load(n, b):
        at = pl.ds(pl.multiple_of(b * fb, fb), fb)
        return pltpu.make_async_copy(wd_h.at[at, :], wd_v.at[n], wd_sem.at[n])

    for n in range(ntx):
        wd_load(n, block_of(n // 2, n % 2 == 0)).start()
    wo_load().start()

    x_peers = [2 * lax.rem(chip + k, nx) + core for k in range(1, nx)]
    y_peers = [lax.rem(row + k, ny) for k in range(1, ny)]
    greet(x_peers + [partner], y_peers)

    mine = block_of(0, True)
    b_v[mine] = act_ref[...]

    def b_copy(s, t):
        b = block_of(s, True)
        at = pl.ds(pl.multiple_of(t * sub, sub), sub)
        return remote(b_v.at[b, at], b_v.at[b, at], b_ss.at[s, t], b_rs.at[s, t], tx=after)

    def b_in(s, t):
        b = block_of(s + 1, True)
        at = pl.ds(pl.multiple_of(t * sub, sub), sub)
        return remote(b_v.at[b, at], b_v.at[b, at], b_ss.at[s, t], b_rs.at[s, t], tx=after)

    def bp_copy(s):
        b = block_of(s, True)
        return remote(b_v.at[b], b_v.at[b], bp_ss.at[s], bp_rs.at[s], tx=partner)

    def bp_in(s):
        b = block_of(s, False)
        return remote(b_v.at[b], b_v.at[b], bp_ss.at[s], bp_rs.at[s], tx=partner)

    for t in range(SUBS):
        b_copy(0, t).start()
    bp_copy(0).start()

    ay_cp = [remote(att_ref.at[y_peers[k - 1]], ay_r.at[row], ay_ss.at[k], ay_rs.at[k], ty=y_peers[k - 1]) for k in range(1, ny)]
    for c in ay_cp:
        c.start()
    ay_r[row] = att_ref[row]
    for k in range(1, ny):
        src = lax.rem(row - k + ny, ny)
        remote(att_ref.at[src], ay_r.at[src], ay_ss.at[k], ay_rs.at[k], ty=y_peers[k - 1]).wait_recv()
    for a in range(ny):
        part = ay_r[a].astype(F32)
        for n in range(lh):
            g32[n, a * sb:(a + 1) * sb, :] = part[n * sb:(n + 1) * sb, :]
    g_v[col] = g32[...].astype(BF16)

    g_cp = [remote(g_v.at[col], g_v.at[col], g_ss.at[k], g_rs.at[k], tx=x_peers[k - 1]) for k in range(1, nx)]
    for c in g_cp:
        c.start()

    def gp_copy(k):
        at = 2 * lax.rem(chip - k + nx, nx) + core
        return remote(g_v.at[at], g_v.at[at], gp_ss.at[k], gp_rs.at[k], tx=partner)

    def gp_in(k):
        at = 2 * lax.rem(chip - k + nx, nx) + 1 - core
        return remote(g_v.at[at], g_v.at[at], gp_ss.at[k], gp_rs.at[k], tx=partner)

    gp_copy(0).start()
    acc[...] = jnp.zeros_like(acc)

    def blocks(s, carry):
        wd_load(2 * s, 0).wait()
        acc[...] += jnp.dot(b_v[block_of(s, True)], wd_v[2 * s], preferred_element_type=F32)

        @pl.when(s < nx - 1)
        def _():
            for t in range(SUBS):
                b_in(s, t).wait_recv()

                @pl.when(s < nx - 2)
                def _():
                    b_copy(s + 1, t).start()

            bp_copy(s + 1).start()

        @pl.when(s == 0)
        def _():
            for k in range(1, nx):
                at = 2 * lax.rem(chip - k + nx, nx) + core
                remote(g_v.at[at], g_v.at[at], g_ss.at[k], g_rs.at[k], tx=x_peers[k - 1]).wait_recv()
                gp_copy(k).start()

        bp_in(s).wait_recv()
        wd_load(2 * s + 1, 0).wait()
        acc[...] += jnp.dot(b_v[block_of(s, False)], wd_v[2 * s + 1], preferred_element_type=F32)

        @pl.when(s == 1)
        def _():
            wo_load().wait()
            for k in range(nx):
                gp_in(k).wait_recv()
            for n in range(0, lh, 2):
                pair = jnp.concatenate([g_v[:, n].reshape(rows, hd), g_v[:, n + 1].reshape(rows, hd)], axis=1)
                acc[...] += jnp.dot(pair, wo_v[n * hd:(n + 2) * hd, :], preferred_element_type=F32)

        return carry

    lax.fori_loop(0, nx, blocks, 0)

    part = lax.dot_general(perm_ref[...], acc[...].astype(BF16), (((0,), (0,)), ((), ())), preferred_element_type=F32)
    y_s[...] = part.astype(BF16).reshape(ny, yb, dl)
    y_cp = [remote(y_s.at[y_peers[k - 1]], y_r.at[k], y_ss.at[k], y_rs.at[k], ty=y_peers[k - 1]) for k in range(1, ny)]
    for c in y_cp:
        c.start()
    total = x_ref[pl.ds(pl.multiple_of(row * yb, yb), yb), :].astype(F32) + y_s[row].astype(F32)
    for k in range(1, ny):
        y_cp[k - 1].wait_recv()
        total = total + y_r[k].astype(F32)
    yf[row] = total.astype(BF16)
    f_cp = [remote(yf.at[row], yf.at[row], f_ss.at[k], f_rs.at[k], ty=y_peers[k - 1]) for k in range(1, ny)]
    for c in f_cp:
        c.start()
    for k in range(1, ny):
        src = lax.rem(row - k + ny, ny)
        remote(yf.at[src], yf.at[src], f_ss.at[k], f_rs.at[k], ty=y_peers[k - 1]).wait_recv()
    y_out[...] = yf[...].reshape(rows, dl)

    for s in range(nx - 1):
        for t in range(SUBS):
            b_copy(s, t).wait_send()
    for s in range(nx):
        bp_copy(s).wait_send()
        gp_copy(s).wait_send()
    for c in ay_cp + g_cp + y_cp + f_cp:
        c.wait_send()


def solution(mesh):
    ny = mesh.shape["ty"]
    ntx = mesh.shape["tx"]
    nx = ntx // 2
    cache_spec = P(("dp", "ty", "tx"), None, None)
    vspec = pl.BlockSpec(memory_space=VMEM)
    hspec = pl.BlockSpec(memory_space=pltpu.HBM)
    sspec = pl.BlockSpec(memory_space=pltpu.SMEM)

    def layer_shard(x_blk, lens_part, k_blk, v_blk, gamma_blk, w_query, w_key, w_value, w_gate, w_up, w_out, w_down):
        rows, dl = x_blk.shape
        sb, ctx, hd = k_blk.shape
        qn = w_query.shape[1]
        lh = qn // hd
        qw = qn + 2 * hd
        ffl = w_gate.shape[1]
        fb = ffl // ntx
        rb = rows // ntx
        row_idx = lax.axis_index("ty")
        col_idx = lax.axis_index("tx")

        natural = np.arange(rows)
        order = np.reshape(np.transpose(np.reshape(natural, (ny, ntx, sb)), (1, 0, 2)), (rows,))
        perm = jnp.asarray(order[:, None] == natural[None, :], dtype=BF16)

        q_parts, kv_sum, act = pl.pallas_call(
            functools.partial(proj_kernel, ny, nx, dl * ntx),
            out_shape=(
                jax.ShapeDtypeStruct((ny, sb * lh, hd), F32),
                jax.ShapeDtypeStruct((rb, 2 * hd), F32),
                jax.ShapeDtypeStruct((rows, fb), BF16),
            ),
            in_specs=[vspec] * 3 + [hspec] * 5,
            out_specs=(vspec,) * 3,
            scratch_shapes=[
                VMEM((dl, qw), BF16), VMEM((ntx, dl, 2 * fb), BF16), VMEM((rows, dl), BF16),
                VMEM((8, rows), F32), VMEM((ntx, 8, rows), F32),
                VMEM((ntx, rb, qw), F32), VMEM((nx, rb, qw), BF16), VMEM((nx, rb, qw), BF16),
                VMEM((nx, rb, qw), BF16), VMEM((nx, rb, qw), BF16), VMEM((rb, qw), F32),
                VMEM((ny, sb * lh, hd), F32), VMEM((ny, sb * lh, hd), F32),
                VMEM((nx, rows, 2 * fb), BF16), VMEM((nx, rows, 2 * fb), BF16), VMEM((rows, 2 * fb), F32),
                VMEM((nx - 1, rows, 2 * fb), BF16), VMEM((nx - 1, rows, 2 * fb), BF16),
                DMA((3,)), DMA((ntx, 2)), DMA((ntx,)), DMA((ntx,)), DMA, DMA, DMA((nx,)), DMA((nx,)), DMA((ny,)), DMA((ny,)),
                DMA((nx,)), DMA((nx,)), DMA((nx - 1, SUBS)), DMA((nx - 1, SUBS)),
            ],
            compiler_params=pltpu.CompilerParams(collective_id=0, has_side_effects=True, vmem_limit_bytes=60 * 1024 * 1024),
            name="proj",
        )(x_blk, gamma_blk[None, :], perm, w_query, w_key, w_value, w_gate, w_up)

        lens_own = lax.dynamic_slice_in_dim(lens_part, (row_idx * ntx + col_idx) * sb, sb)
        inv_freqs = ROPE_BASE ** (-(jnp.arange(hd // 2, dtype=F32) * 2.0) / hd)
        angles = lens_own.astype(F32)[:, None] * inv_freqs[None, :]
        cosines, sines = jnp.cos(angles), jnp.sin(angles)
        turns = jnp.concatenate([jnp.concatenate([cosines, cosines], axis=1), jnp.concatenate([-sines, sines], axis=1)], axis=0)

        att, k_out, v_out = pl.pallas_call(
            functools.partial(attn_kernel, ny, ntx, 512),
            out_shape=(
                jax.ShapeDtypeStruct((ny, sb * lh, hd), BF16),
                jax.ShapeDtypeStruct(k_blk.shape, BF16),
                jax.ShapeDtypeStruct(v_blk.shape, BF16),
            ),
            in_specs=[sspec, vspec, vspec, vspec, hspec, hspec],
            out_specs=(vspec, hspec, hspec),
            scratch_shapes=[
                VMEM((sb, ctx, hd), BF16), VMEM((sb, ctx, hd), BF16), VMEM((ny * lh, ctx), F32), VMEM((ny * lh, hd), F32),
                VMEM((ny, sb * lh, hd), F32), DMA((2, sb)), DMA((2, sb)),
            ],
            compiler_params=pltpu.CompilerParams(vmem_limit_bytes=40 * 1024 * 1024),
            name="attn",
        )(lens_part, q_parts, kv_sum, turns, k_blk, v_blk)

        y_blk = pl.pallas_call(
            functools.partial(out_kernel, ny, nx),
            out_shape=jax.ShapeDtypeStruct((rows, dl), BF16),
            in_specs=[vspec] * 4 + [hspec] * 2,
            out_specs=vspec,
            scratch_shapes=[
                VMEM((qn, dl), BF16), VMEM((ntx, fb, dl), BF16), VMEM((ny, sb * lh, hd), BF16), VMEM((lh, rb, hd), F32),
                VMEM((ntx, lh, rb, hd), BF16), VMEM((ntx, rows, fb), BF16), VMEM((rows, dl), F32),
                VMEM((ny, rows // ny, dl), BF16), VMEM((ny, rows // ny, dl), BF16), VMEM((ny, rows // ny, dl), BF16),
                DMA, DMA((ntx,)), DMA((ny,)), DMA((ny,)), DMA((nx,)), DMA((nx,)), DMA((nx,)), DMA((nx,)),
                DMA((nx - 1, SUBS)), DMA((nx - 1, SUBS)), DMA((nx,)), DMA((nx,)), DMA((ny,)), DMA((ny,)), DMA((ny,)), DMA((ny,)),
            ],
            compiler_params=pltpu.CompilerParams(collective_id=1, has_side_effects=True, vmem_limit_bytes=60 * 1024 * 1024),
            name="outs",
        )(x_blk, perm, att, act, w_out, w_down)
        return y_blk, k_out, v_out

    in_specs = (P("dp", "tx"), P("dp"), cache_spec, cache_spec, P("tx"), P("tx", "ty"), P("tx", None), P("tx", None), P("tx", "ty"), P("tx", "ty"), P("ty", "tx"), P("ty", "tx"))
    out_specs = (P("dp", "tx"), cache_spec, cache_spec)
    return jax.shard_map(layer_shard, mesh=mesh, in_specs=in_specs, out_specs=out_specs, check_vma=False)
```

time: 262 us -> 83.9 us (0.32)
  waiting for transfers between devices: 149 us -> 0 us
  Pallas kernels: 0 us -> 72.8 us
  matrix products: 33.6 us -> 0 us
  blocking collectives: 33.6 us -> 0 us
  other arithmetic: 18 us -> 0.93 us
  between operations: 13.9 us -> 0.69 us
  starting transfers between devices: 8.41 us -> 0 us
  local copies, waits for them, and re-layouts: 4.33 us -> 9.49 us
    psum x3 -> x0, waiting for transfers between devices: 148 us -> none  [the longest x2 108 us: layer_shard(): q_sum, k_sum, v_new, gate, up_proj = lax.psum(partials, 'tx')]
    pallas_call x0 -> x3, Pallas kernels: none -> 72.8 us  [the longest x1 33.3 us: layer_shard(): pl.pallas_call(functools.partial(proj_kernel, ny, nx, dl * ntx), out_shap...]
    dot_general x8 -> x0, matrix products: 27.3 us -> none  [the longest x5 13.6 us: layer_shard(): jnp.dot(normed, weight, preferred_element_type=jnp.float32)]
    all_gather x1 -> x0, blocking collectives: 19.7 us -> none  [layer_shard(): lax.all_gather(att_column, 'tx', axis=1, tiled=False)]
    psum x1 -> x0, blocking collectives: 13.9 us -> none  [layer_shard(): row_stats = lax.psum(row_stats, 'tx')]
    select_n x1 -> x0, other arithmetic: 11.4 us -> none  [layer_shard(): v_out = jnp.where(at_slot, v_own[:, None, :], v_blk)]
    all_to_all x2 -> x0, starting transfers between devices: 8.28 us -> none  [the longest x1 4.25 us: layer_shard(): att_column = lax.all_to_all(att_owned, 'ty', 0, 0, tiled=True)]
    unnamed x12 -> x13, local copies, waits for them, and re-layouts: 0.15 us -> 8.21 us
  transfers between devices with their start and end apart: 5 -> 0, of which waited for: 3 -> 0; matrix products, arithmetic and copies ran while one was open for 12% -> 0% of each run, Pallas kernels for 0% -> 0%
where the time goes in v1:
time: 83.9 us
  Pallas kernels  72.8 us (87%)
  local copies, waits for them, and re-layouts  9.49 us (11%)
  other arithmetic  0.93 us (1%)
    pallas_call x1, Pallas kernels, layer_shard(): pl.pallas_call(functools.partial(proj_kernel, ny, nx, dl * ntx), out_shap...  33.3 us
    pallas_call x1, Pallas kernels, layer_shard(): pl.pallas_call(functools.partial(out_kernel, ny, nx), out_shape=jax.Shape...  29.1 us
    pallas_call x1, Pallas kernels, layer_shard(): pl.pallas_call(functools.partial(attn_kernel, ny, ntx, 512), out_shape=(j...  10.4 us
    unnamed x13, local copies, waits for them, and re-layouts  8.21 us

profile of v1, /device:TPU:97, one launch (start us, length us, event | category | flops | bytes accessed | tf_op | source)
XLA Modules:
  0.0 83.9 jit_solution(1365912101455773134)
XLA Ops:
  0.6 0.7 dynamic-slice_convert_fusion
  1.4 1.3 %broadcast_in_dim.2.gamma_ref = f32[1,768]{1,0:T(1,128)} reshape(f32[768]{0:T(1024)} %param.17) | data formatting | bytes 6144 | tf_op jit(solution)/shard_map/broadcast_in_dim | solution.py:500
  2.7 0.1 multiply_cosine_fusion
  2.8 0.1 maximum_maximum_fusion.cs_ref
  2.8 0.0 copy-start.5
  2.8 33.3 %proj.1 = (f32[4,48,128]{2,1,0:T(8,128)}, f32[16,256]{1,0:T(8,128)}, bf16[128,768]{1,0:T(8,128)(2,1)}) custom-call(bf16[128,768]{1,0:T(8,128)(2,1)} %x_ref.3, f32[1,768]{1,0:T(1,128)} %broadcast_in_dim.2.gamma_ref, bf16[128,128]{1,0:T(8,128)(2,1)} %constant.25.clone.perm_ref, bf16[768,1536]{1,0:T(8,128)(2,1)} %wq_h.1, bf16[768,128]{1,0:T(8,128)(2,1)} %wk_h.1, ...), custom_call_target="tpu_custom_call" | custom-call | tf_op jit(solution)/shard_map/proj/pallas_call | solution.py:478
  36.2 0.0 copy-done.5
  36.2 0.0 copy-start
  36.2 2.2 %copy-done = bf16[4,4096,128]{2,1,0:T(8,128)(2,1)S(1)} copy-done((bf16[4,4096,128]{2,1,0:T(8,128)(2,1)S(1)}, bf16[4,4096,128]{2,1,0:T(8,128)(2,1)}, u32[]{:S(2)}) %copy-start) | copy-done | bytes 4194328
  38.4 0.0 copy-start.1
  38.4 2.2 %copy-done.1 = bf16[4,4096,128]{2,1,0:T(8,128)(2,1)S(1)} copy-done((bf16[4,4096,128]{2,1,0:T(8,128)(2,1)S(1)}, bf16[4,4096,128]{2,1,0:T(8,128)(2,1)}, u32[]{:S(2)}) %copy-start.1) | copy-done | bytes 4194328
  40.5 0.0 copy-start.2
  40.6 0.9 %copy-done.2 = f32[4,48,128]{2,1,0:T(8,128)S(1)} copy-done((f32[4,48,128]{2,1,0:T(8,128)S(1)}, f32[4,48,128]{2,1,0:T(8,128)}, u32[]{:S(2)}) %copy-start.2) | copy-done | bytes 98328
  41.4 0.0 copy-start.4
  41.4 0.7 copy-done.4
  42.2 10.4 %attn.1 = (bf16[4,48,128]{2,1,0:T(8,128)(2,1)S(1)}, bf16[4,4096,128]{2,1,0:T(8,128)(2,1)}, bf16[4,4096,128]{2,1,0:T(8,128)(2,1)}) custom-call(s32[128]{0:T(128)S(1)} %copy-done.5, f32[4,48,128]{2,1,0:T(8,128)S(1)} %copy-done.2, f32[16,256]{1,0:T(8,128)S(1)} %copy-done.4, f32[8,128]{1,0:T(8,128)S(1)} %maximum_maximum_fusion.cs_ref, ...), custom_call_target="tpu_custom_call" | custom-call | tf_op jit(solution)/shard_map/attn/pallas_call | solution.py:508
  52.5 0.0 copy-start.3
  52.5 0.6 copy-done.3
  53.2 29.1 %outs.1 = bf16[128,768]{1,0:T(8,128)(2,1)} custom-call(bf16[128,768]{1,0:T(8,128)(2,1)} %x_ref.3, bf16[128,128]{1,0:T(8,128)(2,1)} %constant.25.clone.perm_ref, bf16[4,48,128]{2,1,0:T(8,128)(2,1)} %copy-done.3, bf16[128,768]{1,0:T(8,128)(2,1)} %get-tuple-element.12.act_ref, bf16[1536,768]{1,0:T(8,128)(2,1)} %wo_h.1, bf16[6144,768]{1,0:T(8,128)(2,1)} %wd_h.1), custom_call_target="tpu_custom_call" | custom-call | tf_op jit(solution)/shard_map/outs/pallas_call | solution.py:525
  82.3 1.6 %copy.17 = bf16[128,768]{1,0:T(8,128)(2,1)} copy(bf16[128,768]{1,0:T(8,128)(2,1)} %outs.1) | data formatting | bytes 393216
  (1 shorter events, 0.0 us)
Async XLA Ops:
  2.8 33.3 %copy-start.5 = (s32[128]{0:T(128)S(1)}, s32[128]{0:T(128)}, u32[]{:S(2)}) copy-start(s32[128]{0:T(128)} %lens_ref.1) | copy-start | bytes 1540
  36.2 2.2 %copy-start = (bf16[4,4096,128]{2,1,0:T(8,128)(2,1)S(1)}, bf16[4,4096,128]{2,1,0:T(8,128)(2,1)}, u32[]{:S(2)}) copy-start(bf16[4,4096,128]{2,1,0:T(8,128)(2,1)} %k_h.1) | copy-start | bytes 12582916
  38.4 2.2 %copy-start.1 = (bf16[4,4096,128]{2,1,0:T(8,128)(2,1)S(1)}, bf16[4,4096,128]{2,1,0:T(8,128)(2,1)}, u32[]{:S(2)}) copy-start(bf16[4,4096,128]{2,1,0:T(8,128)(2,1)} %v_h.1) | copy-start | bytes 12582916
  40.5 0.9 %copy-start.2 = (f32[4,48,128]{2,1,0:T(8,128)S(1)}, f32[4,48,128]{2,1,0:T(8,128)}, u32[]{:S(2)}) copy-start(f32[4,48,128]{2,1,0:T(8,128)} %get-tuple-element.9.q_ref) | copy-start | bytes 294916
  41.4 0.7 copy-start.4
  52.5 0.6 copy-start.3

commit v2 on v0

v2 whole, which is shorter than its diff:
```python
import functools

import jax
import jax.numpy as jnp
import numpy as np
from jax import lax
from jax.experimental import pallas as pl
from jax.experimental.pallas import tpu as pltpu
from jax.sharding import PartitionSpec as P

EPSILON = 1e-6
ROPE_BASE = 10000.0
LOG2E = 1.4426950408889634
MESH = pl.DeviceIdType.MESH
F32 = jnp.float32
BF16 = jnp.bfloat16
VMEM = pltpu.VMEM
DMA = pltpu.SemaphoreType.DMA
SUBS = 4
CHUNK = 1024
PIECE = 512
scope = jax.named_scope


def remote(src, dst, send_sem, recv_sem, tx=None, ty=None):
    device = {}
    if tx is not None:
        device["tx"] = tx
    if ty is not None:
        device["ty"] = ty
    return pltpu.make_async_remote_copy(src_ref=src, dst_ref=dst, send_sem=send_sem, recv_sem=recv_sem, device_id=device, device_id_type=MESH)


def step_kernel(ny, nx, d_model, lens_ref, x_h, gamma_h, perm_h, freq_h, wq_h, wk_h, wv_h, wg_h, wu_h, k_h, v_h, wo_h, wd_h,
                y_out, new_out, kbuf, vbuf,
                x_v, gamma_v, perm_v, freq_v, wq_v, wb_v, wo_v, wd_v, h_v, stat_s, stat_r,
                qp, qd_s, qd_r, qx_s, qx_r, qsum, kvs, qy_s, qy_r, own, d_s, d_r, r_s, r_r,
                turns, qs, sbuf, o32, ay_s, ay_r, g32, g_v, b_v, acc, y_s, y_r, yf,
                in_sem, wq_sem, wb_sem, kv_sem, wo_sem, wd_sem, stat_ss, stat_rs, qd_ss, qd_rs, qx_ss, qx_rs, qy_ss, qy_rs,
                d_ss, d_rs, r_ss, r_rs, ay_ss, ay_rs, g_ss, g_rs, gp_ss, gp_rs, b_ss, b_rs, bp_ss, bp_rs, y_ss, y_rs, f_ss, f_rs):
    row = lax.axis_index("ty")
    col = lax.axis_index("tx")
    chip = lax.div(col, 2)
    core = lax.rem(col, 2)
    step = 1 - 2 * core
    ntx = 2 * nx
    rows, dl = x_h.shape
    rb = rows // ntx
    sb = rb // ny
    qn = wq_h.shape[1]
    hd = wk_h.shape[1]
    qw = qn + 2 * hd
    lh = qn // hd
    heads = ny * lh
    ctx = k_h.shape[1]
    fb = wb_v.shape[2] // 2
    sub = rows // SUBS
    yb = rows // ny
    partner = lax.rem(col + 1, 2) + 2 * chip
    after = 2 * lax.rem(chip + step + nx, nx) + core
    tx_peers = [lax.rem(col + k, ntx) for k in range(1, ntx)]
    x_peers = [2 * lax.rem(chip + k, nx) + core for k in range(1, nx)]
    y_peers = [lax.rem(row + k, ny) for k in range(1, ny)]
    y_froms = [lax.rem(row - k + ny, ny) for k in range(1, ny)]

    barrier = pltpu.get_barrier_semaphore()
    for peer in tx_peers:
        pl.semaphore_signal(barrier, inc=1, device_id={"tx": peer}, device_id_type=MESH)
    for peer in y_peers:
        pl.semaphore_signal(barrier, inc=1, device_id={"ty": peer}, device_id_type=MESH)

    def piece(t):
        return pl.ds(pl.multiple_of(t * sub, sub), sub)

    def block_of(s, mine):
        sign = step if mine else -step
        at = lax.rem(chip - (s + 1) * sign + 2 * nx, nx)
        return 2 * at + (core if mine else 1 - core)

    def held(s, mine):
        sign = step if mine else -step
        return 2 * lax.rem(chip - s * sign + 2 * nx, nx) + (core if mine else 1 - core)

    def block_loads(n, b):
        at = pl.ds(pl.multiple_of(b * fb, fb), fb)
        return [
            pltpu.make_async_copy(wg_h.at[:, at], wb_v.at[n, :, pl.ds(0, fb)], wb_sem.at[n, 0]),
            pltpu.make_async_copy(wu_h.at[:, at], wb_v.at[n, :, pl.ds(fb, fb)], wb_sem.at[n, 1]),
        ]

    def wd_load(n, b):
        at = pl.ds(pl.multiple_of(b * fb, fb), fb)
        return pltpu.make_async_copy(wd_h.at[at, :], wd_v.at[n], wd_sem.at[n])

    first_loads = [
        pltpu.make_async_copy(x_h, x_v, in_sem.at[0]),
        pltpu.make_async_copy(perm_h, perm_v, in_sem.at[1]),
        pltpu.make_async_copy(gamma_h, gamma_v, in_sem.at[2]),
        pltpu.make_async_copy(freq_h, freq_v, in_sem.at[3]),
    ]
    q_loads = [
        pltpu.make_async_copy(wq_h, wq_v.at[:, pl.ds(0, qn)], wq_sem.at[0]),
        pltpu.make_async_copy(wk_h, wq_v.at[:, pl.ds(qn, hd)], wq_sem.at[1]),
        pltpu.make_async_copy(wv_h, wq_v.at[:, pl.ds(qn + hd, hd)], wq_sem.at[2]),
    ]
    k_in = [pltpu.make_async_copy(k_h.at[r], kbuf.at[r], kv_sem.at[0, r]) for r in range(sb)]
    v_in = [pltpu.make_async_copy(v_h.at[r], vbuf.at[r], kv_sem.at[1, r]) for r in range(sb)]
    wo_load = pltpu.make_async_copy(wo_h, wo_v, wo_sem)
    for c in first_loads + q_loads:
        c.start()
    for n in range(ntx):
        for c in block_loads(n, block_of(n // 2, n % 2 == 1)):
            c.start()
    for c in k_in + v_in:
        c.start()
    for n in range(ntx):
        wd_load(n, held(n // 2, n % 2 == 0)).start()
    wo_load.start()

    for c in first_loads:
        c.wait()
    xp = jnp.dot(perm_v[...], x_v[...], preferred_element_type=F32)
    s1 = jnp.sum(xp, axis=1, keepdims=True)
    s2 = jnp.sum(xp * xp, axis=1, keepdims=True)
    lane = lax.broadcasted_iota(jnp.int32, (rows, rows), 1)
    both = jnp.where(lane == 0, s1, jnp.where(lane == 1, s2, 0.0))
    stat_s[...] = jnp.transpose(both)[:8]

    at_row = lax.broadcasted_iota(jnp.int32, (8, hd), 0)
    places = jnp.zeros((8, hd), F32)
    for r in range(sb):
        places = jnp.where(at_row == r, lens_ref[(row * ntx + col) * sb + r].astype(F32), places)
    angles = places * freq_v[...]
    turns[0] = jnp.cos(angles)
    low_half = lax.broadcasted_iota(jnp.int32, (8, hd), 1) < hd // 2
    sines = jnp.sin(angles)
    turns[1] = jnp.where(low_half, -sines, sines)

    with scope("greet"):
        pl.semaphore_wait(barrier, ntx - 1 + ny - 1)

    stat_cp = [remote(stat_s, stat_r.at[k], stat_ss.at[k], stat_rs.at[k], tx=tx_peers[k - 1]) for k in range(1, ntx)]
    for c in stat_cp:
        c.start()
    total = stat_s[...]
    with scope("stat"):
        for k, c in enumerate(stat_cp):
            c.wait_recv()
            total = total + stat_r[k + 1]
    square = jnp.transpose(jnp.concatenate([total, jnp.zeros((rows - 8, rows), F32)], axis=0))
    mean = square[:, 0:1] / d_model
    var = square[:, 1:2] / d_model - mean * mean
    h_v[...] = ((xp - mean) * lax.rsqrt(var + EPSILON) * gamma_v[...].reshape(1, dl)).astype(BF16)

    for c in q_loads:
        c.wait()
    qp[...] = jnp.dot(h_v[...], wq_v[...], preferred_element_type=F32).reshape(ntx, rb, qw)
    for n in range(nx):
        qd_s[n] = qp[2 * n + 1 - core].astype(BF16)
    qd_cp = remote(qd_s, qd_r, qd_ss, qd_rs, tx=partner)
    qd_cp.start()
    qx_cp = [remote(qx_s.at[k], qx_r.at[k], qx_ss.at[k], qx_rs.at[k], tx=x_peers[k - 1]) for k in range(1, nx)]
    qy_cp = [remote(qy_s.at[y_peers[k - 1]], qy_r.at[row], qy_ss.at[k], qy_rs.at[k], ty=y_peers[k - 1]) for k in range(1, ny)]
    qy_in = [remote(qy_s.at[y_froms[k - 1]], qy_r.at[y_froms[k - 1]], qy_ss.at[k], qy_rs.at[k], ty=y_peers[k - 1]) for k in range(1, ny)]

    def q_pair():
        with scope("qd"):
            qd_cp.wait_recv()
        for k in range(1, nx):
            at = lax.rem(chip + k, nx)
            qx_s[k] = (qp[2 * at + core] + qd_r[at].astype(F32)).astype(BF16)
            qx_cp[k - 1].start()

    def q_rows():
        mine = qp[2 * chip + core] + qd_r[chip].astype(F32)
        with scope("qx"):
            for k in range(1, nx):
                qx_cp[k - 1].wait_recv()
                mine = mine + qx_r[k].astype(F32)
        qsum[...] = mine
        kvs[0] = mine[:, qn:qn + hd]
        kvs[1] = mine[:, qn + hd:]
        for a in range(ny):
            for n in range(lh):
                qy_s[a, n * sb:(n + 1) * sb, :] = qsum[a * sb:(a + 1) * sb, n * hd:(n + 1) * hd]
        for c in qy_cp:
            c.start()
        qy_r[row] = qy_s[row]

    def d_copy(s):
        return remote(d_s.at[s], d_r.at[s], d_ss.at[s], d_rs.at[s], tx=partner)

    def r_copy(s, t):
        return remote(r_s.at[s, piece(t)], r_r.at[s, piece(t)], r_ss.at[s, t], r_rs.at[s, t], tx=after)

    def product(s, carry):
        for c in block_loads(2 * s, 0):
            c.wait()
        d_s[s] = jnp.dot(h_v[...], wb_v[2 * s], preferred_element_type=F32).astype(BF16)
        d_copy(s).start()

        @pl.when(s == 0)
        def _():
            q_pair()

        for c in block_loads(2 * s + 1, 0):
            c.wait()
        own[s] = jnp.dot(h_v[...], wb_v[2 * s + 1], preferred_element_type=F32)

        @pl.when(s == 0)
        def _():
            with scope("d0"):
                d_copy(0).wait_recv()
            for t in range(SUBS):
                at = piece(t)
                r_s[0, at] = (own[0, at] + d_r[0, at].astype(F32)).astype(BF16)
                r_copy(0, t).start()

        return carry

    with scope("products"):
        lax.fori_loop(0, nx, product, 0)

    def ring(s, t):
        at = piece(t)
        if t == 0:
            with scope("d%d" % s):
                d_copy(s).wait_recv()
        part = own[s, at] + d_r[s, at].astype(F32)
        with scope("r%d%d" % (s, t)):
            r_copy(s - 1, t).wait_recv()
        part = part + r_r[s - 1, at].astype(F32)
        if s < nx - 1:
            r_s[s, at] = part.astype(BF16)
            r_copy(s, t).start()
        else:
            gate = part[:, :fb].astype(BF16).astype(F32)
            up = part[:, fb:].astype(BF16).astype(F32)
            b_v[col, at] = (gate * (1.0 / (1.0 + jnp.exp(-gate))) * up).astype(BF16)

    def turn(vals, r):
        return vals * turns[0, r:r + 1, :] + pltpu.roll(vals, hd // 2, 1) * turns[1, r:r + 1, :]

    def attend(r):
        length = lens_ref[(row * ntx + col) * sb + r]
        for a in range(ny):
            qs[a * lh:(a + 1) * lh, :] = turn(qy_r[a, pl.ds(r, lh, stride=sb), :], r)
        q = qs[...].astype(BF16)
        k_new = turn(kvs[0, pl.ds(row * sb + r, 1), :], r).astype(BF16).astype(F32)
        v_new = kvs[1, pl.ds(row * sb + r, 1), :].astype(BF16).astype(F32)
        new_out[r:r + 1, :] = k_new
        new_out[sb + r:sb + r + 1, :] = v_new
        k_in[r].wait()
        s_new = jnp.sum(q.astype(F32) * k_new, axis=1, keepdims=True)
        top = jnp.full((heads, hd), -1e30, F32)
        for c in range(ctx // CHUNK):
            s = lax.dot_general(q, kbuf[r, c * CHUNK:(c + 1) * CHUNK, :], (((1,), (1,)), ((), ())), preferred_element_type=F32)
            pos = lax.broadcasted_iota(jnp.int32, (1, CHUNK), 1) + c * CHUNK
            s = jnp.where(pos < length, s, -1e30)
            sbuf[:, c * CHUNK:(c + 1) * CHUNK] = s
            for t in range(CHUNK // hd):
                top = jnp.maximum(top, s[:, t * hd:(t + 1) * hd])
        high = jnp.maximum(jnp.max(top, axis=1, keepdims=True), s_new)
        rate = hd ** -0.5 * LOG2E
        e_new = jnp.exp2((s_new - high) * rate)
        low = jnp.zeros((heads, hd), F32)
        out = e_new.astype(BF16).astype(F32) * v_new
        v_in[r].wait()
        for c in range(ctx // CHUNK):
            e = jnp.exp2((sbuf[:, c * CHUNK:(c + 1) * CHUNK] - high) * rate)
            for t in range(CHUNK // hd):
                low = low + e[:, t * hd:(t + 1) * hd]
            out = out + jnp.dot(e.astype(BF16), vbuf[r, c * CHUNK:(c + 1) * CHUNK, :], preferred_element_type=F32)
        out = out / (jnp.sum(low, axis=1, keepdims=True) + e_new)
        for a in range(ny):
            o32[a, pl.ds(r, lh, stride=sb), :] = out[a * lh:(a + 1) * lh]

    def b_copy(s, t):
        b = held(s, True)
        return remote(b_v.at[b, piece(t)], b_v.at[b, piece(t)], b_ss.at[s, t], b_rs.at[s, t], tx=after)

    def b_in(s, t):
        b = held(s + 1, True)
        return remote(b_v.at[b, piece(t)], b_v.at[b, piece(t)], b_ss.at[s, t], b_rs.at[s, t], tx=after)

    def bp_copy(s, t):
        b = held(s, True)
        return remote(b_v.at[b, piece(t)], b_v.at[b, piece(t)], bp_ss.at[s, t], bp_rs.at[s, t], tx=partner)

    def bp_in(s, t):
        b = held(s, False)
        return remote(b_v.at[b, piece(t)], b_v.at[b, piece(t)], bp_ss.at[s, t], bp_rs.at[s, t], tx=partner)

    ay_cp = [remote(ay_s.at[y_peers[k - 1]], ay_r.at[row], ay_ss.at[k], ay_rs.at[k], ty=y_peers[k - 1]) for k in range(1, ny)]
    ay_in = [remote(ay_s.at[y_froms[k - 1]], ay_r.at[y_froms[k - 1]], ay_ss.at[k], ay_rs.at[k], ty=y_peers[k - 1]) for k in range(1, ny)]
    g_cp = [remote(g_v.at[col], g_v.at[col], g_ss.at[k], g_rs.at[k], tx=x_peers[k - 1]) for k in range(1, nx)]

    def g_from(k, mine):
        return 2 * lax.rem(chip - k + nx, nx) + (core if mine else 1 - core)

    def g_in(k):
        at = g_from(k, True)
        return remote(g_v.at[at], g_v.at[at], g_ss.at[k], g_rs.at[k], tx=x_peers[k - 1])

    def gp_copy(k):
        at = g_from(k, True)
        return remote(g_v.at[at], g_v.at[at], gp_ss.at[k], gp_rs.at[k], tx=partner)

    def gp_in(k):
        at = g_from(k, False)
        return remote(g_v.at[at], g_v.at[at], gp_ss.at[k], gp_rs.at[k], tx=partner)

    def att_out():
        ay_s[...] = o32[...].astype(BF16)
        for c in ay_cp:
            c.start()
        ay_r[row] = ay_s[row]

    def att_rows():
        with scope("ay"):
            for c in ay_in:
                c.wait_recv()
        for a in range(ny):
            part = ay_r[a].astype(F32)
            for n in range(lh):
                g32[n, a * sb:(a + 1) * sb, :] = part[n * sb:(n + 1) * sb, :]
        g_v[col] = g32[...].astype(BF16)
        for c in g_cp:
            c.start()
        gp_copy(0).start()

    def forward(s):
        for t in range(SUBS):
            with scope("b%d%d" % (s, t)):
                b_in(s, t).wait_recv()
            if s < nx - 2:
                b_copy(s + 1, t).start()
            bp_copy(s + 1, t).start()

    def down(n, first=False):
        wd_load(n, 0).wait()
        part = jnp.dot(b_v[held(n // 2, n % 2 == 0)], wd_v[n], preferred_element_type=F32)
        acc[...] = part if first else acc[...] + part

    def from_pair(s):
        with scope("bp%d" % s):
            for t in range(SUBS):
                bp_in(s, t).wait_recv()

    ring(1, 0)
    q_rows()
    for t in range(1, SUBS):
        ring(1, t)
    ring(2, 0)
    ring(2, 1)
    with scope("qy"):
        for c in qy_in:
            c.wait_recv()
    with scope("a0"):
        attend(0)
    ring(2, 2)
    ring(2, 3)
    with scope("a1"):
        attend(1)
    ring(3, 0)
    with scope("a2"):
        attend(2)
    ring(3, 1)
    with scope("a3"):
        attend(3)
    att_out()
    for t in range(2, SUBS):
        ring(3, t)
    for t in range(SUBS):
        b_copy(0, t).start()
        bp_copy(0, t).start()
    down(0, True)
    att_rows()
    forward(0)
    from_pair(0)
    down(1)
    down(2)
    forward(1)
    with scope("g"):
        for k in range(1, nx):
            g_in(k).wait_recv()
            gp_copy(k).start()
    from_pair(1)
    down(3)
    down(4)
    with scope("gp"):
        for k in range(nx):
            gp_in(k).wait_recv()
    wo_load.wait()
    for n in range(0, lh, 2):
        pair = jnp.concatenate([g_v[:, n].reshape(rows, hd), g_v[:, n + 1].reshape(rows, hd)], axis=1)
        acc[...] += jnp.dot(pair, wo_v[n * hd:(n + 2) * hd, :], preferred_element_type=F32)
    forward(2)
    from_pair(2)
    down(5)
    down(6)
    from_pair(3)
    down(7)

    part = lax.dot_general(perm_v[...], acc[...].astype(BF16), (((0,), (0,)), ((), ())), preferred_element_type=F32)
    y_s[...] = part.astype(BF16).reshape(ny, yb, dl)
    y_cp = [remote(y_s.at[y_peers[k - 1]], y_r.at[k], y_ss.at[k], y_rs.at[k], ty=y_peers[k - 1]) for k in range(1, ny)]
    for c in y_cp:
        c.start()
    total = x_v[pl.ds(pl.multiple_of(row * yb, yb), yb), :].astype(F32) + y_s[row].astype(F32)
    with scope("y"):
        for k in range(1, ny):
            y_cp[k - 1].wait_recv()
            total = total + y_r[k].astype(F32)
    yf[row] = total.astype(BF16)
    f_cp = [remote(yf.at[row], yf.at[row], f_ss.at[k], f_rs.at[k], ty=y_peers[k - 1]) for k in range(1, ny)]
    for c in f_cp:
        c.start()
    with scope("f"):
        for k in range(1, ny):
            src = y_froms[k - 1]
            remote(yf.at[src], yf.at[src], f_ss.at[k], f_rs.at[k], ty=y_peers[k - 1]).wait_recv()
    y_out[...] = yf[...].reshape(rows, dl)

    with scope("sends"):
        for c in stat_cp + [qd_cp] + qx_cp + qy_cp + ay_cp + g_cp + y_cp + f_cp:
            c.wait_send()
        for s in range(nx):
            d_copy(s).wait_send()
            gp_copy(s).wait_send()
            for t in range(SUBS):
                bp_copy(s, t).wait_send()
        for s in range(nx - 1):
            for t in range(SUBS):
                r_copy(s, t).wait_send()
                b_copy(s, t).wait_send()


def store_kernel(ny, ntx, lens_ref, y_v, new_v, k_v, v_v, y_h, ko_h, vo_h, patch, y_sem, out_sem):
    first = (lax.axis_index("ty") * ntx + lax.axis_index("tx")) * k_v.shape[0]
    sb, ctx, hd = k_v.shape
    pieces = ctx // PIECE
    y_cp = pltpu.make_async_copy(y_v, y_h, y_sem)
    y_cp.start()

    def write(a, buf, out):
        def sequence(r, carry):
            length = lens_ref[first + r]
            spot = lax.div(length, PIECE)
            at = pl.ds(pl.multiple_of(spot * PIECE, PIECE), PIECE)
            here = lax.broadcasted_iota(jnp.int32, (PIECE, hd), 0) == length - spot * PIECE
            patch[a, r] = jnp.where(here, new_v[pl.ds(a * sb + r, 1), :], buf[r, at, :].astype(F32)).astype(BF16)
            pltpu.make_async_copy(patch.at[a, r], out.at[r, at], out_sem.at[a, r, 0]).start()

            def other(c, inner):
                c = c + jnp.where(c >= spot, 1, 0)
                rest = pl.ds(pl.multiple_of(c * PIECE, PIECE), PIECE)
                pltpu.make_async_copy(buf.at[r, rest], out.at[r, rest], out_sem.at[a, r, 1]).start()
                return inner

            lax.fori_loop(0, pieces - 1, other, 0)
            return carry

        lax.fori_loop(0, sb, sequence, 0)

    def finish(a, buf, out):
        for r in range(sb):
            pltpu.make_async_copy(patch.at[a, r], out.at[r, pl.ds(0, PIECE)], out_sem.at[a, r, 0]).wait()
            rest = pl.ds(0, ctx - PIECE)
            pltpu.make_async_copy(buf.at[r, rest], out.at[r, rest], out_sem.at[a, r, 1]).wait()

    write(0, k_v, ko_h)
    write(1, v_v, vo_h)
    y_cp.wait()
    finish(0, k_v, ko_h)
    finish(1, v_v, vo_h)


def solution(mesh):
    ny = mesh.shape["ty"]
    ntx = mesh.shape["tx"]
    nx = ntx // 2
    cache_spec = P(("dp", "ty", "tx"), None, None)
    vspec = pl.BlockSpec(memory_space=VMEM)
    hspec = pl.BlockSpec(memory_space=pltpu.HBM)
    sspec = pl.BlockSpec(memory_space=pltpu.SMEM)

    def layer_shard(x_blk, lens_part, k_blk, v_blk, gamma_blk, w_query, w_key, w_value, w_gate, w_up, w_out, w_down):
        rows, dl = x_blk.shape
        sb, ctx, hd = k_blk.shape
        qn = w_query.shape[1]
        lh = qn // hd
        qw = qn + 2 * hd
        fb = w_gate.shape[1] // ntx
        rb = rows // ntx
        yb = rows // ny

        natural = np.arange(rows)
        order = np.reshape(np.transpose(np.reshape(natural, (ny, ntx, sb)), (1, 0, 2)), (rows,))
        perm = jnp.asarray(order[:, None] == natural[None, :], dtype=BF16)
        freqs = np.power(ROPE_BASE, -(np.arange(hd // 2, dtype=np.float32) * 2.0) / hd).astype(np.float32)
        freqs = jnp.asarray(np.tile(np.concatenate([freqs, freqs])[None, :], (8, 1)))

        y_vm, new_rows, k_vm, v_vm = pl.pallas_call(
            functools.partial(step_kernel, ny, nx, dl * ntx),
            out_shape=(
                pltpu.VMEM((rows, dl), BF16),
                pltpu.VMEM((2 * sb, hd), F32),
                pltpu.VMEM(k_blk.shape, BF16),
                pltpu.VMEM(v_blk.shape, BF16),
            ),
            in_specs=[sspec] + [hspec] * 13,
            out_specs=(vspec,) * 4,
            scratch_shapes=[
                VMEM((rows, dl), BF16), VMEM((dl,), F32), VMEM((rows, rows), BF16), VMEM((8, hd), F32),
                VMEM((dl, qw), BF16), VMEM((ntx, dl, 2 * fb), BF16), VMEM((qn, dl), BF16), VMEM((ntx, fb, dl), BF16),
                VMEM((rows, dl), BF16), VMEM((8, rows), F32), VMEM((ntx, 8, rows), F32),
                VMEM((ntx, rb, qw), F32), VMEM((nx, rb, qw), BF16), VMEM((nx, rb, qw), BF16),
                VMEM((nx, rb, qw), BF16), VMEM((nx, rb, qw), BF16), VMEM((rb, qw), F32), VMEM((2, rb, hd), F32),
                VMEM((ny, sb * lh, hd), F32), VMEM((ny, sb * lh, hd), F32),
                VMEM((nx, rows, 2 * fb), F32), VMEM((nx, rows, 2 * fb), BF16), VMEM((nx, rows, 2 * fb), BF16),
                VMEM((nx - 1, rows, 2 * fb), BF16), VMEM((nx - 1, rows, 2 * fb), BF16),
                VMEM((2, 8, hd), F32), VMEM((ny * lh, hd), F32), VMEM((ny * lh, ctx), F32), VMEM((ny, sb * lh, hd), F32),
                VMEM((ny, sb * lh, hd), BF16), VMEM((ny, sb * lh, hd), BF16), VMEM((lh, rb, hd), F32),
                VMEM((ntx, lh, rb, hd), BF16), VMEM((ntx, rows, fb), BF16), VMEM((rows, dl), F32),
                VMEM((ny, yb, dl), BF16), VMEM((ny, yb, dl), BF16), VMEM((ny, yb, dl), BF16),
                DMA((4,)), DMA((3,)), DMA((ntx, 2)), DMA((2, sb)), DMA, DMA((ntx,)),
                DMA((ntx,)), DMA((ntx,)), DMA, DMA, DMA((nx,)), DMA((nx,)), DMA((ny,)), DMA((ny,)),
                DMA((nx,)), DMA((nx,)), DMA((nx - 1, SUBS)), DMA((nx - 1, SUBS)),
                DMA((ny,)), DMA((ny,)), DMA((nx,)), DMA((nx,)), DMA((nx,)), DMA((nx,)),
                DMA((nx - 1, SUBS)), DMA((nx - 1, SUBS)), DMA((nx, SUBS)), DMA((nx, SUBS)), DMA((ny,)), DMA((ny,)), DMA((ny,)), DMA((ny,)),
            ],
            compiler_params=pltpu.CompilerParams(collective_id=0, has_side_effects=True, vmem_limit_bytes=52 * 1024 * 1024),
            name="step",
        )(lens_part, x_blk, gamma_blk, perm, freqs, w_query, w_key, w_value, w_gate, w_up, k_blk, v_blk, w_out, w_down)

        return pl.pallas_call(
            functools.partial(store_kernel, ny, ntx),
            out_shape=(
                jax.ShapeDtypeStruct((rows, dl), BF16),
                jax.ShapeDtypeStruct(k_blk.shape, BF16),
                jax.ShapeDtypeStruct(v_blk.shape, BF16),
            ),
            in_specs=[sspec] + [vspec] * 4,
            out_specs=(hspec,) * 3,
            scratch_shapes=[VMEM((2, sb, PIECE, hd), BF16), DMA, DMA((2, sb, 2))],
            compiler_params=pltpu.CompilerParams(vmem_limit_bytes=4 * 1024 * 1024),
            name="store",
        )(lens_part, y_vm, new_rows, k_vm, v_vm)

    in_specs = (P("dp", "tx"), P("dp"), cache_spec, cache_spec, P("tx"), P("tx", "ty"), P("tx", None), P("tx", None), P("tx", "ty"), P("tx", "ty"), P("ty", "tx"), P("ty", "tx"))
    out_specs = (P("dp", "tx"), cache_spec, cache_spec)
    return jax.shard_map(layer_shard, mesh=mesh, in_specs=in_specs, out_specs=out_specs, check_vma=False)
```

time: 262 us -> 69.8 us (0.27)
  waiting for transfers between devices: 149 us -> 0 us
  Pallas kernels: 0 us -> 69.1 us
  matrix products: 33.6 us -> 0 us
  blocking collectives: 33.6 us -> 0 us
  other arithmetic: 18 us -> 0 us
  between operations: 13.9 us -> 0.66 us
  starting transfers between devices: 8.41 us -> 0 us
  local copies, waits for them, and re-layouts: 4.33 us -> 0.01 us
    psum x3 -> x0, waiting for transfers between devices: 148 us -> none  [the longest x2 108 us: layer_shard(): q_sum, k_sum, v_new, gate, up_proj = lax.psum(partials, 'tx')]
    pallas_call x0 -> x2, Pallas kernels: none -> 69.1 us  [the longest x1 65.1 us: layer_shard(): pl.pallas_call(functools.partial(step_kernel, ny, nx, dl * ntx), out_shap...]
    dot_general x8 -> x0, matrix products: 27.3 us -> none  [the longest x5 13.6 us: layer_shard(): jnp.dot(normed, weight, preferred_element_type=jnp.float32)]
    all_gather x1 -> x0, blocking collectives: 19.7 us -> none  [layer_shard(): lax.all_gather(att_column, 'tx', axis=1, tiled=False)]
    psum x1 -> x0, blocking collectives: 13.9 us -> none  [layer_shard(): row_stats = lax.psum(row_stats, 'tx')]
    select_n x1 -> x0, other arithmetic: 11.4 us -> none  [layer_shard(): v_out = jnp.where(at_slot, v_own[:, None, :], v_blk)]
    all_to_all x2 -> x0, starting transfers between devices: 8.28 us -> none  [the longest x1 4.25 us: layer_shard(): att_column = lax.all_to_all(att_owned, 'ty', 0, 0, tiled=True)]
    sub x1 -> x0, matrix products: 6.24 us -> none  [layer_shard(): att_probs = jax.nn.softmax(scores, axis=-1).astype(jnp.bfloat16)]
  transfers between devices with their start and end apart: 5 -> 0, of which waited for: 3 -> 0; matrix products, arithmetic and copies ran while one was open for 12% -> 0% of each run, Pallas kernels for 0% -> 0%
where the time goes in v2:
time: 69.8 us; the launch traced here: 69.7 us
  Pallas kernels  69.1 us (99%)
    pallas_call x1, Pallas kernels, layer_shard(): pl.pallas_call(functools.partial(step_kernel, ny, nx, dl * ntx), out_shap...  65.1 us
    pallas_call x1, Pallas kernels, layer_shard(): pl.pallas_call(functools.partial(store_kernel, ny, ntx), out_shape=(jax.S...  3.98 us

profile of v2, /device:TPU:97, one launch (start us, length us, event | category | flops | bytes accessed | tf_op | source)
XLA Modules:
  0.0 69.7 jit_solution(13294815446344429612)
XLA Ops:
  0.6 0.0 copy-start
  0.6 65.1 %step.1 = (bf16[128,768]{1,0:T(8,128)(2,1)S(1)}, f32[8,128]{1,0:T(8,128)S(1)}, bf16[4,4096,128]{2,1,0:T(8,128)(2,1)S(1)}, bf16[4,4096,128]{2,1,0:T(8,128)(2,1)S(1)}) custom-call(s32[128]{0:T(128)} %lens_ref.3, bf16[128,768]{1,0:T(8,128)(2,1)} %x_h.1, f32[768]{0:T(1024)} %gamma_h.1, bf16[128,128]{1,0:T(8,128)(2,1)} %constant.4.clone.perm_h, ...), custom_call_target="tpu_custom_call" | custom-call | tf_op jit(solution)/shard_map/step/pallas_call | solution.py:504
  65.8 0.0 copy-done
  65.8 4.0 %store.1 = (bf16[128,768]{1,0:T(8,128)(2,1)}, bf16[4,4096,128]{2,1,0:T(8,128)(2,1)}, bf16[4,4096,128]{2,1,0:T(8,128)(2,1)}) custom-call(s32[128]{0:T(128)S(1)} %copy-done, bf16[128,768]{1,0:T(8,128)(2,1)S(1)} %get-tuple-element.7.y_v, f32[8,128]{1,0:T(8,128)S(1)} %get-tuple-element.8.new_v, bf16[4,4096,128]{2,1,0:T(8,128)(2,1)S(1)} %get-tuple-element.9.k_v, ...), custom_call_target="tpu_custom_call" | custom-call | tf_op jit(solution)/shard_map/store/pallas_call | solution.py:537
Async XLA Ops:
  0.6 65.1 %copy-start = (s32[128]{0:T(128)S(1)}, s32[128]{0:T(128)}, u32[]{:S(2)}) copy-start(s32[128]{0:T(128)} %lens_ref.3) | copy-start | bytes 1540

commit v3 on v2

--- a/solution.py
+++ b/solution.py
@@ -106,19 +106,16 @@
     k_in = [pltpu.make_async_copy(k_h.at[r], kbuf.at[r], kv_sem.at[0, r]) for r in range(sb)]
     v_in = [pltpu.make_async_copy(v_h.at[r], vbuf.at[r], kv_sem.at[1, r]) for r in range(sb)]
     wo_load = pltpu.make_async_copy(wo_h, wo_v, wo_sem)
-    for c in first_loads + q_loads:
+    for c in first_loads:
+        c.start()
+    for c in first_loads:
+        c.wait()
+    for c in q_loads:
         c.start()
     for n in range(ntx):
         for c in block_loads(n, block_of(n // 2, n % 2 == 1)):
             c.start()
-    for c in k_in + v_in:
-        c.start()
-    for n in range(ntx):
-        wd_load(n, held(n // 2, n % 2 == 0)).start()
-    wo_load.start()
-
-    for c in first_loads:
-        c.wait()
+
     xp = jnp.dot(perm_v[...], x_v[...], preferred_element_type=F32)
     s1 = jnp.sum(xp, axis=1, keepdims=True)
     s2 = jnp.sum(xp * xp, axis=1, keepdims=True)
@@ -218,8 +215,13 @@
 
         return carry
 
+    for c in k_in + v_in:
+        c.start()
     with scope("products"):
         lax.fori_loop(0, nx, product, 0)
+    for n in range(ntx):
+        wd_load(n, held(n // 2, n % 2 == 0)).start()
+    wo_load.start()
 
     def ring(s, t):
         at = piece(t)
@@ -375,8 +377,8 @@
         b_copy(0, t).start()
         bp_copy(0, t).start()
     down(0, True)
+    forward(0)
     att_rows()
-    forward(0)
     from_pair(0)
     down(1)
     down(2)
@@ -447,10 +449,6 @@
         def sequence(r, carry):
             length = lens_ref[first + r]
             spot = lax.div(length, PIECE)
-            at = pl.ds(pl.multiple_of(spot * PIECE, PIECE), PIECE)
-            here = lax.broadcasted_iota(jnp.int32, (PIECE, hd), 0) == length - spot * PIECE
-            patch[a, r] = jnp.where(here, new_v[pl.ds(a * sb + r, 1), :], buf[r, at, :].astype(F32)).astype(BF16)
-            pltpu.make_async_copy(patch.at[a, r], out.at[r, at], out_sem.at[a, r, 0]).start()
 
             def other(c, inner):
                 c = c + jnp.where(c >= spot, 1, 0)
@@ -459,6 +457,10 @@
                 return inner
 
             lax.fori_loop(0, pieces - 1, other, 0)
+            at = pl.ds(pl.multiple_of(spot * PIECE, PIECE), PIECE)
+            here = lax.broadcasted_iota(jnp.int32, (PIECE, hd), 0) == length - spot * PIECE
+            patch[a, r] = jnp.where(here, new_v[pl.ds(a * sb + r, 1), :], buf[r, at, :].astype(F32)).astype(BF16)
+            pltpu.make_async_copy(patch.at[a, r], out.at[r, at], out_sem.at[a, r, 0]).start()
             return carry
 
         lax.fori_loop(0, sb, sequence, 0)

time: 69.8 us -> 62.2 us (0.89)
  Pallas kernels: 69.1 us -> 61.5 us
    pallas_call x1, Pallas kernels: 65.1 us -> 57.5 us  [layer_shard(): pl.pallas_call(functools.partial(step_kernel, ny, nx, dl * ntx), out_shap...]
where the time goes in v3:
time: 62.2 us; the launch traced here: 62.1 us
  Pallas kernels  61.5 us (99%)
  between operations  0.66 us (1%)
    pallas_call x1, Pallas kernels, layer_shard(): pl.pallas_call(functools.partial(step_kernel, ny, nx, dl * ntx), out_shap...  57.5 us
    pallas_call x1, Pallas kernels, layer_shard(): pl.pallas_call(functools.partial(store_kernel, ny, ntx), out_shape=(jax.S...  3.98 us

profile of v3, /device:TPU:97, one launch (start us, length us, event | category | flops | bytes accessed | tf_op | source)
XLA Modules:
  0.0 62.1 jit_solution(7423998146983544318)
XLA Ops:
  0.6 0.0 copy-start
  0.6 57.5 %step.1 = (bf16[128,768]{1,0:T(8,128)(2,1)S(1)}, f32[8,128]{1,0:T(8,128)S(1)}, bf16[4,4096,128]{2,1,0:T(8,128)(2,1)S(1)}, bf16[4,4096,128]{2,1,0:T(8,128)(2,1)S(1)}) custom-call(s32[128]{0:T(128)} %lens_ref.3, bf16[128,768]{1,0:T(8,128)(2,1)} %x_h.1, f32[768]{0:T(1024)} %gamma_h.1, bf16[128,128]{1,0:T(8,128)(2,1)} %constant.4.clone.perm_h, ...), custom_call_target="tpu_custom_call" | custom-call | tf_op jit(solution)/shard_map/step/pallas_call | solution.py:506
  58.1 0.0 copy-done
  58.1 4.0 %store.1 = (bf16[128,768]{1,0:T(8,128)(2,1)}, bf16[4,4096,128]{2,1,0:T(8,128)(2,1)}, bf16[4,4096,128]{2,1,0:T(8,128)(2,1)}) custom-call(s32[128]{0:T(128)S(1)} %copy-done, bf16[128,768]{1,0:T(8,128)(2,1)S(1)} %get-tuple-element.7.y_v, f32[8,128]{1,0:T(8,128)S(1)} %get-tuple-element.8.new_v, bf16[4,4096,128]{2,1,0:T(8,128)(2,1)S(1)} %get-tuple-element.9.k_v, ...), custom_call_target="tpu_custom_call" | custom-call | tf_op jit(solution)/shard_map/store/pallas_call | solution.py:539
Async XLA Ops:
  0.6 57.5 %copy-start = (s32[128]{0:T(128)S(1)}, s32[128]{0:T(128)}, u32[]{:S(2)}) copy-start(s32[128]{0:T(128)} %lens_ref.3) | copy-start | bytes 1540

commit v4 on v3

--- a/solution.py
+++ b/solution.py
@@ -33,10 +33,10 @@
 
 def step_kernel(ny, nx, d_model, lens_ref, x_h, gamma_h, perm_h, freq_h, wq_h, wk_h, wv_h, wg_h, wu_h, k_h, v_h, wo_h, wd_h,
                 y_out, new_out, kbuf, vbuf,
-                x_v, gamma_v, perm_v, freq_v, wq_v, wb_v, wo_v, wd_v, h_v, stat_s, stat_r,
+                x_v, gamma_v, perm_v, freq_v, wq_v, wb_v, wo_v, wd_v, h_v, stat_s, stat_r, gq_s, gq_r, gb_s, gb_r, norm,
                 qp, qd_s, qd_r, qx_s, qx_r, qsum, kvs, qy_s, qy_r, own, d_s, d_r, r_s, r_r,
                 turns, qs, sbuf, o32, ay_s, ay_r, g32, g_v, b_v, acc, y_s, y_r, yf,
-                in_sem, wq_sem, wb_sem, kv_sem, wo_sem, wd_sem, stat_ss, stat_rs, qd_ss, qd_rs, qx_ss, qx_rs, qy_ss, qy_rs,
+                in_sem, wq_sem, wb_sem, kv_sem, wo_sem, wd_sem, stat_ss, stat_rs, gq_ss, gq_rs, gb_ss, gb_rs, qd_ss, qd_rs, qx_ss, qx_rs, qy_ss, qy_rs,
                 d_ss, d_rs, r_ss, r_rs, ay_ss, ay_rs, g_ss, g_rs, gp_ss, gp_rs, b_ss, b_rs, bp_ss, bp_rs, y_ss, y_rs, f_ss, f_rs):
     row = lax.axis_index("ty")
     col = lax.axis_index("tx")
@@ -84,8 +84,8 @@
     def block_loads(n, b):
         at = pl.ds(pl.multiple_of(b * fb, fb), fb)
         return [
-            pltpu.make_async_copy(wg_h.at[:, at], wb_v.at[n, :, pl.ds(0, fb)], wb_sem.at[n, 0]),
-            pltpu.make_async_copy(wu_h.at[:, at], wb_v.at[n, :, pl.ds(fb, fb)], wb_sem.at[n, 1]),
+            pltpu.make_async_copy(wg_h.at[:, at], wb_v.at[n, :, pl.ds(0, fb)], wb_sem.at[n]),
+            pltpu.make_async_copy(wu_h.at[:, at], wb_v.at[n, :, pl.ds(fb, fb)], wb_sem.at[n]),
         ]
 
     def wd_load(n, b):
@@ -99,9 +99,9 @@
         pltpu.make_async_copy(freq_h, freq_v, in_sem.at[3]),
     ]
     q_loads = [
-        pltpu.make_async_copy(wq_h, wq_v.at[:, pl.ds(0, qn)], wq_sem.at[0]),
-        pltpu.make_async_copy(wk_h, wq_v.at[:, pl.ds(qn, hd)], wq_sem.at[1]),
-        pltpu.make_async_copy(wv_h, wq_v.at[:, pl.ds(qn + hd, hd)], wq_sem.at[2]),
+        pltpu.make_async_copy(wq_h, wq_v.at[:, pl.ds(0, qn)], wq_sem),
+        pltpu.make_async_copy(wk_h, wq_v.at[:, pl.ds(qn, hd)], wq_sem),
+        pltpu.make_async_copy(wv_h, wq_v.at[:, pl.ds(qn + hd, hd)], wq_sem),
     ]
     k_in = [pltpu.make_async_copy(k_h.at[r], kbuf.at[r], kv_sem.at[0, r]) for r in range(sb)]
     v_in = [pltpu.make_async_copy(v_h.at[r], vbuf.at[r], kv_sem.at[1, r]) for r in range(sb)]
@@ -117,48 +117,62 @@
             c.start()
 
     xp = jnp.dot(perm_v[...], x_v[...], preferred_element_type=F32)
-    s1 = jnp.sum(xp, axis=1, keepdims=True)
-    s2 = jnp.sum(xp * xp, axis=1, keepdims=True)
+    own_mean = jnp.sum(xp, axis=1, keepdims=True) / dl
+    xc = xp - own_mean
+    gamma = gamma_v[...].reshape(1, dl)
+    h_v[:rows] = (xc * gamma).astype(BF16)
+    extra = lax.broadcasted_iota(jnp.int32, (16, dl), 0)
+    h_v[rows:] = jnp.where(extra == 0, gamma, jnp.where(extra == 1, gamma - gamma.astype(BF16).astype(F32), 0.0)).astype(BF16)
     lane = lax.broadcasted_iota(jnp.int32, (rows, rows), 1)
-    both = jnp.where(lane == 0, s1, jnp.where(lane == 1, s2, 0.0))
+    both = jnp.where(lane == 0, own_mean, jnp.where(lane == 1, jnp.sum(xc * xc, axis=1, keepdims=True), 0.0))
     stat_s[...] = jnp.transpose(both)[:8]
 
-    at_row = lax.broadcasted_iota(jnp.int32, (8, hd), 0)
-    places = jnp.zeros((8, hd), F32)
-    for r in range(sb):
-        places = jnp.where(at_row == r, lens_ref[(row * ntx + col) * sb + r].astype(F32), places)
-    angles = places * freq_v[...]
-    turns[0] = jnp.cos(angles)
-    low_half = lax.broadcasted_iota(jnp.int32, (8, hd), 1) < hd // 2
-    sines = jnp.sin(angles)
-    turns[1] = jnp.where(low_half, -sines, sines)
-
-    with scope("greet"):
-        pl.semaphore_wait(barrier, ntx - 1 + ny - 1)
-
-    stat_cp = [remote(stat_s, stat_r.at[k], stat_ss.at[k], stat_rs.at[k], tx=tx_peers[k - 1]) for k in range(1, ntx)]
-    for c in stat_cp:
-        c.start()
-    total = stat_s[...]
-    with scope("stat"):
-        for k, c in enumerate(stat_cp):
-            c.wait_recv()
-            total = total + stat_r[k + 1]
-    square = jnp.transpose(jnp.concatenate([total, jnp.zeros((rows - 8, rows), F32)], axis=0))
-    mean = square[:, 0:1] / d_model
-    var = square[:, 1:2] / d_model - mean * mean
-    h_v[...] = ((xp - mean) * lax.rsqrt(var + EPSILON) * gamma_v[...].reshape(1, dl)).astype(BF16)
-
-    for c in q_loads:
-        c.wait()
-    qp[...] = jnp.dot(h_v[...], wq_v[...], preferred_element_type=F32).reshape(ntx, rb, qw)
+    def gamma_row(vals, tiles):
+        row_sum = vals[0:1, :] + vals[1:2, :]
+        parts = [row_sum[:, n * hd:(n + 1) * hd] for n in range(tiles)]
+        return jnp.concatenate(parts + [jnp.zeros((16 - tiles, hd), F32)], axis=0).astype(BF16)
+
+    pltpu.make_async_copy(wq_v, wq_v, wq_sem).wait()
+    part = jnp.dot(h_v[...], wq_v[...], preferred_element_type=F32)
+    qp[...] = part[:rows].reshape(ntx, rb, qw)
+    gq_s[...] = gamma_row(part[rows:], qw // hd)
     for n in range(nx):
         qd_s[n] = qp[2 * n + 1 - core].astype(BF16)
     qd_cp = remote(qd_s, qd_r, qd_ss, qd_rs, tx=partner)
+    stat_cp = [remote(stat_s, stat_r.at[k], stat_ss, stat_rs, tx=tx_peers[k - 1]) for k in range(1, ntx)]
+    gq_cp = [remote(gq_s, gq_r.at[k], gq_ss, gq_rs, tx=tx_peers[k - 1]) for k in range(1, ntx)]
+    gb_cp = [remote(gb_s.at[tx_peers[k - 1]], gb_r.at[k], gb_ss, gb_rs, tx=tx_peers[k - 1]) for k in range(1, ntx)]
+    with scope("greet"):
+        pl.semaphore_wait(barrier, ntx - 1 + ny - 1)
     qd_cp.start()
-    qx_cp = [remote(qx_s.at[k], qx_r.at[k], qx_ss.at[k], qx_rs.at[k], tx=x_peers[k - 1]) for k in range(1, nx)]
-    qy_cp = [remote(qy_s.at[y_peers[k - 1]], qy_r.at[row], qy_ss.at[k], qy_rs.at[k], ty=y_peers[k - 1]) for k in range(1, ny)]
-    qy_in = [remote(qy_s.at[y_froms[k - 1]], qy_r.at[y_froms[k - 1]], qy_ss.at[k], qy_rs.at[k], ty=y_peers[k - 1]) for k in range(1, ny)]
+    for c in stat_cp + gq_cp:
+        c.start()
+    stat_r[0] = stat_s[...]
+    gq_r[0] = gq_s[...]
+
+    def rest_of_norm():
+        with scope("stat"):
+            remote(stat_r.at[pl.ds(1, ntx - 1)], stat_r.at[pl.ds(1, ntx - 1)], stat_ss, stat_rs, tx=partner).wait_recv()
+            remote(gq_r.at[pl.ds(1, ntx - 1)], gq_r.at[pl.ds(1, ntx - 1)], gq_ss, gq_rs, tx=partner).wait_recv()
+        means = jnp.concatenate([stat_r[k, 0:1, :] for k in range(ntx)], axis=0)
+        squares = jnp.concatenate([stat_r[k, 1:2, :] for k in range(ntx)], axis=0)
+        off = means - jnp.sum(means, axis=0, keepdims=True) / ntx
+        var = jnp.sum(squares, axis=0, keepdims=True) / d_model + jnp.sum(off * off, axis=0, keepdims=True) / ntx
+        scale = lax.rsqrt(var + EPSILON)
+        norm[...] = jnp.transpose(jnp.concatenate([off, scale, jnp.zeros((rows - ntx - 1, rows), F32)], axis=0))
+
+    def normed(vals, at, g_ref):
+        cols = norm[at, :]
+        tiles = []
+        for n in range(vals.shape[1] // hd):
+            tile = vals[:, n * hd:(n + 1) * hd]
+            for k in range(ntx):
+                tile = tile + cols[:, k:k + 1] * g_ref[k, n:n + 1, :].astype(F32)
+            tiles.append(tile * cols[:, ntx:ntx + 1])
+        return jnp.concatenate(tiles, axis=1)
+
+    qx_cp = [remote(qx_s.at[k], qx_r.at[k], qx_ss, qx_rs, tx=x_peers[k - 1]) for k in range(1, nx)]
+    qy_cp = [remote(qy_s.at[y_peers[k - 1]], qy_r.at[row], qy_ss, qy_rs, ty=y_peers[k - 1]) for k in range(1, ny)]
 
     def q_pair():
         with scope("qd"):
@@ -170,10 +184,12 @@
 
     def q_rows():
         mine = qp[2 * chip + core] + qd_r[chip].astype(F32)
+        rest_of_norm()
         with scope("qx"):
-            for k in range(1, nx):
-                qx_cp[k - 1].wait_recv()
-                mine = mine + qx_r[k].astype(F32)
+            remote(qx_r.at[pl.ds(1, nx - 1)], qx_r.at[pl.ds(1, nx - 1)], qx_ss, qx_rs, tx=partner).wait_recv()
+        for k in range(1, nx):
+            mine = mine + qx_r[k].astype(F32)
+        mine = normed(mine, pl.ds(pl.multiple_of(col * rb, rb), rb), gq_r)
         qsum[...] = mine
         kvs[0] = mine[:, qn:qn + hd]
         kvs[1] = mine[:, qn + hd:]
@@ -184,25 +200,38 @@
             c.start()
         qy_r[row] = qy_s[row]
 
+    def tables():
+        at_row = lax.broadcasted_iota(jnp.int32, (8, hd), 0)
+        places = jnp.zeros((8, hd), F32)
+        for r in range(sb):
+            places = jnp.where(at_row == r, lens_ref[(row * ntx + col) * sb + r].astype(F32), places)
+        angles = places * freq_v[...]
+        turns[0] = jnp.cos(angles)
+        low_half = lax.broadcasted_iota(jnp.int32, (8, hd), 1) < hd // 2
+        sines = jnp.sin(angles)
+        turns[1] = jnp.where(low_half, -sines, sines)
+
     def d_copy(s):
-        return remote(d_s.at[s], d_r.at[s], d_ss.at[s], d_rs.at[s], tx=partner)
+        return remote(d_s.at[s], d_r.at[s], d_ss, d_rs.at[s], tx=partner)
 
     def r_copy(s, t):
-        return remote(r_s.at[s, piece(t)], r_r.at[s, piece(t)], r_ss.at[s, t], r_rs.at[s, t], tx=after)
+        return remote(r_s.at[s, piece(t)], r_r.at[s, piece(t)], r_ss, r_rs.at[s, t], tx=after)
 
     def product(s, carry):
-        for c in block_loads(2 * s, 0):
-            c.wait()
-        d_s[s] = jnp.dot(h_v[...], wb_v[2 * s], preferred_element_type=F32).astype(BF16)
+        pltpu.make_async_copy(wb_v.at[2 * s], wb_v.at[2 * s], wb_sem.at[2 * s]).wait()
+        part = jnp.dot(h_v[...], wb_v[2 * s], preferred_element_type=F32)
+        d_s[s] = part[:rows].astype(BF16)
         d_copy(s).start()
+        gb_s[block_of(s, False)] = gamma_row(part[rows:], 2 * fb // hd)
 
         @pl.when(s == 0)
         def _():
             q_pair()
 
-        for c in block_loads(2 * s + 1, 0):
-            c.wait()
-        own[s] = jnp.dot(h_v[...], wb_v[2 * s + 1], preferred_element_type=F32)
+        pltpu.make_async_copy(wb_v.at[2 * s + 1], wb_v.at[2 * s + 1], wb_sem.at[2 * s + 1]).wait()
+        part = jnp.dot(h_v[...], wb_v[2 * s + 1], preferred_element_type=F32)
+        own[s] = part[:rows]
+        gb_s[block_of(s, True)] = gamma_row(part[rows:], 2 * fb // hd)
 
         @pl.when(s == 0)
         def _():
@@ -215,13 +244,12 @@
 
         return carry
 
-    for c in k_in + v_in:
-        c.start()
     with scope("products"):
         lax.fori_loop(0, nx, product, 0)
-    for n in range(ntx):
-        wd_load(n, held(n // 2, n % 2 == 0)).start()
-    wo_load.start()
+    for c in gb_cp + k_in + v_in:
+        c.start()
+    gb_r[0] = gb_s[col]
+    tables()
 
     def ring(s, t):
         at = piece(t)
@@ -236,6 +264,10 @@
             r_s[s, at] = part.astype(BF16)
             r_copy(s, t).start()
         else:
+            if t == 0:
+                with scope("gb"):
+                    remote(gb_r.at[pl.ds(1, ntx - 1)], gb_r.at[pl.ds(1, ntx - 1)], gb_ss, gb_rs, tx=partner).wait_recv()
+            part = normed(part, at, gb_r)
             gate = part[:, :fb].astype(BF16).astype(F32)
             up = part[:, fb:].astype(BF16).astype(F32)
             b_v[col, at] = (gate * (1.0 / (1.0 + jnp.exp(-gate))) * up).astype(BF16)
@@ -279,38 +311,29 @@
 
     def b_copy(s, t):
         b = held(s, True)
-        return remote(b_v.at[b, piece(t)], b_v.at[b, piece(t)], b_ss.at[s, t], b_rs.at[s, t], tx=after)
+        return remote(b_v.at[b, piece(t)], b_v.at[b, piece(t)], b_ss, b_rs.at[s, t], tx=after)
 
     def b_in(s, t):
         b = held(s + 1, True)
-        return remote(b_v.at[b, piece(t)], b_v.at[b, piece(t)], b_ss.at[s, t], b_rs.at[s, t], tx=after)
+        return remote(b_v.at[b, piece(t)], b_v.at[b, piece(t)], b_ss, b_rs.at[s, t], tx=after)
 
     def bp_copy(s, t):
         b = held(s, True)
-        return remote(b_v.at[b, piece(t)], b_v.at[b, piece(t)], bp_ss.at[s, t], bp_rs.at[s, t], tx=partner)
-
-    def bp_in(s, t):
-        b = held(s, False)
-        return remote(b_v.at[b, piece(t)], b_v.at[b, piece(t)], bp_ss.at[s, t], bp_rs.at[s, t], tx=partner)
-
-    ay_cp = [remote(ay_s.at[y_peers[k - 1]], ay_r.at[row], ay_ss.at[k], ay_rs.at[k], ty=y_peers[k - 1]) for k in range(1, ny)]
-    ay_in = [remote(ay_s.at[y_froms[k - 1]], ay_r.at[y_froms[k - 1]], ay_ss.at[k], ay_rs.at[k], ty=y_peers[k - 1]) for k in range(1, ny)]
-    g_cp = [remote(g_v.at[col], g_v.at[col], g_ss.at[k], g_rs.at[k], tx=x_peers[k - 1]) for k in range(1, nx)]
+        return remote(b_v.at[b, piece(t)], b_v.at[b, piece(t)], bp_ss, bp_rs.at[s], tx=partner)
+
+    ay_cp = [remote(ay_s.at[y_peers[k - 1]], ay_r.at[row], ay_ss, ay_rs, ty=y_peers[k - 1]) for k in range(1, ny)]
+    g_cp = [remote(g_v.at[col], g_v.at[col], g_ss, g_rs.at[k], tx=x_peers[k - 1]) for k in range(1, nx)]
 
     def g_from(k, mine):
         return 2 * lax.rem(chip - k + nx, nx) + (core if mine else 1 - core)
 
     def g_in(k):
         at = g_from(k, True)
-        return remote(g_v.at[at], g_v.at[at], g_ss.at[k], g_rs.at[k], tx=x_peers[k - 1])
+        return remote(g_v.at[at], g_v.at[at], g_ss, g_rs.at[k], tx=x_peers[k - 1])
 
     def gp_copy(k):
         at = g_from(k, True)
-        return remote(g_v.at[at], g_v.at[at], gp_ss.at[k], gp_rs.at[k], tx=partner)
-
-    def gp_in(k):
-        at = g_from(k, False)
-        return remote(g_v.at[at], g_v.at[at], gp_ss.at[k], gp_rs.at[k], tx=partner)
+        return remote(g_v.at[at], g_v.at[at], gp_ss, gp_rs, tx=partner)
 
     def att_out():
         ay_s[...] = o32[...].astype(BF16)
@@ -320,8 +343,7 @@
 
     def att_rows():
         with scope("ay"):
-            for c in ay_in:
-                c.wait_recv()
+            remote(ay_r.at[pl.ds(0, ny - 1)], ay_r.at[pl.ds(0, ny - 1)], ay_ss, ay_rs, ty=y_peers[0]).wait_recv()
         for a in range(ny):
             part = ay_r[a].astype(F32)
             for n in range(lh):
@@ -346,18 +368,20 @@
 
     def from_pair(s):
         with scope("bp%d" % s):
-            for t in range(SUBS):
-                bp_in(s, t).wait_recv()
+            b = held(s, False)
+            remote(b_v.at[b], b_v.at[b], bp_ss, bp_rs.at[s], tx=partner).wait_recv()
 
     ring(1, 0)
     q_rows()
     for t in range(1, SUBS):
         ring(1, t)
+    for n in range(ntx):
+        wd_load(n, held(n // 2, n % 2 == 0)).start()
+    wo_load.start()
     ring(2, 0)
     ring(2, 1)
     with scope("qy"):
-        for c in qy_in:
-            c.wait_recv()
+        remote(qy_r.at[pl.ds(0, ny - 1)], qy_r.at[pl.ds(0, ny - 1)], qy_ss, qy_rs, ty=y_peers[0]).wait_recv()
     with scope("a0"):
         attend(0)
     ring(2, 2)
@@ -391,8 +415,7 @@
     down(3)
     down(4)
     with scope("gp"):
-        for k in range(nx):
-            gp_in(k).wait_recv()
+        remote(g_v.at[pl.ds(0, nx)], g_v.at[pl.ds(0, nx)], gp_ss, gp_rs, tx=partner).wait_recv()
     wo_load.wait()
     for n in range(0, lh, 2):
         pair = jnp.concatenate([g_v[:, n].reshape(rows, hd), g_v[:, n + 1].reshape(rows, hd)], axis=1)
@@ -406,36 +429,32 @@
 
     part = lax.dot_general(perm_v[...], acc[...].astype(BF16), (((0,), (0,)), ((), ())), preferred_element_type=F32)
     y_s[...] = part.astype(BF16).reshape(ny, yb, dl)
-    y_cp = [remote(y_s.at[y_peers[k - 1]], y_r.at[k], y_ss.at[k], y_rs.at[k], ty=y_peers[k - 1]) for k in range(1, ny)]
+    y_cp = [remote(y_s.at[y_peers[k - 1]], y_r.at[k], y_ss, y_rs, ty=y_peers[k - 1]) for k in range(1, ny)]
     for c in y_cp:
         c.start()
     total = x_v[pl.ds(pl.multiple_of(row * yb, yb), yb), :].astype(F32) + y_s[row].astype(F32)
     with scope("y"):
-        for k in range(1, ny):
-            y_cp[k - 1].wait_recv()
-            total = total + y_r[k].astype(F32)
+        remote(y_r.at[pl.ds(1, ny - 1)], y_r.at[pl.ds(1, ny - 1)], y_ss, y_rs, ty=y_peers[0]).wait_recv()
+    for k in range(1, ny):
+        total = total + y_r[k].astype(F32)
     yf[row] = total.astype(BF16)
-    f_cp = [remote(yf.at[row], yf.at[row], f_ss.at[k], f_rs.at[k], ty=y_peers[k - 1]) for k in range(1, ny)]
+    f_cp = [remote(yf.at[row], yf.at[row], f_ss, f_rs, ty=y_peers[k - 1]) for k in range(1, ny)]
     for c in f_cp:
         c.start()
     with scope("f"):
-        for k in range(1, ny):
-            src = y_froms[k - 1]
-            remote(yf.at[src], yf.at[src], f_ss.at[k], f_rs.at[k], ty=y_peers[k - 1]).wait_recv()
+        remote(yf.at[pl.ds(0, ny - 1)], yf.at[pl.ds(0, ny - 1)], f_ss, f_rs, ty=y_peers[0]).wait_recv()
     y_out[...] = yf[...].reshape(rows, dl)
 
     with scope("sends"):
-        for c in stat_cp + [qd_cp] + qx_cp + qy_cp + ay_cp + g_cp + y_cp + f_cp:
-            c.wait_send()
-        for s in range(nx):
-            d_copy(s).wait_send()
-            gp_copy(s).wait_send()
-            for t in range(SUBS):
-                bp_copy(s, t).wait_send()
-        for s in range(nx - 1):
-            for t in range(SUBS):
-                r_copy(s, t).wait_send()
-                b_copy(s, t).wait_send()
+        qd_cp.wait_send()
+        for ref, send, recv in (
+            (stat_r.at[pl.ds(1, ntx - 1)], stat_ss, stat_rs), (gq_r.at[pl.ds(1, ntx - 1)], gq_ss, gq_rs), (gb_r.at[pl.ds(1, ntx - 1)], gb_ss, gb_rs),
+            (qx_s.at[pl.ds(1, nx - 1)], qx_ss, qx_rs), (qy_s.at[pl.ds(1, ny - 1)], qy_ss, qy_rs), (ay_s.at[pl.ds(1, ny - 1)], ay_ss, ay_rs),
+            (y_s.at[pl.ds(1, ny - 1)], y_ss, y_rs), (yf.at[pl.ds(1, ny - 1)], f_ss, f_rs),
+            (d_s, d_ss, d_rs.at[0]), (r_s, r_ss, r_rs.at[0, 0]), (g_v.at[pl.ds(1, nx - 1)], g_ss, g_rs.at[0]), (g_v.at[pl.ds(0, nx)], gp_ss, gp_rs),
+            (b_v.at[pl.ds(1, nx - 1)], b_ss, b_rs.at[0, 0]), (b_v.at[pl.ds(0, nx)], bp_ss, bp_rs.at[0]),
+        ):
+            remote(ref, ref, send, recv, tx=partner).wait_send()
 
 
 def store_kernel(ny, ntx, lens_ref, y_v, new_v, k_v, v_v, y_h, ko_h, vo_h, patch, y_sem, out_sem):
@@ -516,7 +535,8 @@
             scratch_shapes=[
                 VMEM((rows, dl), BF16), VMEM((dl,), F32), VMEM((rows, rows), BF16), VMEM((8, hd), F32),
                 VMEM((dl, qw), BF16), VMEM((ntx, dl, 2 * fb), BF16), VMEM((qn, dl), BF16), VMEM((ntx, fb, dl), BF16),
-                VMEM((rows, dl), BF16), VMEM((8, rows), F32), VMEM((ntx, 8, rows), F32),
+                VMEM((rows + 16, dl), BF16), VMEM((8, rows), F32), VMEM((ntx, 8, rows), F32),
+                VMEM((16, hd), BF16), VMEM((ntx, 16, hd), BF16), VMEM((ntx, 16, hd), BF16), VMEM((ntx, 16, hd), BF16), VMEM((rows, rows), F32),
                 VMEM((ntx, rb, qw), F32), VMEM((nx, rb, qw), BF16), VMEM((nx, rb, qw), BF16),
                 VMEM((nx, rb, qw), BF16), VMEM((nx, rb, qw), BF16), VMEM((rb, qw), F32), VMEM((2, rb, hd), F32),
                 VMEM((ny, sb * lh, hd), F32), VMEM((ny, sb * lh, hd), F32),
@@ -526,11 +546,11 @@
                 VMEM((ny, sb * lh, hd), BF16), VMEM((ny, sb * lh, hd), BF16), VMEM((lh, rb, hd), F32),
                 VMEM((ntx, lh, rb, hd), BF16), VMEM((ntx, rows, fb), BF16), VMEM((rows, dl), F32),
                 VMEM((ny, yb, dl), BF16), VMEM((ny, yb, dl), BF16), VMEM((ny, yb, dl), BF16),
-                DMA((4,)), DMA((3,)), DMA((ntx, 2)), DMA((2, sb)), DMA, DMA((ntx,)),
-                DMA((ntx,)), DMA((ntx,)), DMA, DMA, DMA((nx,)), DMA((nx,)), DMA((ny,)), DMA((ny,)),
-                DMA((nx,)), DMA((nx,)), DMA((nx - 1, SUBS)), DMA((nx - 1, SUBS)),
-                DMA((ny,)), DMA((ny,)), DMA((nx,)), DMA((nx,)), DMA((nx,)), DMA((nx,)),
-                DMA((nx - 1, SUBS)), DMA((nx - 1, SUBS)), DMA((nx, SUBS)), DMA((nx, SUBS)), DMA((ny,)), DMA((ny,)), DMA((ny,)), DMA((ny,)),
+                DMA((4,)), DMA, DMA((ntx,)), DMA((2, sb)), DMA, DMA((ntx,)),
+                DMA, DMA, DMA, DMA, DMA, DMA, DMA, DMA, DMA, DMA, DMA, DMA,
+                DMA, DMA((nx,)), DMA, DMA((nx - 1, SUBS)),
+                DMA, DMA, DMA, DMA((nx,)), DMA, DMA,
+                DMA, DMA((nx - 1, SUBS)), DMA, DMA((nx,)), DMA, DMA, DMA, DMA,
             ],
             compiler_params=pltpu.CompilerParams(collective_id=0, has_side_effects=True, vmem_limit_bytes=52 * 1024 * 1024),
             name="step",

time: 62.2 us -> 61.7 us (level)
  no operation moved by 1% of the time
where the time goes in v4:
time: 61.7 us; the launch traced here: 61.6 us
  Pallas kernels  61 us (99%)
  between operations  0.66 us (1%)
    pallas_call x1, Pallas kernels, layer_shard(): pl.pallas_call(functools.partial(step_kernel, ny, nx, dl * ntx), out_shap...  57 us
    pallas_call x1, Pallas kernels, layer_shard(): pl.pallas_call(functools.partial(store_kernel, ny, ntx), out_shape=(jax.S...  3.98 us

profile of v4, /device:TPU:97, one launch (start us, length us, event | category | flops | bytes accessed | tf_op | source)
XLA Modules:
  0.0 61.6 jit_solution(5686738202584510978)
XLA Ops:
  0.6 0.0 copy-start
  0.6 57.0 %step.1 = (bf16[128,768]{1,0:T(8,128)(2,1)S(1)}, f32[8,128]{1,0:T(8,128)S(1)}, bf16[4,4096,128]{2,1,0:T(8,128)(2,1)S(1)}, bf16[4,4096,128]{2,1,0:T(8,128)(2,1)S(1)}) custom-call(s32[128]{0:T(128)} %lens_ref.3, bf16[128,768]{1,0:T(8,128)(2,1)} %x_h.1, f32[768]{0:T(1024)} %gamma_h.1, bf16[128,128]{1,0:T(8,128)(2,1)} %constant.4.clone.perm_h, ...), custom_call_target="tpu_custom_call" | custom-call | tf_op jit(solution)/shard_map/step/pallas_call | solution.py:525
  57.6 0.0 copy-done
  57.6 4.0 %store.1 = (bf16[128,768]{1,0:T(8,128)(2,1)}, bf16[4,4096,128]{2,1,0:T(8,128)(2,1)}, bf16[4,4096,128]{2,1,0:T(8,128)(2,1)}) custom-call(s32[128]{0:T(128)S(1)} %copy-done, bf16[128,768]{1,0:T(8,128)(2,1)S(1)} %get-tuple-element.7.y_v, f32[8,128]{1,0:T(8,128)S(1)} %get-tuple-element.8.new_v, bf16[4,4096,128]{2,1,0:T(8,128)(2,1)S(1)} %get-tuple-element.9.k_v, ...), custom_call_target="tpu_custom_call" | custom-call | tf_op jit(solution)/shard_map/store/pallas_call | solution.py:559
Async XLA Ops:
  0.6 57.0 %copy-start = (s32[128]{0:T(128)S(1)}, s32[128]{0:T(128)}, u32[]{:S(2)}) copy-start(s32[128]{0:T(128)} %lens_ref.3) | copy-start | bytes 1540

commit v5 on v4

--- a/solution.py
+++ b/solution.py
@@ -106,15 +106,16 @@
     k_in = [pltpu.make_async_copy(k_h.at[r], kbuf.at[r], kv_sem.at[0, r]) for r in range(sb)]
     v_in = [pltpu.make_async_copy(v_h.at[r], vbuf.at[r], kv_sem.at[1, r]) for r in range(sb)]
     wo_load = pltpu.make_async_copy(wo_h, wo_v, wo_sem)
-    for c in first_loads:
+    def start_block(s, mine):
+        for c in block_loads(2 * s + int(mine), block_of(s, mine)):
+            c.start()
+
+    for c in first_loads + q_loads:
         c.start()
     for c in first_loads:
         c.wait()
-    for c in q_loads:
-        c.start()
-    for n in range(ntx):
-        for c in block_loads(n, block_of(n // 2, n % 2 == 1)):
-            c.start()
+    start_block(0, False)
+    start_block(0, True)
 
     xp = jnp.dot(perm_v[...], x_v[...], preferred_element_type=F32)
     own_mean = jnp.sum(xp, axis=1, keepdims=True) / dl
@@ -133,6 +134,7 @@
         return jnp.concatenate(parts + [jnp.zeros((16 - tiles, hd), F32)], axis=0).astype(BF16)
 
     pltpu.make_async_copy(wq_v, wq_v, wq_sem).wait()
+    start_block(1, False)
     part = jnp.dot(h_v[...], wq_v[...], preferred_element_type=F32)
     qp[...] = part[:rows].reshape(ntx, rb, qw)
     gq_s[...] = gamma_row(part[rows:], qw // hd)
@@ -219,6 +221,11 @@
 
     def product(s, carry):
         pltpu.make_async_copy(wb_v.at[2 * s], wb_v.at[2 * s], wb_sem.at[2 * s]).wait()
+
+        @pl.when(s < nx - 1)
+        def _():
+            start_block(s + 1, True)
+
         part = jnp.dot(h_v[...], wb_v[2 * s], preferred_element_type=F32)
         d_s[s] = part[:rows].astype(BF16)
         d_copy(s).start()
@@ -229,6 +236,11 @@
             q_pair()
 
         pltpu.make_async_copy(wb_v.at[2 * s + 1], wb_v.at[2 * s + 1], wb_sem.at[2 * s + 1]).wait()
+
+        @pl.when(s < nx - 2)
+        def _():
+            start_block(s + 2, False)
+
         part = jnp.dot(h_v[...], wb_v[2 * s + 1], preferred_element_type=F32)
         own[s] = part[:rows]
         gb_s[block_of(s, True)] = gamma_row(part[rows:], 2 * fb // hd)
@@ -371,9 +383,8 @@
             b = held(s, False)
             remote(b_v.at[b], b_v.at[b], bp_ss, bp_rs.at[s], tx=partner).wait_recv()
 
-    ring(1, 0)
     q_rows()
-    for t in range(1, SUBS):
+    for t in range(SUBS):
         ring(1, t)
     for n in range(ntx):
         wd_load(n, held(n // 2, n % 2 == 0)).start()

time: 61.7 us -> 56.6 us (0.917)
  Pallas kernels: 61 us -> 55.8 us
    pallas_call x1, Pallas kernels: 57 us -> 51.8 us  [layer_shard(): pl.pallas_call(functools.partial(step_kernel, ny, nx, dl * ntx), out_shap...]
where the time goes in v5:
time: 56.6 us; the launch traced here: 56.4 us
  Pallas kernels  55.8 us (99%)
  between operations  0.66 us (1%)
    pallas_call x1, Pallas kernels, layer_shard(): pl.pallas_call(functools.partial(step_kernel, ny, nx, dl * ntx), out_shap...  51.8 us
    pallas_call x1, Pallas kernels, layer_shard(): pl.pallas_call(functools.partial(store_kernel, ny, ntx), out_shape=(jax.S...  3.98 us

profile of v5, /device:TPU:97, one launch (start us, length us, event | category | flops | bytes accessed | tf_op | source)
XLA Modules:
  0.0 56.4 jit_solution(2586118015658130089)
XLA Ops:
  0.6 0.0 copy-start
  0.6 51.8 %step.1 = (bf16[128,768]{1,0:T(8,128)(2,1)S(1)}, f32[8,128]{1,0:T(8,128)S(1)}, bf16[4,4096,128]{2,1,0:T(8,128)(2,1)S(1)}, bf16[4,4096,128]{2,1,0:T(8,128)(2,1)S(1)}) custom-call(s32[128]{0:T(128)} %lens_ref.3, bf16[128,768]{1,0:T(8,128)(2,1)} %x_h.1, f32[768]{0:T(1024)} %gamma_h.1, bf16[128,128]{1,0:T(8,128)(2,1)} %constant.4.clone.perm_h, ...), custom_call_target="tpu_custom_call" | custom-call | tf_op jit(solution)/shard_map/step/pallas_call | solution.py:536
  52.4 0.0 copy-done
  52.4 4.0 %store.1 = (bf16[128,768]{1,0:T(8,128)(2,1)}, bf16[4,4096,128]{2,1,0:T(8,128)(2,1)}, bf16[4,4096,128]{2,1,0:T(8,128)(2,1)}) custom-call(s32[128]{0:T(128)S(1)} %copy-done, bf16[128,768]{1,0:T(8,128)(2,1)S(1)} %get-tuple-element.7.y_v, f32[8,128]{1,0:T(8,128)S(1)} %get-tuple-element.8.new_v, bf16[4,4096,128]{2,1,0:T(8,128)(2,1)S(1)} %get-tuple-element.9.k_v, ...), custom_call_target="tpu_custom_call" | custom-call | tf_op jit(solution)/shard_map/store/pallas_call | solution.py:570
Async XLA Ops:
  0.6 51.8 %copy-start = (s32[128]{0:T(128)S(1)}, s32[128]{0:T(128)}, u32[]{:S(2)}) copy-start(s32[128]{0:T(128)} %lens_ref.3) | copy-start | bytes 1540

commit v6 on v5

--- a/solution.py
+++ b/solution.py
@@ -58,6 +58,7 @@
     yb = rows // ny
     partner = lax.rem(col + 1, 2) + 2 * chip
     after = 2 * lax.rem(chip + step + nx, nx) + core
+    before = 2 * lax.rem(chip - step + nx, nx) + core
     tx_peers = [lax.rem(col + k, ntx) for k in range(1, ntx)]
     x_peers = [2 * lax.rem(chip + k, nx) + core for k in range(1, nx)]
     y_peers = [lax.rem(row + k, ny) for k in range(1, ny)]
@@ -77,9 +78,9 @@
         at = lax.rem(chip - (s + 1) * sign + 2 * nx, nx)
         return 2 * at + (core if mine else 1 - core)
 
-    def held(s, mine):
-        sign = step if mine else -step
-        return 2 * lax.rem(chip - s * sign + 2 * nx, nx) + (core if mine else 1 - core)
+    def held(kind, mine):
+        away = (0, -1, 1, -2)[kind] * (step if mine else -step)
+        return 2 * lax.rem(chip + away + 2 * nx, nx) + (core if mine else 1 - core)
 
     def block_loads(n, b):
         at = pl.ds(pl.multiple_of(b * fb, fb), fb)
@@ -283,6 +284,7 @@
             gate = part[:, :fb].astype(BF16).astype(F32)
             up = part[:, fb:].astype(BF16).astype(F32)
             b_v[col, at] = (gate * (1.0 / (1.0 + jnp.exp(-gate))) * up).astype(BF16)
+            act_out(t)
 
     def turn(vals, r):
         return vals * turns[0, r:r + 1, :] + pltpu.roll(vals, hd // 2, 1) * turns[1, r:r + 1, :]
@@ -321,31 +323,48 @@
         for a in range(ny):
             o32[a, pl.ds(r, lh, stride=sb), :] = out[a * lh:(a + 1) * lh]
 
-    def b_copy(s, t):
-        b = held(s, True)
-        return remote(b_v.at[b, piece(t)], b_v.at[b, piece(t)], b_ss, b_rs.at[s, t], tx=after)
-
-    def b_in(s, t):
-        b = held(s + 1, True)
-        return remote(b_v.at[b, piece(t)], b_v.at[b, piece(t)], b_ss, b_rs.at[s, t], tx=after)
-
-    def bp_copy(s, t):
-        b = held(s, True)
-        return remote(b_v.at[b, piece(t)], b_v.at[b, piece(t)], bp_ss, bp_rs.at[s], tx=partner)
+    def b_send(kind, t, slot, to):
+        b = held(kind, True)
+        return remote(b_v.at[b, piece(t)], b_v.at[b, piece(t)], b_ss, b_rs.at[slot - 1, t], tx=to)
+
+    def b_in(kind, t):
+        b = held(kind, True)
+        return remote(b_v.at[b, piece(t)], b_v.at[b, piece(t)], b_ss, b_rs.at[kind - 1, t], tx=after)
+
+    def b_pair(kind, t):
+        b = held(kind, True)
+        return remote(b_v.at[b, piece(t)], b_v.at[b, piece(t)], bp_ss, bp_rs.at[kind], tx=partner)
+
+    def act_out(t):
+        b_send(0, t, 1, after).start()
+        b_send(0, t, 2, before).start()
+        b_pair(0, t).start()
+
+    def act_in(kind):
+        for t in range(SUBS):
+            with scope("b%d%d" % (kind, t)):
+                b_in(kind, t).wait_recv()
+            if kind == 1:
+                b_send(1, t, 3, after).start()
+            b_pair(kind, t).start()
 
     ay_cp = [remote(ay_s.at[y_peers[k - 1]], ay_r.at[row], ay_ss, ay_rs, ty=y_peers[k - 1]) for k in range(1, ny)]
-    g_cp = [remote(g_v.at[col], g_v.at[col], g_ss, g_rs.at[k], tx=x_peers[k - 1]) for k in range(1, nx)]
-
-    def g_from(k, mine):
-        return 2 * lax.rem(chip - k + nx, nx) + (core if mine else 1 - core)
-
-    def g_in(k):
-        at = g_from(k, True)
-        return remote(g_v.at[at], g_v.at[at], g_ss, g_rs.at[k], tx=x_peers[k - 1])
-
-    def gp_copy(k):
-        at = g_from(k, True)
+
+    def g_send(kind, slot, to):
+        at = held(kind, True)
+        return remote(g_v.at[at], g_v.at[at], g_ss, g_rs.at[slot - 1], tx=to)
+
+    def g_pair(kind):
+        at = held(kind, True)
         return remote(g_v.at[at], g_v.at[at], gp_ss, gp_rs, tx=partner)
+
+    def g_in(kind):
+        at = held(kind, True)
+        with scope("g%d" % kind):
+            remote(g_v.at[at], g_v.at[at], g_ss, g_rs.at[kind - 1], tx=after).wait_recv()
+        if kind == 1:
+            g_send(1, 3, after).start()
+        g_pair(kind).start()
 
     def att_out():
         ay_s[...] = o32[...].astype(BF16)
@@ -361,17 +380,9 @@
             for n in range(lh):
                 g32[n, a * sb:(a + 1) * sb, :] = part[n * sb:(n + 1) * sb, :]
         g_v[col] = g32[...].astype(BF16)
-        for c in g_cp:
-            c.start()
-        gp_copy(0).start()
-
-    def forward(s):
-        for t in range(SUBS):
-            with scope("b%d%d" % (s, t)):
-                b_in(s, t).wait_recv()
-            if s < nx - 2:
-                b_copy(s + 1, t).start()
-            bp_copy(s + 1, t).start()
+        g_send(0, 1, after).start()
+        g_send(0, 2, before).start()
+        g_pair(0).start()
 
     def down(n, first=False):
         wd_load(n, 0).wait()
@@ -389,54 +400,41 @@
     for n in range(ntx):
         wd_load(n, held(n // 2, n % 2 == 0)).start()
     wo_load.start()
-    ring(2, 0)
-    ring(2, 1)
     with scope("qy"):
         remote(qy_r.at[pl.ds(0, ny - 1)], qy_r.at[pl.ds(0, ny - 1)], qy_ss, qy_rs, ty=y_peers[0]).wait_recv()
-    with scope("a0"):
-        attend(0)
-    ring(2, 2)
-    ring(2, 3)
-    with scope("a1"):
-        attend(1)
-    ring(3, 0)
-    with scope("a2"):
-        attend(2)
-    ring(3, 1)
-    with scope("a3"):
-        attend(3)
-    att_out()
-    for t in range(2, SUBS):
+    for t in range(SUBS):
+        with scope("a%d" % t):
+            attend(t)
+        if t == SUBS - 1:
+            att_out()
+        ring(2, t)
+    for t in range(SUBS):
         ring(3, t)
-    for t in range(SUBS):
-        b_copy(0, t).start()
-        bp_copy(0, t).start()
     down(0, True)
-    forward(0)
     att_rows()
+    act_in(1)
+    act_in(2)
     from_pair(0)
     down(1)
     down(2)
-    forward(1)
-    with scope("g"):
-        for k in range(1, nx):
-            g_in(k).wait_recv()
-            gp_copy(k).start()
+    g_in(1)
+    g_in(2)
+    down(4)
     from_pair(1)
     down(3)
-    down(4)
+    act_in(3)
+    from_pair(2)
+    down(5)
+    down(6)
+    g_in(3)
+    from_pair(3)
+    down(7)
     with scope("gp"):
         remote(g_v.at[pl.ds(0, nx)], g_v.at[pl.ds(0, nx)], gp_ss, gp_rs, tx=partner).wait_recv()
     wo_load.wait()
     for n in range(0, lh, 2):
         pair = jnp.concatenate([g_v[:, n].reshape(rows, hd), g_v[:, n + 1].reshape(rows, hd)], axis=1)
         acc[...] += jnp.dot(pair, wo_v[n * hd:(n + 2) * hd, :], preferred_element_type=F32)
-    forward(2)
-    from_pair(2)
-    down(5)
-    down(6)
-    from_pair(3)
-    down(7)
 
     part = lax.dot_general(perm_v[...], acc[...].astype(BF16), (((0,), (0,)), ((), ())), preferred_element_type=F32)
     y_s[...] = part.astype(BF16).reshape(ny, yb, dl)
@@ -560,7 +558,7 @@
                 DMA((4,)), DMA, DMA((ntx,)), DMA((2, sb)), DMA, DMA((ntx,)),
                 DMA, DMA, DMA, DMA, DMA, DMA, DMA, DMA, DMA, DMA, DMA, DMA,
                 DMA, DMA((nx,)), DMA, DMA((nx - 1, SUBS)),
-                DMA, DMA, DMA, DMA((nx,)), DMA, DMA,
+                DMA, DMA, DMA, DMA((nx - 1,)), DMA, DMA,
                 DMA, DMA((nx - 1, SUBS)), DMA, DMA((nx,)), DMA, DMA, DMA, DMA,
             ],
             compiler_params=pltpu.CompilerParams(collective_id=0, has_side_effects=True, vmem_limit_bytes=52 * 1024 * 1024),

time: 56.6 us -> 55 us (0.972)
  Pallas kernels: 55.8 us -> 54.2 us
    pallas_call x1, Pallas kernels: 51.8 us -> 50.2 us  [layer_shard(): pl.pallas_call(functools.partial(step_kernel, ny, nx, dl * ntx), out_shap...]
where the time goes in v6:
time: 55 us; the launch traced here: 54.8 us
  Pallas kernels  54.2 us (99%)
  between operations  0.66 us (1%)
    pallas_call x1, Pallas kernels, layer_shard(): pl.pallas_call(functools.partial(step_kernel, ny, nx, dl * ntx), out_shap...  50.2 us
    pallas_call x1, Pallas kernels, layer_shard(): pl.pallas_call(functools.partial(store_kernel, ny, ntx), out_shape=(jax.S...  3.98 us

profile of v6, /device:TPU:97, one launch (start us, length us, event | category | flops | bytes accessed | tf_op | source)
XLA Modules:
  0.0 54.8 jit_solution(10017318413796404573)
XLA Ops:
  0.6 0.0 copy-start
  0.6 50.2 %step.1 = (bf16[128,768]{1,0:T(8,128)(2,1)S(1)}, f32[8,128]{1,0:T(8,128)S(1)}, bf16[4,4096,128]{2,1,0:T(8,128)(2,1)S(1)}, bf16[4,4096,128]{2,1,0:T(8,128)(2,1)S(1)}) custom-call(s32[128]{0:T(128)} %lens_ref.3, bf16[128,768]{1,0:T(8,128)(2,1)} %x_h.1, f32[768]{0:T(1024)} %gamma_h.1, bf16[128,128]{1,0:T(8,128)(2,1)} %constant.4.clone.perm_h, ...), custom_call_target="tpu_custom_call" | custom-call | tf_op jit(solution)/shard_map/step/pallas_call | solution.py:534
  50.8 0.0 copy-done
  50.8 4.0 %store.1 = (bf16[128,768]{1,0:T(8,128)(2,1)}, bf16[4,4096,128]{2,1,0:T(8,128)(2,1)}, bf16[4,4096,128]{2,1,0:T(8,128)(2,1)}) custom-call(s32[128]{0:T(128)S(1)} %copy-done, bf16[128,768]{1,0:T(8,128)(2,1)S(1)} %get-tuple-element.7.y_v, f32[8,128]{1,0:T(8,128)S(1)} %get-tuple-element.8.new_v, bf16[4,4096,128]{2,1,0:T(8,128)(2,1)S(1)} %get-tuple-element.9.k_v, ...), custom_call_target="tpu_custom_call" | custom-call | tf_op jit(solution)/shard_map/store/pallas_call | solution.py:568
Async XLA Ops:
  0.6 50.2 %copy-start = (s32[128]{0:T(128)S(1)}, s32[128]{0:T(128)}, u32[]{:S(2)}) copy-start(s32[128]{0:T(128)} %lens_ref.3) | copy-start | bytes 1540

commit v7 on v6

--- a/solution.py
+++ b/solution.py
@@ -18,7 +18,7 @@
 DMA = pltpu.SemaphoreType.DMA
 SUBS = 4
 CHUNK = 1024
-PIECE = 512
+PIECE = 1024
 scope = jax.named_scope
 
 
@@ -31,9 +31,9 @@
     return pltpu.make_async_remote_copy(src_ref=src, dst_ref=dst, send_sem=send_sem, recv_sem=recv_sem, device_id=device, device_id_type=MESH)
 
 
-def step_kernel(ny, nx, d_model, lens_ref, x_h, gamma_h, perm_h, freq_h, wq_h, wk_h, wv_h, wg_h, wu_h, k_h, v_h, wo_h, wd_h,
+def step_kernel(ny, nx, d_model, lens_ref, x_h, gamma_h, perm_h, back_h, freq_h, wq_h, wk_h, wv_h, wg_h, wu_h, k_h, v_h, wo_h, wd_h,
                 y_out, new_out, kbuf, vbuf,
-                x_v, gamma_v, perm_v, freq_v, wq_v, wb_v, wo_v, wd_v, h_v, stat_s, stat_r, gq_s, gq_r, gb_s, gb_r, norm,
+                x_v, gamma_v, perm_v, back_v, freq_v, wq_v, wb_v, wo_v, wd_v, h_v, stat_s, stat_r, gq_s, gq_r, gb_s, gb_r, norm,
                 qp, qd_s, qd_r, qx_s, qx_r, qsum, kvs, qy_s, qy_r, own, d_s, d_r, r_s, r_r,
                 turns, qs, sbuf, o32, ay_s, ay_r, g32, g_v, b_v, acc, y_s, y_r, yf,
                 in_sem, wq_sem, wb_sem, kv_sem, wo_sem, wd_sem, stat_ss, stat_rs, gq_ss, gq_rs, gb_ss, gb_rs, qd_ss, qd_rs, qx_ss, qx_rs, qy_ss, qy_rs,
@@ -98,6 +98,7 @@
         pltpu.make_async_copy(perm_h, perm_v, in_sem.at[1]),
         pltpu.make_async_copy(gamma_h, gamma_v, in_sem.at[2]),
         pltpu.make_async_copy(freq_h, freq_v, in_sem.at[3]),
+        pltpu.make_async_copy(back_h, back_v, in_sem.at[4]),
     ]
     q_loads = [
         pltpu.make_async_copy(wq_h, wq_v.at[:, pl.ds(0, qn)], wq_sem),
@@ -174,24 +175,37 @@
             tiles.append(tile * cols[:, ntx:ntx + 1])
         return jnp.concatenate(tiles, axis=1)
 
-    qx_cp = [remote(qx_s.at[k], qx_r.at[k], qx_ss, qx_rs, tx=x_peers[k - 1]) for k in range(1, nx)]
+
+    def q_of(away):
+        at = lax.rem(chip + away * step + 2 * nx, nx)
+        return qp[2 * at + core] + qd_r[at].astype(F32)
+
+    def qx_copy(slot, to):
+        return remote(qx_s.at[slot], qx_r.at[slot], qx_ss, qx_rs.at[slot], tx=to)
+
     qy_cp = [remote(qy_s.at[y_peers[k - 1]], qy_r.at[row], qy_ss, qy_rs, ty=y_peers[k - 1]) for k in range(1, ny)]
 
     def q_pair():
         with scope("qd"):
             qd_cp.wait_recv()
-        for k in range(1, nx):
-            at = lax.rem(chip + k, nx)
-            qx_s[k] = (qp[2 * at + core] + qd_r[at].astype(F32)).astype(BF16)
-            qx_cp[k - 1].start()
+        qx_s[0] = q_of(2).astype(BF16)
+        qx_copy(0, after).start()
+        qx_s[1] = q_of(-1).astype(BF16)
+        qx_copy(1, before).start()
+
+    def q_relay():
+        with scope("qa"):
+            qx_copy(0, after).wait_recv()
+        qx_s[2] = (q_of(1) + qx_r[0].astype(F32)).astype(BF16)
+        qx_copy(2, after).start()
 
     def q_rows():
-        mine = qp[2 * chip + core] + qd_r[chip].astype(F32)
+        mine = q_of(0)
         rest_of_norm()
         with scope("qx"):
-            remote(qx_r.at[pl.ds(1, nx - 1)], qx_r.at[pl.ds(1, nx - 1)], qx_ss, qx_rs, tx=partner).wait_recv()
-        for k in range(1, nx):
-            mine = mine + qx_r[k].astype(F32)
+            qx_copy(1, before).wait_recv()
+            qx_copy(2, after).wait_recv()
+        mine = mine + qx_r[1].astype(F32) + qx_r[2].astype(F32)
         mine = normed(mine, pl.ds(pl.multiple_of(col * rb, rb), rb), gq_r)
         qsum[...] = mine
         kvs[0] = mine[:, qn:qn + hd]
@@ -221,6 +235,10 @@
         return remote(r_s.at[s, piece(t)], r_r.at[s, piece(t)], r_ss, r_rs.at[s, t], tx=after)
 
     def product(s, carry):
+        @pl.when(s == 2)
+        def _():
+            q_relay()
+
         pltpu.make_async_copy(wb_v.at[2 * s], wb_v.at[2 * s], wb_sem.at[2 * s]).wait()
 
         @pl.when(s < nx - 1)
@@ -333,15 +351,15 @@
 
     def b_pair(kind, t):
         b = held(kind, True)
-        return remote(b_v.at[b, piece(t)], b_v.at[b, piece(t)], bp_ss, bp_rs.at[kind], tx=partner)
+        return remote(b_v.at[b, piece(t)], b_v.at[b, piece(t)], bp_ss, bp_rs.at[kind, t * 2 // SUBS], tx=partner)
 
     def act_out(t):
         b_send(0, t, 1, after).start()
         b_send(0, t, 2, before).start()
         b_pair(0, t).start()
 
-    def act_in(kind):
-        for t in range(SUBS):
+    def act_in(kind, half):
+        for t in range(half * SUBS // 2, (half + 1) * SUBS // 2):
             with scope("b%d%d" % (kind, t)):
                 b_in(kind, t).wait_recv()
             if kind == 1:
@@ -384,15 +402,52 @@
         g_send(0, 2, before).start()
         g_pair(0).start()
 
-    def down(n, first=False):
-        wd_load(n, 0).wait()
-        part = jnp.dot(b_v[held(n // 2, n % 2 == 0)], wd_v[n], preferred_element_type=F32)
-        acc[...] = part if first else acc[...] + part
-
-    def from_pair(s):
-        with scope("bp%d" % s):
-            b = held(s, False)
-            remote(b_v.at[b], b_v.at[b], bp_ss, bp_rs.at[s], tx=partner).wait_recv()
+    mid = rows // 2
+
+    def half_rows(half):
+        return pl.ds(half * mid, mid)
+
+    def down(n, half):
+        if half == 0:
+            wd_load(n, 0).wait()
+        part = jnp.dot(b_v[held(n // 2, n % 2 == 0), half_rows(half)], wd_v[n], preferred_element_type=F32)
+        acc[half_rows(half)] = part if n == 0 else acc[half_rows(half)] + part
+
+    def from_pair(kind, half):
+        b = held(kind, False)
+        with scope("bp%d%d" % (kind, half)):
+            remote(b_v.at[b, half_rows(half)], b_v.at[b, half_rows(half)], bp_ss, bp_rs.at[kind, half], tx=partner).wait_recv()
+
+    def att_down(half):
+        at = pl.ds(half * nx, nx)
+        for n in range(0, lh, 2):
+            pair = jnp.concatenate([g_v[at, n].reshape(mid, hd), g_v[at, n + 1].reshape(mid, hd)], axis=1)
+            acc[half_rows(half)] += jnp.dot(pair, wo_v[n * hd:(n + 2) * hd, :], preferred_element_type=F32)
+
+    def y_out_half(half):
+        part = jnp.dot(back_v[...], acc[half_rows(half)].astype(BF16), preferred_element_type=F32)
+        y_s[half] = part.astype(BF16).reshape(ny, yb // 2, dl)
+        for k in range(1, ny):
+            remote(y_s.at[half, y_peers[k - 1]], y_r.at[half, k], y_ss.at[half], y_rs.at[half], ty=y_peers[k - 1]).start()
+
+    def y_sum_half(half):
+        at = pl.ds(pl.multiple_of(row * yb + half * (yb // 2), yb // 2), yb // 2)
+        total = x_v[at, :].astype(F32) + y_s[half, row].astype(F32)
+        rest = y_r.at[half, pl.ds(1, ny - 1)]
+        with scope("y%d" % half):
+            remote(rest, rest, y_ss.at[half], y_rs.at[half], ty=y_peers[0]).wait_recv()
+        for k in range(1, ny):
+            total = total + y_r[half, k].astype(F32)
+        yf[half, row] = total.astype(BF16)
+        for k in range(1, ny):
+            remote(yf.at[half, row], yf.at[half, row], f_ss.at[half], f_rs.at[half], ty=y_peers[k - 1]).start()
+
+    def y_all_half(half):
+        rest = yf.at[half, pl.ds(0, ny - 1)]
+        with scope("f%d" % half):
+            remote(rest, rest, f_ss.at[half], f_rs.at[half], ty=y_peers[0]).wait_recv()
+        for a in range(ny):
+            y_out[a * yb + half * (yb // 2):a * yb + (half + 1) * (yb // 2), :] = yf[half, a]
 
     q_rows()
     for t in range(SUBS):
@@ -408,60 +463,58 @@
         if t == SUBS - 1:
             att_out()
         ring(2, t)
-    for t in range(SUBS):
+    for t in range(SUBS - 1):
         ring(3, t)
-    down(0, True)
     att_rows()
-    act_in(1)
-    act_in(2)
-    from_pair(0)
-    down(1)
-    down(2)
+    ring(3, SUBS - 1)
+    down(0, 0)
+    act_in(1, 0)
     g_in(1)
+    act_in(2, 0)
+    down(0, 1)
+    act_in(1, 1)
     g_in(2)
-    down(4)
-    from_pair(1)
-    down(3)
-    act_in(3)
-    from_pair(2)
-    down(5)
-    down(6)
+    act_in(2, 1)
+    from_pair(0, 0)
+    down(1, 0)
+    down(2, 0)
+    down(4, 0)
+    act_in(3, 0)
     g_in(3)
-    from_pair(3)
-    down(7)
+    from_pair(1, 0)
+    down(3, 0)
+    from_pair(2, 0)
+    down(5, 0)
+    down(6, 0)
+    act_in(3, 1)
+    from_pair(3, 0)
+    down(7, 0)
     with scope("gp"):
         remote(g_v.at[pl.ds(0, nx)], g_v.at[pl.ds(0, nx)], gp_ss, gp_rs, tx=partner).wait_recv()
     wo_load.wait()
-    for n in range(0, lh, 2):
-        pair = jnp.concatenate([g_v[:, n].reshape(rows, hd), g_v[:, n + 1].reshape(rows, hd)], axis=1)
-        acc[...] += jnp.dot(pair, wo_v[n * hd:(n + 2) * hd, :], preferred_element_type=F32)
-
-    part = lax.dot_general(perm_v[...], acc[...].astype(BF16), (((0,), (0,)), ((), ())), preferred_element_type=F32)
-    y_s[...] = part.astype(BF16).reshape(ny, yb, dl)
-    y_cp = [remote(y_s.at[y_peers[k - 1]], y_r.at[k], y_ss, y_rs, ty=y_peers[k - 1]) for k in range(1, ny)]
-    for c in y_cp:
-        c.start()
-    total = x_v[pl.ds(pl.multiple_of(row * yb, yb), yb), :].astype(F32) + y_s[row].astype(F32)
-    with scope("y"):
-        remote(y_r.at[pl.ds(1, ny - 1)], y_r.at[pl.ds(1, ny - 1)], y_ss, y_rs, ty=y_peers[0]).wait_recv()
-    for k in range(1, ny):
-        total = total + y_r[k].astype(F32)
-    yf[row] = total.astype(BF16)
-    f_cp = [remote(yf.at[row], yf.at[row], f_ss, f_rs, ty=y_peers[k - 1]) for k in range(1, ny)]
-    for c in f_cp:
-        c.start()
-    with scope("f"):
-        remote(yf.at[pl.ds(0, ny - 1)], yf.at[pl.ds(0, ny - 1)], f_ss, f_rs, ty=y_peers[0]).wait_recv()
-    y_out[...] = yf[...].reshape(rows, dl)
+    att_down(0)
+    y_out_half(0)
+    for kind in range(nx):
+        from_pair(kind, 1)
+        if kind > 0:
+            down(2 * kind, 1)
+        down(2 * kind + 1, 1)
+    att_down(1)
+    y_out_half(1)
+    y_sum_half(0)
+    y_sum_half(1)
+    y_all_half(0)
+    y_all_half(1)
 
     with scope("sends"):
         qd_cp.wait_send()
         for ref, send, recv in (
             (stat_r.at[pl.ds(1, ntx - 1)], stat_ss, stat_rs), (gq_r.at[pl.ds(1, ntx - 1)], gq_ss, gq_rs), (gb_r.at[pl.ds(1, ntx - 1)], gb_ss, gb_rs),
-            (qx_s.at[pl.ds(1, nx - 1)], qx_ss, qx_rs), (qy_s.at[pl.ds(1, ny - 1)], qy_ss, qy_rs), (ay_s.at[pl.ds(1, ny - 1)], ay_ss, ay_rs),
-            (y_s.at[pl.ds(1, ny - 1)], y_ss, y_rs), (yf.at[pl.ds(1, ny - 1)], f_ss, f_rs),
+            (qx_s, qx_ss, qx_rs.at[0]), (qy_s.at[pl.ds(1, ny - 1)], qy_ss, qy_rs), (ay_s.at[pl.ds(1, ny - 1)], ay_ss, ay_rs),
+            *((y_s.at[half, pl.ds(1, ny - 1)], y_ss.at[half], y_rs.at[half]) for half in range(2)),
+            *((yf.at[half, pl.ds(1, ny - 1)], f_ss.at[half], f_rs.at[half]) for half in range(2)),
             (d_s, d_ss, d_rs.at[0]), (r_s, r_ss, r_rs.at[0, 0]), (g_v.at[pl.ds(1, nx - 1)], g_ss, g_rs.at[0]), (g_v.at[pl.ds(0, nx)], gp_ss, gp_rs),
-            (b_v.at[pl.ds(1, nx - 1)], b_ss, b_rs.at[0, 0]), (b_v.at[pl.ds(0, nx)], bp_ss, bp_rs.at[0]),
+            (b_v.at[pl.ds(1, nx - 1)], b_ss, b_rs.at[0, 0]), (b_v.at[pl.ds(0, nx)], bp_ss, bp_rs.at[0, 0]),
         ):
             remote(ref, ref, send, recv, tx=partner).wait_send()
 
@@ -528,6 +581,9 @@
         natural = np.arange(rows)
         order = np.reshape(np.transpose(np.reshape(natural, (ny, ntx, sb)), (1, 0, 2)), (rows,))
         perm = jnp.asarray(order[:, None] == natural[None, :], dtype=BF16)
+        part = np.arange(rows // 2)
+        order = np.reshape(np.transpose(np.reshape(part, (nx, ny, sb)), (1, 0, 2)), (rows // 2,))
+        back = jnp.asarray(order[:, None] == part[None, :], dtype=BF16)
         freqs = np.power(ROPE_BASE, -(np.arange(hd // 2, dtype=np.float32) * 2.0) / hd).astype(np.float32)
         freqs = jnp.asarray(np.tile(np.concatenate([freqs, freqs])[None, :], (8, 1)))
 
@@ -539,31 +595,31 @@
                 pltpu.VMEM(k_blk.shape, BF16),
                 pltpu.VMEM(v_blk.shape, BF16),
             ),
-            in_specs=[sspec] + [hspec] * 13,
+            in_specs=[sspec] + [hspec] * 14,
             out_specs=(vspec,) * 4,
             scratch_shapes=[
-                VMEM((rows, dl), BF16), VMEM((dl,), F32), VMEM((rows, rows), BF16), VMEM((8, hd), F32),
+                VMEM((rows, dl), BF16), VMEM((dl,), F32), VMEM((rows, rows), BF16), VMEM((rows // 2, rows // 2), BF16), VMEM((8, hd), F32),
                 VMEM((dl, qw), BF16), VMEM((ntx, dl, 2 * fb), BF16), VMEM((qn, dl), BF16), VMEM((ntx, fb, dl), BF16),
                 VMEM((rows + 16, dl), BF16), VMEM((8, rows), F32), VMEM((ntx, 8, rows), F32),
                 VMEM((16, hd), BF16), VMEM((ntx, 16, hd), BF16), VMEM((ntx, 16, hd), BF16), VMEM((ntx, 16, hd), BF16), VMEM((rows, rows), F32),
                 VMEM((ntx, rb, qw), F32), VMEM((nx, rb, qw), BF16), VMEM((nx, rb, qw), BF16),
-                VMEM((nx, rb, qw), BF16), VMEM((nx, rb, qw), BF16), VMEM((rb, qw), F32), VMEM((2, rb, hd), F32),
+                VMEM((3, rb, qw), BF16), VMEM((3, rb, qw), BF16), VMEM((rb, qw), F32), VMEM((2, rb, hd), F32),
                 VMEM((ny, sb * lh, hd), F32), VMEM((ny, sb * lh, hd), F32),
                 VMEM((nx, rows, 2 * fb), F32), VMEM((nx, rows, 2 * fb), BF16), VMEM((nx, rows, 2 * fb), BF16),
                 VMEM((nx - 1, rows, 2 * fb), BF16), VMEM((nx - 1, rows, 2 * fb), BF16),
                 VMEM((2, 8, hd), F32), VMEM((ny * lh, hd), F32), VMEM((ny * lh, ctx), F32), VMEM((ny, sb * lh, hd), F32),
                 VMEM((ny, sb * lh, hd), BF16), VMEM((ny, sb * lh, hd), BF16), VMEM((lh, rb, hd), F32),
                 VMEM((ntx, lh, rb, hd), BF16), VMEM((ntx, rows, fb), BF16), VMEM((rows, dl), F32),
-                VMEM((ny, yb, dl), BF16), VMEM((ny, yb, dl), BF16), VMEM((ny, yb, dl), BF16),
-                DMA((4,)), DMA, DMA((ntx,)), DMA((2, sb)), DMA, DMA((ntx,)),
-                DMA, DMA, DMA, DMA, DMA, DMA, DMA, DMA, DMA, DMA, DMA, DMA,
+                VMEM((2, ny, yb // 2, dl), BF16), VMEM((2, ny, yb // 2, dl), BF16), VMEM((2, ny, yb // 2, dl), BF16),
+                DMA((5,)), DMA, DMA((ntx,)), DMA((2, sb)), DMA, DMA((ntx,)),
+                DMA, DMA, DMA, DMA, DMA, DMA, DMA, DMA, DMA, DMA((3,)), DMA, DMA,
                 DMA, DMA((nx,)), DMA, DMA((nx - 1, SUBS)),
                 DMA, DMA, DMA, DMA((nx - 1,)), DMA, DMA,
-                DMA, DMA((nx - 1, SUBS)), DMA, DMA((nx,)), DMA, DMA, DMA, DMA,
+                DMA, DMA((nx - 1, SUBS)), DMA, DMA((nx, 2)), DMA((2,)), DMA((2,)), DMA((2,)), DMA((2,)),
             ],
             compiler_params=pltpu.CompilerParams(collective_id=0, has_side_effects=True, vmem_limit_bytes=52 * 1024 * 1024),
             name="step",
-        )(lens_part, x_blk, gamma_blk, perm, freqs, w_query, w_key, w_value, w_gate, w_up, k_blk, v_blk, w_out, w_down)
+        )(lens_part, x_blk, gamma_blk, perm, back, freqs, w_query, w_key, w_value, w_gate, w_up, k_blk, v_blk, w_out, w_down)
 
         return pl.pallas_call(
             functools.partial(store_kernel, ny, ntx),
@@ -575,7 +631,7 @@
             in_specs=[sspec] + [vspec] * 4,
             out_specs=(hspec,) * 3,
             scratch_shapes=[VMEM((2, sb, PIECE, hd), BF16), DMA, DMA((2, sb, 2))],
-            compiler_params=pltpu.CompilerParams(vmem_limit_bytes=4 * 1024 * 1024),
+            compiler_params=pltpu.CompilerParams(vmem_limit_bytes=6 * 1024 * 1024),
             name="store",
         )(lens_part, y_vm, new_rows, k_vm, v_vm)
 

time: 55 us -> 55.5 us (level)
  no operation moved by 1% of the time
where the time goes in v7:
time: 55.5 us; the launch traced here: 55 us
  Pallas kernels  54.3 us (98%)
  between operations  0.66 us (1%)
    pallas_call x1, Pallas kernels, layer_shard(): pl.pallas_call(functools.partial(step_kernel, ny, nx, dl * ntx), out_shap...  50.3 us
    pallas_call x1, Pallas kernels, layer_shard(): pl.pallas_call(functools.partial(store_kernel, ny, ntx), out_shape=(jax.S...  4.01 us

profile of v7, /device:TPU:97, one launch (start us, length us, event | category | flops | bytes accessed | tf_op | source)
XLA Modules:
  0.0 55.0 jit_solution(11506883073066815267)
XLA Ops:
  0.6 0.0 copy-start
  0.6 50.3 %step.1 = (bf16[128,768]{1,0:T(8,128)(2,1)S(1)}, f32[8,128]{1,0:T(8,128)S(1)}, bf16[4,4096,128]{2,1,0:T(8,128)(2,1)S(1)}, bf16[4,4096,128]{2,1,0:T(8,128)(2,1)S(1)}) custom-call(s32[128]{0:T(128)} %lens_ref.3, bf16[128,768]{1,0:T(8,128)(2,1)} %x_h.1, f32[768]{0:T(1024)} %gamma_h.1, bf16[128,128]{1,0:T(8,128)(2,1)} %constant.6.clone.perm_h, ...), custom_call_target="tpu_custom_call" | custom-call | tf_op jit(solution)/shard_map/step/pallas_call | solution.py:590
  51.0 0.0 copy-done
  51.0 4.0 %store.1 = (bf16[128,768]{1,0:T(8,128)(2,1)}, bf16[4,4096,128]{2,1,0:T(8,128)(2,1)}, bf16[4,4096,128]{2,1,0:T(8,128)(2,1)}) custom-call(s32[128]{0:T(128)S(1)} %copy-done, bf16[128,768]{1,0:T(8,128)(2,1)S(1)} %get-tuple-element.7.y_v, f32[8,128]{1,0:T(8,128)S(1)} %get-tuple-element.8.new_v, bf16[4,4096,128]{2,1,0:T(8,128)(2,1)S(1)} %get-tuple-element.9.k_v, ...), custom_call_target="tpu_custom_call" | custom-call | tf_op jit(solution)/shard_map/store/pallas_call | solution.py:624
Async XLA Ops:
  0.6 50.3 %copy-start = (s32[128]{0:T(128)S(1)}, s32[128]{0:T(128)}, u32[]{:S(2)}) copy-start(s32[128]{0:T(128)} %lens_ref.3) | copy-start | bytes 1540

commit v8 on v7

--- a/solution.py
+++ b/solution.py
@@ -18,7 +18,7 @@
 DMA = pltpu.SemaphoreType.DMA
 SUBS = 4
 CHUNK = 1024
-PIECE = 1024
+PIECE = 512
 scope = jax.named_scope
 
 
@@ -58,7 +58,8 @@
     yb = rows // ny
     partner = lax.rem(col + 1, 2) + 2 * chip
     after = 2 * lax.rem(chip + step + nx, nx) + core
-    before = 2 * lax.rem(chip - step + nx, nx) + core
+    left = 2 * lax.rem(chip + nx - 1, nx) + core
+    right = 2 * lax.rem(chip + 1, nx) + core
     tx_peers = [lax.rem(col + k, ntx) for k in range(1, ntx)]
     x_peers = [2 * lax.rem(chip + k, nx) + core for k in range(1, nx)]
     y_peers = [lax.rem(row + k, ny) for k in range(1, ny)]
@@ -79,8 +80,7 @@
         return 2 * at + (core if mine else 1 - core)
 
     def held(kind, mine):
-        away = (0, -1, 1, -2)[kind] * (step if mine else -step)
-        return 2 * lax.rem(chip + away + 2 * nx, nx) + (core if mine else 1 - core)
+        return 2 * lax.rem(chip + (0, 1, nx - 1, 2)[kind], nx) + (core if mine else 1 - core)
 
     def block_loads(n, b):
         at = pl.ds(pl.multiple_of(b * fb, fb), fb)
@@ -177,35 +177,27 @@
 
 
     def q_of(away):
-        at = lax.rem(chip + away * step + 2 * nx, nx)
+        at = lax.rem(chip + away + nx, nx)
         return qp[2 * at + core] + qd_r[at].astype(F32)
 
-    def qx_copy(slot, to):
-        return remote(qx_s.at[slot], qx_r.at[slot], qx_ss, qx_rs.at[slot], tx=to)
+    qx_in = qx_r.at[pl.ds(1, nx - 1)]
 
     qy_cp = [remote(qy_s.at[y_peers[k - 1]], qy_r.at[row], qy_ss, qy_rs, ty=y_peers[k - 1]) for k in range(1, ny)]
 
     def q_pair():
         with scope("qd"):
             qd_cp.wait_recv()
-        qx_s[0] = q_of(2).astype(BF16)
-        qx_copy(0, after).start()
-        qx_s[1] = q_of(-1).astype(BF16)
-        qx_copy(1, before).start()
-
-    def q_relay():
-        with scope("qa"):
-            qx_copy(0, after).wait_recv()
-        qx_s[2] = (q_of(1) + qx_r[0].astype(F32)).astype(BF16)
-        qx_copy(2, after).start()
+        for k in (2, 1, 3):
+            qx_s[k] = q_of(k).astype(BF16)
+            remote(qx_s.at[k], qx_r.at[k], qx_ss, qx_rs, tx=x_peers[k - 1]).start()
 
     def q_rows():
         mine = q_of(0)
         rest_of_norm()
         with scope("qx"):
-            qx_copy(1, before).wait_recv()
-            qx_copy(2, after).wait_recv()
-        mine = mine + qx_r[1].astype(F32) + qx_r[2].astype(F32)
+            remote(qx_in, qx_in, qx_ss, qx_rs, tx=partner).wait_recv()
+        for k in range(1, nx):
+            mine = mine + qx_r[k].astype(F32)
         mine = normed(mine, pl.ds(pl.multiple_of(col * rb, rb), rb), gq_r)
         qsum[...] = mine
         kvs[0] = mine[:, qn:qn + hd]
@@ -235,10 +227,6 @@
         return remote(r_s.at[s, piece(t)], r_r.at[s, piece(t)], r_ss, r_rs.at[s, t], tx=after)
 
     def product(s, carry):
-        @pl.when(s == 2)
-        def _():
-            q_relay()
-
         pltpu.make_async_copy(wb_v.at[2 * s], wb_v.at[2 * s], wb_sem.at[2 * s]).wait()
 
         @pl.when(s < nx - 1)
@@ -347,24 +335,23 @@
 
     def b_in(kind, t):
         b = held(kind, True)
-        return remote(b_v.at[b, piece(t)], b_v.at[b, piece(t)], b_ss, b_rs.at[kind - 1, t], tx=after)
+        return remote(b_v.at[b, piece(t)], b_v.at[b, piece(t)], b_ss, b_rs.at[kind - 1, t], tx=left)
 
     def b_pair(kind, t):
         b = held(kind, True)
-        return remote(b_v.at[b, piece(t)], b_v.at[b, piece(t)], bp_ss, bp_rs.at[kind, t * 2 // SUBS], tx=partner)
+        return remote(b_v.at[b, piece(t)], b_v.at[b, piece(t)], bp_ss, bp_rs.at[kind], tx=partner)
 
     def act_out(t):
-        b_send(0, t, 1, after).start()
-        b_send(0, t, 2, before).start()
+        b_send(0, t, 1, left).start()
+        b_send(0, t, 2, right).start()
         b_pair(0, t).start()
 
-    def act_in(kind, half):
-        for t in range(half * SUBS // 2, (half + 1) * SUBS // 2):
-            with scope("b%d%d" % (kind, t)):
-                b_in(kind, t).wait_recv()
-            if kind == 1:
-                b_send(1, t, 3, after).start()
-            b_pair(kind, t).start()
+    def act_in(kind, t):
+        with scope("b%d%d" % (kind, t)):
+            b_in(kind, t).wait_recv()
+        if kind == 1:
+            b_send(1, t, 3, left).start()
+        b_pair(kind, t).start()
 
     ay_cp = [remote(ay_s.at[y_peers[k - 1]], ay_r.at[row], ay_ss, ay_rs, ty=y_peers[k - 1]) for k in range(1, ny)]
 
@@ -379,9 +366,9 @@
     def g_in(kind):
         at = held(kind, True)
         with scope("g%d" % kind):
-            remote(g_v.at[at], g_v.at[at], g_ss, g_rs.at[kind - 1], tx=after).wait_recv()
+            remote(g_v.at[at], g_v.at[at], g_ss, g_rs.at[kind - 1], tx=left).wait_recv()
         if kind == 1:
-            g_send(1, 3, after).start()
+            g_send(1, 3, left).start()
         g_pair(kind).start()
 
     def att_out():
@@ -398,8 +385,8 @@
             for n in range(lh):
                 g32[n, a * sb:(a + 1) * sb, :] = part[n * sb:(n + 1) * sb, :]
         g_v[col] = g32[...].astype(BF16)
-        g_send(0, 1, after).start()
-        g_send(0, 2, before).start()
+        g_send(0, 1, left).start()
+        g_send(0, 2, right).start()
         g_pair(0).start()
 
     mid = rows // 2
@@ -407,16 +394,14 @@
     def half_rows(half):
         return pl.ds(half * mid, mid)
 
-    def down(n, half):
-        if half == 0:
-            wd_load(n, 0).wait()
-        part = jnp.dot(b_v[held(n // 2, n % 2 == 0), half_rows(half)], wd_v[n], preferred_element_type=F32)
-        acc[half_rows(half)] = part if n == 0 else acc[half_rows(half)] + part
-
-    def from_pair(kind, half):
-        b = held(kind, False)
-        with scope("bp%d%d" % (kind, half)):
-            remote(b_v.at[b, half_rows(half)], b_v.at[b, half_rows(half)], bp_ss, bp_rs.at[kind, half], tx=partner).wait_recv()
+    def down(n):
+        wd_load(n, 0).wait()
+        if n % 2:
+            b = held(n // 2, False)
+            with scope("bp%d" % (n // 2)):
+                remote(b_v.at[b], b_v.at[b], bp_ss, bp_rs.at[n // 2], tx=partner).wait_recv()
+        part = jnp.dot(b_v[held(n // 2, n % 2 == 0)], wd_v[n], preferred_element_type=F32)
+        acc[...] = part if n == 0 else acc[...] + part
 
     def att_down(half):
         at = pl.ds(half * nx, nx)
@@ -458,47 +443,33 @@
     with scope("qy"):
         remote(qy_r.at[pl.ds(0, ny - 1)], qy_r.at[pl.ds(0, ny - 1)], qy_ss, qy_rs, ty=y_peers[0]).wait_recv()
     for t in range(SUBS):
+        ring(2, t)
         with scope("a%d" % t):
             attend(t)
-        if t == SUBS - 1:
-            att_out()
-        ring(2, t)
+    att_out()
     for t in range(SUBS - 1):
         ring(3, t)
     att_rows()
     ring(3, SUBS - 1)
-    down(0, 0)
-    act_in(1, 0)
-    g_in(1)
-    act_in(2, 0)
-    down(0, 1)
-    act_in(1, 1)
+    down(0)
+    for t in range(SUBS):
+        act_in(1, t)
+        act_in(2, t)
+        if t == 2:
+            g_in(1)
     g_in(2)
-    act_in(2, 1)
-    from_pair(0, 0)
-    down(1, 0)
-    down(2, 0)
-    down(4, 0)
-    act_in(3, 0)
+    for n in (1, 2, 4, 3, 5):
+        down(n)
+    for t in range(SUBS):
+        act_in(3, t)
+    down(6)
     g_in(3)
-    from_pair(1, 0)
-    down(3, 0)
-    from_pair(2, 0)
-    down(5, 0)
-    down(6, 0)
-    act_in(3, 1)
-    from_pair(3, 0)
-    down(7, 0)
+    down(7)
     with scope("gp"):
         remote(g_v.at[pl.ds(0, nx)], g_v.at[pl.ds(0, nx)], gp_ss, gp_rs, tx=partner).wait_recv()
     wo_load.wait()
     att_down(0)
     y_out_half(0)
-    for kind in range(nx):
-        from_pair(kind, 1)
-        if kind > 0:
-            down(2 * kind, 1)
-        down(2 * kind + 1, 1)
     att_down(1)
     y_out_half(1)
     y_sum_half(0)
@@ -510,11 +481,11 @@
         qd_cp.wait_send()
         for ref, send, recv in (
             (stat_r.at[pl.ds(1, ntx - 1)], stat_ss, stat_rs), (gq_r.at[pl.ds(1, ntx - 1)], gq_ss, gq_rs), (gb_r.at[pl.ds(1, ntx - 1)], gb_ss, gb_rs),
-            (qx_s, qx_ss, qx_rs.at[0]), (qy_s.at[pl.ds(1, ny - 1)], qy_ss, qy_rs), (ay_s.at[pl.ds(1, ny - 1)], ay_ss, ay_rs),
+            (qx_in, qx_ss, qx_rs), (qy_s.at[pl.ds(1, ny - 1)], qy_ss, qy_rs), (ay_s.at[pl.ds(1, ny - 1)], ay_ss, ay_rs),
             *((y_s.at[half, pl.ds(1, ny - 1)], y_ss.at[half], y_rs.at[half]) for half in range(2)),
             *((yf.at[half, pl.ds(1, ny - 1)], f_ss.at[half], f_rs.at[half]) for half in range(2)),
             (d_s, d_ss, d_rs.at[0]), (r_s, r_ss, r_rs.at[0, 0]), (g_v.at[pl.ds(1, nx - 1)], g_ss, g_rs.at[0]), (g_v.at[pl.ds(0, nx)], gp_ss, gp_rs),
-            (b_v.at[pl.ds(1, nx - 1)], b_ss, b_rs.at[0, 0]), (b_v.at[pl.ds(0, nx)], bp_ss, bp_rs.at[0, 0]),
+            (b_v.at[pl.ds(1, nx - 1)], b_ss, b_rs.at[0, 0]), (b_v.at[pl.ds(0, nx)], bp_ss, bp_rs.at[0]),
         ):
             remote(ref, ref, send, recv, tx=partner).wait_send()
 
@@ -603,7 +574,7 @@
                 VMEM((rows + 16, dl), BF16), VMEM((8, rows), F32), VMEM((ntx, 8, rows), F32),
                 VMEM((16, hd), BF16), VMEM((ntx, 16, hd), BF16), VMEM((ntx, 16, hd), BF16), VMEM((ntx, 16, hd), BF16), VMEM((rows, rows), F32),
                 VMEM((ntx, rb, qw), F32), VMEM((nx, rb, qw), BF16), VMEM((nx, rb, qw), BF16),
-                VMEM((3, rb, qw), BF16), VMEM((3, rb, qw), BF16), VMEM((rb, qw), F32), VMEM((2, rb, hd), F32),
+                VMEM((nx, rb, qw), BF16), VMEM((nx, rb, qw), BF16), VMEM((rb, qw), F32), VMEM((2, rb, hd), F32),
                 VMEM((ny, sb * lh, hd), F32), VMEM((ny, sb * lh, hd), F32),
                 VMEM((nx, rows, 2 * fb), F32), VMEM((nx, rows, 2 * fb), BF16), VMEM((nx, rows, 2 * fb), BF16),
                 VMEM((nx - 1, rows, 2 * fb), BF16), VMEM((nx - 1, rows, 2 * fb), BF16),
@@ -612,10 +583,10 @@
                 VMEM((ntx, lh, rb, hd), BF16), VMEM((ntx, rows, fb), BF16), VMEM((rows, dl), F32),
                 VMEM((2, ny, yb // 2, dl), BF16), VMEM((2, ny, yb // 2, dl), BF16), VMEM((2, ny, yb // 2, dl), BF16),
                 DMA((5,)), DMA, DMA((ntx,)), DMA((2, sb)), DMA, DMA((ntx,)),
-                DMA, DMA, DMA, DMA, DMA, DMA, DMA, DMA, DMA, DMA((3,)), DMA, DMA,
+                DMA, DMA, DMA, DMA, DMA, DMA, DMA, DMA, DMA, DMA, DMA, DMA,
                 DMA, DMA((nx,)), DMA, DMA((nx - 1, SUBS)),
                 DMA, DMA, DMA, DMA((nx - 1,)), DMA, DMA,
-                DMA, DMA((nx - 1, SUBS)), DMA, DMA((nx, 2)), DMA((2,)), DMA((2,)), DMA((2,)), DMA((2,)),
+                DMA, DMA((nx - 1, SUBS)), DMA, DMA((nx,)), DMA((2,)), DMA((2,)), DMA((2,)), DMA((2,)),
             ],
             compiler_params=pltpu.CompilerParams(collective_id=0, has_side_effects=True, vmem_limit_bytes=52 * 1024 * 1024),
             name="step",
@@ -631,7 +602,7 @@
             in_specs=[sspec] + [vspec] * 4,
             out_specs=(hspec,) * 3,
             scratch_shapes=[VMEM((2, sb, PIECE, hd), BF16), DMA, DMA((2, sb, 2))],
-            compiler_params=pltpu.CompilerParams(vmem_limit_bytes=6 * 1024 * 1024),
+            compiler_params=pltpu.CompilerParams(vmem_limit_bytes=4 * 1024 * 1024),
             name="store",
         )(lens_part, y_vm, new_rows, k_vm, v_vm)
 

time: 55.5 us -> 54.1 us (0.975)
  Pallas kernels: 54.3 us -> 53.3 us
    pallas_call x1, Pallas kernels: 50.3 us -> 49.3 us  [layer_shard(): pl.pallas_call(functools.partial(step_kernel, ny, nx, dl * ntx), out_shap...]
where the time goes in v8:
time: 54.1 us; the launch traced here: 53.9 us
  Pallas kernels  53.3 us (99%)
  between operations  0.66 us (1%)
    pallas_call x1, Pallas kernels, layer_shard(): pl.pallas_call(functools.partial(step_kernel, ny, nx, dl * ntx), out_shap...  49.3 us
    pallas_call x1, Pallas kernels, layer_shard(): pl.pallas_call(functools.partial(store_kernel, ny, ntx), out_shape=(jax.S...  3.98 us

profile of v8, /device:TPU:97, one launch (start us, length us, event | category | flops | bytes accessed | tf_op | source)
XLA Modules:
  0.0 53.9 jit_solution(3364205366960641931)
XLA Ops:
  0.6 0.0 copy-start
  0.6 49.3 %step.1 = (bf16[128,768]{1,0:T(8,128)(2,1)S(1)}, f32[8,128]{1,0:T(8,128)S(1)}, bf16[4,4096,128]{2,1,0:T(8,128)(2,1)S(1)}, bf16[4,4096,128]{2,1,0:T(8,128)(2,1)S(1)}) custom-call(s32[128]{0:T(128)} %lens_ref.3, bf16[128,768]{1,0:T(8,128)(2,1)} %x_h.1, f32[768]{0:T(1024)} %gamma_h.1, bf16[128,128]{1,0:T(8,128)(2,1)} %constant.6.clone.perm_h, ...), custom_call_target="tpu_custom_call" | custom-call | tf_op jit(solution)/shard_map/step/pallas_call | solution.py:561
  49.9 0.0 copy-done
  50.0 4.0 %store.1 = (bf16[128,768]{1,0:T(8,128)(2,1)}, bf16[4,4096,128]{2,1,0:T(8,128)(2,1)}, bf16[4,4096,128]{2,1,0:T(8,128)(2,1)}) custom-call(s32[128]{0:T(128)S(1)} %copy-done, bf16[128,768]{1,0:T(8,128)(2,1)S(1)} %get-tuple-element.7.y_v, f32[8,128]{1,0:T(8,128)S(1)} %get-tuple-element.8.new_v, bf16[4,4096,128]{2,1,0:T(8,128)(2,1)S(1)} %get-tuple-element.9.k_v, ...), custom_call_target="tpu_custom_call" | custom-call | tf_op jit(solution)/shard_map/store/pallas_call | solution.py:595
Async XLA Ops:
  0.6 49.3 %copy-start = (s32[128]{0:T(128)S(1)}, s32[128]{0:T(128)}, u32[]{:S(2)}) copy-start(s32[128]{0:T(128)} %lens_ref.3) | copy-start | bytes 1540

commit v9 on v8

--- a/solution.py
+++ b/solution.py
@@ -58,8 +58,7 @@
     yb = rows // ny
     partner = lax.rem(col + 1, 2) + 2 * chip
     after = 2 * lax.rem(chip + step + nx, nx) + core
-    left = 2 * lax.rem(chip + nx - 1, nx) + core
-    right = 2 * lax.rem(chip + 1, nx) + core
+    before = 2 * lax.rem(chip - step + nx, nx) + core
     tx_peers = [lax.rem(col + k, ntx) for k in range(1, ntx)]
     x_peers = [2 * lax.rem(chip + k, nx) + core for k in range(1, nx)]
     y_peers = [lax.rem(row + k, ny) for k in range(1, ny)]
@@ -80,7 +79,8 @@
         return 2 * at + (core if mine else 1 - core)
 
     def held(kind, mine):
-        return 2 * lax.rem(chip + (0, 1, nx - 1, 2)[kind], nx) + (core if mine else 1 - core)
+        away = (0, -1, 1, 2)[kind] * (step if mine else -step)
+        return 2 * lax.rem(chip + away + 2 * nx, nx) + (core if mine else 1 - core)
 
     def block_loads(n, b):
         at = pl.ds(pl.multiple_of(b * fb, fb), fb)
@@ -91,7 +91,7 @@
 
     def wd_load(n, b):
         at = pl.ds(pl.multiple_of(b * fb, fb), fb)
-        return pltpu.make_async_copy(wd_h.at[at, :], wd_v.at[n], wd_sem.at[n])
+        return pltpu.make_async_copy(wd_h.at[at, :], wd_v.at[n], wd_sem)
 
     first_loads = [
         pltpu.make_async_copy(x_h, x_v, in_sem.at[0]),
@@ -105,8 +105,8 @@
         pltpu.make_async_copy(wk_h, wq_v.at[:, pl.ds(qn, hd)], wq_sem),
         pltpu.make_async_copy(wv_h, wq_v.at[:, pl.ds(qn + hd, hd)], wq_sem),
     ]
-    k_in = [pltpu.make_async_copy(k_h.at[r], kbuf.at[r], kv_sem.at[0, r]) for r in range(sb)]
-    v_in = [pltpu.make_async_copy(v_h.at[r], vbuf.at[r], kv_sem.at[1, r]) for r in range(sb)]
+    k_in = [pltpu.make_async_copy(k_h.at[r], kbuf.at[r], kv_sem.at[0]) for r in range(sb)]
+    v_in = [pltpu.make_async_copy(v_h.at[r], vbuf.at[r], kv_sem.at[1]) for r in range(sb)]
     wo_load = pltpu.make_async_copy(wo_h, wo_v, wo_sem)
     def start_block(s, mine):
         for c in block_loads(2 * s + int(mine), block_of(s, mine)):
@@ -304,7 +304,6 @@
         v_new = kvs[1, pl.ds(row * sb + r, 1), :].astype(BF16).astype(F32)
         new_out[r:r + 1, :] = k_new
         new_out[sb + r:sb + r + 1, :] = v_new
-        k_in[r].wait()
         s_new = jnp.sum(q.astype(F32) * k_new, axis=1, keepdims=True)
         top = jnp.full((heads, hd), -1e30, F32)
         for c in range(ctx // CHUNK):
@@ -319,7 +318,6 @@
         e_new = jnp.exp2((s_new - high) * rate)
         low = jnp.zeros((heads, hd), F32)
         out = e_new.astype(BF16).astype(F32) * v_new
-        v_in[r].wait()
         for c in range(ctx // CHUNK):
             e = jnp.exp2((sbuf[:, c * CHUNK:(c + 1) * CHUNK] - high) * rate)
             for t in range(CHUNK // hd):
@@ -335,22 +333,22 @@
 
     def b_in(kind, t):
         b = held(kind, True)
-        return remote(b_v.at[b, piece(t)], b_v.at[b, piece(t)], b_ss, b_rs.at[kind - 1, t], tx=left)
+        return remote(b_v.at[b, piece(t)], b_v.at[b, piece(t)], b_ss, b_rs.at[kind - 1, t], tx=after)
 
     def b_pair(kind, t):
         b = held(kind, True)
         return remote(b_v.at[b, piece(t)], b_v.at[b, piece(t)], bp_ss, bp_rs.at[kind], tx=partner)
 
     def act_out(t):
-        b_send(0, t, 1, left).start()
-        b_send(0, t, 2, right).start()
+        b_send(0, t, 1, after).start()
+        b_send(0, t, 2, before).start()
         b_pair(0, t).start()
 
     def act_in(kind, t):
         with scope("b%d%d" % (kind, t)):
             b_in(kind, t).wait_recv()
         if kind == 1:
-            b_send(1, t, 3, left).start()
+            b_send(1, t, 3, after).start()
         b_pair(kind, t).start()
 
     ay_cp = [remote(ay_s.at[y_peers[k - 1]], ay_r.at[row], ay_ss, ay_rs, ty=y_peers[k - 1]) for k in range(1, ny)]
@@ -366,9 +364,9 @@
     def g_in(kind):
         at = held(kind, True)
         with scope("g%d" % kind):
-            remote(g_v.at[at], g_v.at[at], g_ss, g_rs.at[kind - 1], tx=left).wait_recv()
+            remote(g_v.at[at], g_v.at[at], g_ss, g_rs.at[kind - 1], tx=after).wait_recv()
         if kind == 1:
-            g_send(1, 3, left).start()
+            g_send(1, 3, after).start()
         g_pair(kind).start()
 
     def att_out():
@@ -385,8 +383,8 @@
             for n in range(lh):
                 g32[n, a * sb:(a + 1) * sb, :] = part[n * sb:(n + 1) * sb, :]
         g_v[col] = g32[...].astype(BF16)
-        g_send(0, 1, left).start()
-        g_send(0, 2, right).start()
+        g_send(0, 1, after).start()
+        g_send(0, 2, before).start()
         g_pair(0).start()
 
     mid = rows // 2
@@ -394,20 +392,24 @@
     def half_rows(half):
         return pl.ds(half * mid, mid)
 
-    def down(n):
-        wd_load(n, 0).wait()
-        if n % 2:
+    def down(n, half=None):
+        if n % 2 and half != 1:
             b = held(n // 2, False)
             with scope("bp%d" % (n // 2)):
                 remote(b_v.at[b], b_v.at[b], bp_ss, bp_rs.at[n // 2], tx=partner).wait_recv()
-        part = jnp.dot(b_v[held(n // 2, n % 2 == 0)], wd_v[n], preferred_element_type=F32)
-        acc[...] = part if n == 0 else acc[...] + part
-
-    def att_down(half):
-        at = pl.ds(half * nx, nx)
+        at = pl.ds(0, rows) if half is None else half_rows(half)
+        part = jnp.dot(b_v[held(n // 2, n % 2 == 0), at], wd_v[n], preferred_element_type=F32)
+        acc[at] = part if n == 0 else acc[at] + part
+
+    def att_down():
+        with scope("gp"):
+            remote(g_v.at[pl.ds(0, nx)], g_v.at[pl.ds(0, nx)], gp_ss, gp_rs, tx=partner).wait_recv()
+        wo_load.wait()
+        part = acc[...]
         for n in range(0, lh, 2):
-            pair = jnp.concatenate([g_v[at, n].reshape(mid, hd), g_v[at, n + 1].reshape(mid, hd)], axis=1)
-            acc[half_rows(half)] += jnp.dot(pair, wo_v[n * hd:(n + 2) * hd, :], preferred_element_type=F32)
+            pair = jnp.concatenate([g_v[:, n].reshape(rows, hd), g_v[:, n + 1].reshape(rows, hd)], axis=1)
+            part = part + jnp.dot(pair, wo_v[n * hd:(n + 2) * hd, :], preferred_element_type=F32)
+        acc[...] = part
 
     def y_out_half(half):
         part = jnp.dot(back_v[...], acc[half_rows(half)].astype(BF16), preferred_element_type=F32)
@@ -440,17 +442,20 @@
     for n in range(ntx):
         wd_load(n, held(n // 2, n % 2 == 0)).start()
     wo_load.start()
-    with scope("qy"):
-        remote(qy_r.at[pl.ds(0, ny - 1)], qy_r.at[pl.ds(0, ny - 1)], qy_ss, qy_rs, ty=y_peers[0]).wait_recv()
     for t in range(SUBS):
         ring(2, t)
+        if t == 0:
+            with scope("qy"):
+                remote(qy_r.at[pl.ds(0, ny - 1)], qy_r.at[pl.ds(0, ny - 1)], qy_ss, qy_rs, ty=y_peers[0]).wait_recv()
+            pltpu.make_async_copy(kbuf, kbuf, kv_sem.at[0]).wait()
+            pltpu.make_async_copy(vbuf, vbuf, kv_sem.at[1]).wait()
         with scope("a%d" % t):
             attend(t)
     att_out()
-    for t in range(SUBS - 1):
+    for t in range(SUBS):
         ring(3, t)
     att_rows()
-    ring(3, SUBS - 1)
+    pltpu.make_async_copy(wd_v, wd_v, wd_sem).wait()
     down(0)
     for t in range(SUBS):
         act_in(1, t)
@@ -462,16 +467,12 @@
         down(n)
     for t in range(SUBS):
         act_in(3, t)
+    g_in(3)
     down(6)
-    g_in(3)
-    down(7)
-    with scope("gp"):
-        remote(g_v.at[pl.ds(0, nx)], g_v.at[pl.ds(0, nx)], gp_ss, gp_rs, tx=partner).wait_recv()
-    wo_load.wait()
-    att_down(0)
-    y_out_half(0)
-    att_down(1)
-    y_out_half(1)
+    att_down()
+    for half in range(2):
+        down(7, half)
+        y_out_half(half)
     y_sum_half(0)
     y_sum_half(1)
     y_all_half(0)
@@ -582,7 +583,7 @@
                 VMEM((ny, sb * lh, hd), BF16), VMEM((ny, sb * lh, hd), BF16), VMEM((lh, rb, hd), F32),
                 VMEM((ntx, lh, rb, hd), BF16), VMEM((ntx, rows, fb), BF16), VMEM((rows, dl), F32),
                 VMEM((2, ny, yb // 2, dl), BF16), VMEM((2, ny, yb // 2, dl), BF16), VMEM((2, ny, yb // 2, dl), BF16),
-                DMA((5,)), DMA, DMA((ntx,)), DMA((2, sb)), DMA, DMA((ntx,)),
+                DMA((5,)), DMA, DMA((ntx,)), DMA((2,)), DMA, DMA,
                 DMA, DMA, DMA, DMA, DMA, DMA, DMA, DMA, DMA, DMA, DMA, DMA,
                 DMA, DMA((nx,)), DMA, DMA((nx - 1, SUBS)),
                 DMA, DMA, DMA, DMA((nx - 1,)), DMA, DMA,

time: 54.1 us -> 53 us (0.980)
  Pallas kernels: 53.3 us -> 52.2 us
    pallas_call x1, Pallas kernels: 49.3 us -> 48.2 us  [layer_shard(): pl.pallas_call(functools.partial(step_kernel, ny, nx, dl * ntx), out_shap...]
where the time goes in v9:
time: 53 us; the launch traced here: 52.9 us
  Pallas kernels  52.2 us (98%)
  between operations  0.66 us (1%)
    pallas_call x1, Pallas kernels, layer_shard(): pl.pallas_call(functools.partial(step_kernel, ny, nx, dl * ntx), out_shap...  48.2 us
    pallas_call x1, Pallas kernels, layer_shard(): pl.pallas_call(functools.partial(store_kernel, ny, ntx), out_shape=(jax.S...  3.98 us

profile of v9, /device:TPU:97, one launch (start us, length us, event | category | flops | bytes accessed | tf_op | source)
XLA Modules:
  0.0 52.9 jit_solution(13487624902520389887)
XLA Ops:
  0.6 0.0 copy-start
  0.6 48.2 %step.1 = (bf16[128,768]{1,0:T(8,128)(2,1)S(1)}, f32[8,128]{1,0:T(8,128)S(1)}, bf16[4,4096,128]{2,1,0:T(8,128)(2,1)S(1)}, bf16[4,4096,128]{2,1,0:T(8,128)(2,1)S(1)}) custom-call(s32[128]{0:T(128)} %lens_ref.3, bf16[128,768]{1,0:T(8,128)(2,1)} %x_h.1, f32[768]{0:T(1024)} %gamma_h.1, bf16[128,128]{1,0:T(8,128)(2,1)} %constant.6.clone.perm_h, ...), custom_call_target="tpu_custom_call" | custom-call | tf_op jit(solution)/shard_map/step/pallas_call | solution.py:562
  48.9 0.0 copy-done
  48.9 4.0 %store.1 = (bf16[128,768]{1,0:T(8,128)(2,1)}, bf16[4,4096,128]{2,1,0:T(8,128)(2,1)}, bf16[4,4096,128]{2,1,0:T(8,128)(2,1)}) custom-call(s32[128]{0:T(128)S(1)} %copy-done, bf16[128,768]{1,0:T(8,128)(2,1)S(1)} %get-tuple-element.7.y_v, f32[8,128]{1,0:T(8,128)S(1)} %get-tuple-element.8.new_v, bf16[4,4096,128]{2,1,0:T(8,128)(2,1)S(1)} %get-tuple-element.9.k_v, ...), custom_call_target="tpu_custom_call" | custom-call | tf_op jit(solution)/shard_map/store/pallas_call | solution.py:596
Async XLA Ops:
  0.6 48.2 %copy-start = (s32[128]{0:T(128)S(1)}, s32[128]{0:T(128)}, u32[]{:S(2)}) copy-start(s32[128]{0:T(128)} %lens_ref.3) | copy-start | bytes 1540

commit v10 on v9

--- a/solution.py
+++ b/solution.py
@@ -16,7 +16,7 @@
 BF16 = jnp.bfloat16
 VMEM = pltpu.VMEM
 DMA = pltpu.SemaphoreType.DMA
-SUBS = 4
+SUBS = 8
 CHUNK = 1024
 PIECE = 512
 scope = jax.named_scope
@@ -392,24 +392,21 @@
     def half_rows(half):
         return pl.ds(half * mid, mid)
 
-    def down(n, half=None):
-        if n % 2 and half != 1:
+    def down(n):
+        if n % 2:
             b = held(n // 2, False)
             with scope("bp%d" % (n // 2)):
                 remote(b_v.at[b], b_v.at[b], bp_ss, bp_rs.at[n // 2], tx=partner).wait_recv()
-        at = pl.ds(0, rows) if half is None else half_rows(half)
-        part = jnp.dot(b_v[held(n // 2, n % 2 == 0), at], wd_v[n], preferred_element_type=F32)
-        acc[at] = part if n == 0 else acc[at] + part
-
-    def att_down():
-        with scope("gp"):
-            remote(g_v.at[pl.ds(0, nx)], g_v.at[pl.ds(0, nx)], gp_ss, gp_rs, tx=partner).wait_recv()
-        wo_load.wait()
-        part = acc[...]
+        part = jnp.dot(b_v[held(n // 2, n % 2 == 0)], wd_v[n], preferred_element_type=F32)
+        acc[...] = part if n == 0 else acc[...] + part
+
+    def att_down(half):
+        at = pl.ds(half * nx, nx)
+        part = acc[half_rows(half)]
         for n in range(0, lh, 2):
-            pair = jnp.concatenate([g_v[:, n].reshape(rows, hd), g_v[:, n + 1].reshape(rows, hd)], axis=1)
+            pair = jnp.concatenate([g_v[at, n].reshape(mid, hd), g_v[at, n + 1].reshape(mid, hd)], axis=1)
             part = part + jnp.dot(pair, wo_v[n * hd:(n + 2) * hd, :], preferred_element_type=F32)
-        acc[...] = part
+        acc[half_rows(half)] = part
 
     def y_out_half(half):
         part = jnp.dot(back_v[...], acc[half_rows(half)].astype(BF16), preferred_element_type=F32)
@@ -449,8 +446,9 @@
                 remote(qy_r.at[pl.ds(0, ny - 1)], qy_r.at[pl.ds(0, ny - 1)], qy_ss, qy_rs, ty=y_peers[0]).wait_recv()
             pltpu.make_async_copy(kbuf, kbuf, kv_sem.at[0]).wait()
             pltpu.make_async_copy(vbuf, vbuf, kv_sem.at[1]).wait()
-        with scope("a%d" % t):
-            attend(t)
+        if t % (SUBS // sb) == 0:
+            with scope("a%d" % (t * sb // SUBS)):
+                attend(t * sb // SUBS)
     att_out()
     for t in range(SUBS):
         ring(3, t)
@@ -460,8 +458,7 @@
     for t in range(SUBS):
         act_in(1, t)
         act_in(2, t)
-        if t == 2:
-            g_in(1)
+    g_in(1)
     g_in(2)
     for n in (1, 2, 4, 3, 5):
         down(n)
@@ -469,9 +466,12 @@
         act_in(3, t)
     g_in(3)
     down(6)
-    att_down()
+    down(7)
+    with scope("gp"):
+        remote(g_v.at[pl.ds(0, nx)], g_v.at[pl.ds(0, nx)], gp_ss, gp_rs, tx=partner).wait_recv()
+    wo_load.wait()
     for half in range(2):
-        down(7, half)
+        att_down(half)
         y_out_half(half)
     y_sum_half(0)
     y_sum_half(1)

time: 53 us -> 52.8 us (level)
  no operation moved by 1% of the time
where the time goes in v10:
time: 52.8 us; the launch traced here: 52.7 us
  Pallas kernels  52.1 us (99%)
  between operations  0.66 us (1%)
    pallas_call x1, Pallas kernels, layer_shard(): pl.pallas_call(functools.partial(step_kernel, ny, nx, dl * ntx), out_shap...  48.1 us
    pallas_call x1, Pallas kernels, layer_shard(): pl.pallas_call(functools.partial(store_kernel, ny, ntx), out_shape=(jax.S...  3.98 us

profile of v10, /device:TPU:97, one launch (start us, length us, event | category | flops | bytes accessed | tf_op | source)
XLA Modules:
  0.0 52.7 jit_solution(14771089956276091706)
XLA Ops:
  0.6 0.0 copy-start
  0.6 48.1 %step.1 = (bf16[128,768]{1,0:T(8,128)(2,1)S(1)}, f32[8,128]{1,0:T(8,128)S(1)}, bf16[4,4096,128]{2,1,0:T(8,128)(2,1)S(1)}, bf16[4,4096,128]{2,1,0:T(8,128)(2,1)S(1)}) custom-call(s32[128]{0:T(128)} %lens_ref.3, bf16[128,768]{1,0:T(8,128)(2,1)} %x_h.1, f32[768]{0:T(1024)} %gamma_h.1, bf16[128,128]{1,0:T(8,128)(2,1)} %constant.6.clone.perm_h, ...), custom_call_target="tpu_custom_call" | custom-call | tf_op jit(solution)/shard_map/step/pallas_call | solution.py:562
  48.7 0.0 copy-done
  48.7 4.0 %store.1 = (bf16[128,768]{1,0:T(8,128)(2,1)}, bf16[4,4096,128]{2,1,0:T(8,128)(2,1)}, bf16[4,4096,128]{2,1,0:T(8,128)(2,1)}) custom-call(s32[128]{0:T(128)S(1)} %copy-done, bf16[128,768]{1,0:T(8,128)(2,1)S(1)} %get-tuple-element.7.y_v, f32[8,128]{1,0:T(8,128)S(1)} %get-tuple-element.8.new_v, bf16[4,4096,128]{2,1,0:T(8,128)(2,1)S(1)} %get-tuple-element.9.k_v, ...), custom_call_target="tpu_custom_call" | custom-call | tf_op jit(solution)/shard_map/store/pallas_call | solution.py:596
Async XLA Ops:
  0.6 48.1 %copy-start = (s32[128]{0:T(128)S(1)}, s32[128]{0:T(128)}, u32[]{:S(2)}) copy-start(s32[128]{0:T(128)} %lens_ref.3) | copy-start | bytes 1540

commit v11 on v10

--- a/solution.py
+++ b/solution.py
@@ -18,7 +18,7 @@
 DMA = pltpu.SemaphoreType.DMA
 SUBS = 8
 CHUNK = 1024
-PIECE = 512
+EVEN = 6
 scope = jax.named_scope
 
 
@@ -32,9 +32,9 @@
 
 
 def step_kernel(ny, nx, d_model, lens_ref, x_h, gamma_h, perm_h, back_h, freq_h, wq_h, wk_h, wv_h, wg_h, wu_h, k_h, v_h, wo_h, wd_h,
-                y_out, new_out, kbuf, vbuf,
+                y_out, kbuf, vbuf,
                 x_v, gamma_v, perm_v, back_v, freq_v, wq_v, wb_v, wo_v, wd_v, h_v, stat_s, stat_r, gq_s, gq_r, gb_s, gb_r, norm,
-                qp, qd_s, qd_r, qx_s, qx_r, qsum, kvs, qy_s, qy_r, own, d_s, d_r, r_s, r_r,
+                qp, qd_s, qd_r, new_rows, qx_s, qx_r, qsum, kvs, qy_s, qy_r, own, d_s, d_r, r_s, r_r,
                 turns, qs, sbuf, o32, ay_s, ay_r, g32, g_v, b_v, acc, y_s, y_r, yf,
                 in_sem, wq_sem, wb_sem, kv_sem, wo_sem, wd_sem, stat_ss, stat_rs, gq_ss, gq_rs, gb_ss, gb_rs, qd_ss, qd_rs, qx_ss, qx_rs, qy_ss, qy_rs,
                 d_ss, d_rs, r_ss, r_rs, ay_ss, ay_rs, g_ss, g_rs, gp_ss, gp_rs, b_ss, b_rs, bp_ss, bp_rs, y_ss, y_rs, f_ss, f_rs):
@@ -59,6 +59,8 @@
     partner = lax.rem(col + 1, 2) + 2 * chip
     after = 2 * lax.rem(chip + step + nx, nx) + core
     before = 2 * lax.rem(chip - step + nx, nx) + core
+    right = 2 * lax.rem(chip + 1, nx) + core
+    left = 2 * lax.rem(chip + nx - 1, nx) + core
     tx_peers = [lax.rem(col + k, ntx) for k in range(1, ntx)]
     x_peers = [2 * lax.rem(chip + k, nx) + core for k in range(1, nx)]
     y_peers = [lax.rem(row + k, ny) for k in range(1, ny)]
@@ -302,8 +304,8 @@
         q = qs[...].astype(BF16)
         k_new = turn(kvs[0, pl.ds(row * sb + r, 1), :], r).astype(BF16).astype(F32)
         v_new = kvs[1, pl.ds(row * sb + r, 1), :].astype(BF16).astype(F32)
-        new_out[r:r + 1, :] = k_new
-        new_out[sb + r:sb + r + 1, :] = v_new
+        new_rows[r:r + 1, :] = k_new
+        new_rows[sb + r:sb + r + 1, :] = v_new
         s_new = jnp.sum(q.astype(F32) * k_new, axis=1, keepdims=True)
         top = jnp.full((heads, hd), -1e30, F32)
         for c in range(ctx // CHUNK):
@@ -327,8 +329,7 @@
         for a in range(ny):
             o32[a, pl.ds(r, lh, stride=sb), :] = out[a * lh:(a + 1) * lh]
 
-    def b_send(kind, t, slot, to):
-        b = held(kind, True)
+    def b_send(b, t, slot, to):
         return remote(b_v.at[b, piece(t)], b_v.at[b, piece(t)], b_ss, b_rs.at[slot - 1, t], tx=to)
 
     def b_in(kind, t):
@@ -340,34 +341,34 @@
         return remote(b_v.at[b, piece(t)], b_v.at[b, piece(t)], bp_ss, bp_rs.at[kind], tx=partner)
 
     def act_out(t):
-        b_send(0, t, 1, after).start()
-        b_send(0, t, 2, before).start()
+        b_send(col, t, 1, after).start()
+        b_send(col, t, 2, before).start()
         b_pair(0, t).start()
 
     def act_in(kind, t):
         with scope("b%d%d" % (kind, t)):
             b_in(kind, t).wait_recv()
+        if kind == 1 and t < EVEN:
+            b_send(before, t, 3, after).start()
+        if kind == 2 and t >= EVEN:
+            b_send(right, t, 3, left).start()
+        b_pair(kind, t).start()
+
+    ay_cp = [remote(ay_s.at[y_peers[k - 1]], ay_r.at[row], ay_ss, ay_rs, ty=y_peers[k - 1]) for k in range(1, ny)]
+
+    def g_send(at, slot, to):
+        return remote(g_v.at[at], g_v.at[at], g_ss, g_rs.at[slot - 1], tx=to)
+
+    def g_pair(at):
+        return remote(g_v.at[at], g_v.at[at], gp_ss, gp_rs, tx=partner)
+
+    def g_in(kind):
+        at = (right, left, held(3, True))[kind - 1]
+        with scope("g%d" % kind):
+            g_send(at, kind, left).wait_recv()
         if kind == 1:
-            b_send(1, t, 3, after).start()
-        b_pair(kind, t).start()
-
-    ay_cp = [remote(ay_s.at[y_peers[k - 1]], ay_r.at[row], ay_ss, ay_rs, ty=y_peers[k - 1]) for k in range(1, ny)]
-
-    def g_send(kind, slot, to):
-        at = held(kind, True)
-        return remote(g_v.at[at], g_v.at[at], g_ss, g_rs.at[slot - 1], tx=to)
-
-    def g_pair(kind):
-        at = held(kind, True)
-        return remote(g_v.at[at], g_v.at[at], gp_ss, gp_rs, tx=partner)
-
-    def g_in(kind):
-        at = held(kind, True)
-        with scope("g%d" % kind):
-            remote(g_v.at[at], g_v.at[at], g_ss, g_rs.at[kind - 1], tx=after).wait_recv()
-        if kind == 1:
-            g_send(1, 3, after).start()
-        g_pair(kind).start()
+            g_send(right, 3, left).start()
+        g_pair(at).start()
 
     def att_out():
         ay_s[...] = o32[...].astype(BF16)
@@ -383,9 +384,9 @@
             for n in range(lh):
                 g32[n, a * sb:(a + 1) * sb, :] = part[n * sb:(n + 1) * sb, :]
         g_v[col] = g32[...].astype(BF16)
-        g_send(0, 1, after).start()
-        g_send(0, 2, before).start()
-        g_pair(0).start()
+        g_send(col, 1, left).start()
+        g_send(col, 2, right).start()
+        g_pair(col).start()
 
     mid = rows // 2
 
@@ -473,8 +474,24 @@
     for half in range(2):
         att_down(half)
         y_out_half(half)
+    def put_rows(buf, base):
+        for r in range(sb):
+            length = lens_ref[(row * ntx + col) * sb + r]
+
+            def some(c, carry):
+                at = pl.ds(pl.multiple_of(c * CHUNK, CHUNK), CHUNK)
+                here = lax.broadcasted_iota(jnp.int32, (CHUNK, hd), 0) + c * CHUNK == length
+                buf[r, at, :] = jnp.where(here, new_rows[base + r:base + r + 1, :], buf[r, at, :].astype(F32)).astype(BF16)
+                return carry
+
+            lax.fori_loop(0, ctx // CHUNK, some, 0)
+
+    with scope("putk"):
+        put_rows(kbuf, 0)
     y_sum_half(0)
     y_sum_half(1)
+    with scope("putv"):
+        put_rows(vbuf, sb)
     y_all_half(0)
     y_all_half(1)
 
@@ -491,44 +508,14 @@
             remote(ref, ref, send, recv, tx=partner).wait_send()
 
 
-def store_kernel(ny, ntx, lens_ref, y_v, new_v, k_v, v_v, y_h, ko_h, vo_h, patch, y_sem, out_sem):
-    first = (lax.axis_index("ty") * ntx + lax.axis_index("tx")) * k_v.shape[0]
-    sb, ctx, hd = k_v.shape
-    pieces = ctx // PIECE
-    y_cp = pltpu.make_async_copy(y_v, y_h, y_sem)
-    y_cp.start()
-
-    def write(a, buf, out):
-        def sequence(r, carry):
-            length = lens_ref[first + r]
-            spot = lax.div(length, PIECE)
-
-            def other(c, inner):
-                c = c + jnp.where(c >= spot, 1, 0)
-                rest = pl.ds(pl.multiple_of(c * PIECE, PIECE), PIECE)
-                pltpu.make_async_copy(buf.at[r, rest], out.at[r, rest], out_sem.at[a, r, 1]).start()
-                return inner
-
-            lax.fori_loop(0, pieces - 1, other, 0)
-            at = pl.ds(pl.multiple_of(spot * PIECE, PIECE), PIECE)
-            here = lax.broadcasted_iota(jnp.int32, (PIECE, hd), 0) == length - spot * PIECE
-            patch[a, r] = jnp.where(here, new_v[pl.ds(a * sb + r, 1), :], buf[r, at, :].astype(F32)).astype(BF16)
-            pltpu.make_async_copy(patch.at[a, r], out.at[r, at], out_sem.at[a, r, 0]).start()
-            return carry
-
-        lax.fori_loop(0, sb, sequence, 0)
-
-    def finish(a, buf, out):
-        for r in range(sb):
-            pltpu.make_async_copy(patch.at[a, r], out.at[r, pl.ds(0, PIECE)], out_sem.at[a, r, 0]).wait()
-            rest = pl.ds(0, ctx - PIECE)
-            pltpu.make_async_copy(buf.at[r, rest], out.at[r, rest], out_sem.at[a, r, 1]).wait()
-
-    write(0, k_v, ko_h)
-    write(1, v_v, vo_h)
-    y_cp.wait()
-    finish(0, k_v, ko_h)
-    finish(1, v_v, vo_h)
+def store_kernel(y_v, k_v, v_v, y_h, ko_h, vo_h, y_sem, out_sem):
+    copies = [pltpu.make_async_copy(k_v.at[r], ko_h.at[r], out_sem.at[0, r]) for r in range(k_v.shape[0])]
+    copies += [pltpu.make_async_copy(v_v.at[r], vo_h.at[r], out_sem.at[1, r]) for r in range(v_v.shape[0])]
+    copies += [pltpu.make_async_copy(y_v, y_h, y_sem)]
+    for c in copies:
+        c.start()
+    for c in copies:
+        c.wait()
 
 
 def solution(mesh):
@@ -559,23 +546,22 @@
         freqs = np.power(ROPE_BASE, -(np.arange(hd // 2, dtype=np.float32) * 2.0) / hd).astype(np.float32)
         freqs = jnp.asarray(np.tile(np.concatenate([freqs, freqs])[None, :], (8, 1)))
 
-        y_vm, new_rows, k_vm, v_vm = pl.pallas_call(
+        y_vm, k_vm, v_vm = pl.pallas_call(
             functools.partial(step_kernel, ny, nx, dl * ntx),
             out_shape=(
                 pltpu.VMEM((rows, dl), BF16),
-                pltpu.VMEM((2 * sb, hd), F32),
                 pltpu.VMEM(k_blk.shape, BF16),
                 pltpu.VMEM(v_blk.shape, BF16),
             ),
             in_specs=[sspec] + [hspec] * 14,
-            out_specs=(vspec,) * 4,
+            out_specs=(vspec,) * 3,
             scratch_shapes=[
                 VMEM((rows, dl), BF16), VMEM((dl,), F32), VMEM((rows, rows), BF16), VMEM((rows // 2, rows // 2), BF16), VMEM((8, hd), F32),
                 VMEM((dl, qw), BF16), VMEM((ntx, dl, 2 * fb), BF16), VMEM((qn, dl), BF16), VMEM((ntx, fb, dl), BF16),
                 VMEM((rows + 16, dl), BF16), VMEM((8, rows), F32), VMEM((ntx, 8, rows), F32),
                 VMEM((16, hd), BF16), VMEM((ntx, 16, hd), BF16), VMEM((ntx, 16, hd), BF16), VMEM((ntx, 16, hd), BF16), VMEM((rows, rows), F32),
                 VMEM((ntx, rb, qw), F32), VMEM((nx, rb, qw), BF16), VMEM((nx, rb, qw), BF16),
-                VMEM((nx, rb, qw), BF16), VMEM((nx, rb, qw), BF16), VMEM((rb, qw), F32), VMEM((2, rb, hd), F32),
+                VMEM((2 * sb, hd), F32), VMEM((nx, rb, qw), BF16), VMEM((nx, rb, qw), BF16), VMEM((rb, qw), F32), VMEM((2, rb, hd), F32),
                 VMEM((ny, sb * lh, hd), F32), VMEM((ny, sb * lh, hd), F32),
                 VMEM((nx, rows, 2 * fb), F32), VMEM((nx, rows, 2 * fb), BF16), VMEM((nx, rows, 2 * fb), BF16),
                 VMEM((nx - 1, rows, 2 * fb), BF16), VMEM((nx - 1, rows, 2 * fb), BF16),
@@ -594,18 +580,18 @@
         )(lens_part, x_blk, gamma_blk, perm, back, freqs, w_query, w_key, w_value, w_gate, w_up, k_blk, v_blk, w_out, w_down)
 
         return pl.pallas_call(
-            functools.partial(store_kernel, ny, ntx),
+            store_kernel,
             out_shape=(
                 jax.ShapeDtypeStruct((rows, dl), BF16),
                 jax.ShapeDtypeStruct(k_blk.shape, BF16),
                 jax.ShapeDtypeStruct(v_blk.shape, BF16),
             ),
-            in_specs=[sspec] + [vspec] * 4,
+            in_specs=[vspec] * 3,
             out_specs=(hspec,) * 3,
-            scratch_shapes=[VMEM((2, sb, PIECE, hd), BF16), DMA, DMA((2, sb, 2))],
+            scratch_shapes=[DMA, DMA((2, sb))],
             compiler_params=pltpu.CompilerParams(vmem_limit_bytes=4 * 1024 * 1024),
             name="store",
-        )(lens_part, y_vm, new_rows, k_vm, v_vm)
+        )(y_vm, k_vm, v_vm)
 
     in_specs = (P("dp", "tx"), P("dp"), cache_spec, cache_spec, P("tx"), P("tx", "ty"), P("tx", None), P("tx", None), P("tx", "ty"), P("tx", "ty"), P("ty", "tx"), P("ty", "tx"))
     out_specs = (P("dp", "tx"), cache_spec, cache_spec)

time: 52.8 us -> 51.6 us (0.977)
  Pallas kernels: 52.1 us -> 50.8 us
    pallas_call x1, Pallas kernels: 48.1 us -> 47.4 us  [layer_shard(): pl.pallas_call(functools.partial(step_kernel, ny, nx, dl * ntx), out_shap...]
    pallas_call x1, Pallas kernels: 3.98 us -> 3.4 us  [layer_shard(): pl.pallas_call(store_kernel, out_shape=(jax.ShapeDtypeStruct((rows, dl),...]
where the time goes in v11:
time: 51.6 us; the launch traced here: 51.4 us
  Pallas kernels  50.8 us (98%)
  between operations  0.64 us (1%)
    pallas_call x1, Pallas kernels, layer_shard(): pl.pallas_call(functools.partial(step_kernel, ny, nx, dl * ntx), out_shap...  47.4 us
    pallas_call x1, Pallas kernels, layer_shard(): pl.pallas_call(store_kernel, out_shape=(jax.ShapeDtypeStruct((rows, dl),...  3.4 us

profile of v11, /device:TPU:97, one launch (start us, length us, event | category | flops | bytes accessed | tf_op | source)
XLA Modules:
  0.0 51.4 jit_solution(18125109528844995503)
XLA Ops:
  0.6 47.4 %step.1 = (bf16[128,768]{1,0:T(8,128)(2,1)S(1)}, bf16[4,4096,128]{2,1,0:T(8,128)(2,1)S(1)}, bf16[4,4096,128]{2,1,0:T(8,128)(2,1)S(1)}) custom-call(s32[128]{0:T(128)} %lens_ref.1, bf16[128,768]{1,0:T(8,128)(2,1)} %x_h.1, f32[768]{0:T(1024)} %gamma_h.1, bf16[128,128]{1,0:T(8,128)(2,1)} %constant.6.clone.perm_h, bf16[64,64]{1,0:T(8,128)(2,1)} %constant.7.clone.back_h, ...), custom_call_target="tpu_custom_call" | custom-call | tf_op jit(solution)/shard_map/step/pallas_call | solution.py:549
  48.0 3.4 %store.1 = (bf16[128,768]{1,0:T(8,128)(2,1)}, bf16[4,4096,128]{2,1,0:T(8,128)(2,1)}, bf16[4,4096,128]{2,1,0:T(8,128)(2,1)}) custom-call(bf16[128,768]{1,0:T(8,128)(2,1)S(1)} %get-tuple-element.6.y_v, bf16[4,4096,128]{2,1,0:T(8,128)(2,1)S(1)} %get-tuple-element.7.k_v, bf16[4,4096,128]{2,1,0:T(8,128)(2,1)S(1)} %get-tuple-element.8.v_v), custom_call_target="tpu_custom_call" | custom-call | tf_op jit(solution)/shard_map/store/pallas_call | solution.py:582

commit v12 on v11

--- a/solution.py
+++ b/solution.py
@@ -18,7 +18,7 @@
 DMA = pltpu.SemaphoreType.DMA
 SUBS = 8
 CHUNK = 1024
-EVEN = 6
+EVEN = 4
 scope = jax.named_scope
 
 
@@ -119,7 +119,6 @@
     for c in first_loads:
         c.wait()
     start_block(0, False)
-    start_block(0, True)
 
     xp = jnp.dot(perm_v[...], x_v[...], preferred_element_type=F32)
     own_mean = jnp.sum(xp, axis=1, keepdims=True) / dl
@@ -138,6 +137,7 @@
         return jnp.concatenate(parts + [jnp.zeros((16 - tiles, hd), F32)], axis=0).astype(BF16)
 
     pltpu.make_async_copy(wq_v, wq_v, wq_sem).wait()
+    start_block(0, True)
     start_block(1, False)
     part = jnp.dot(h_v[...], wq_v[...], preferred_element_type=F32)
     qp[...] = part[:rows].reshape(ntx, rb, qw)

time: 51.6 us -> 52 us (level)
  no operation moved by 1% of the time
where the time goes in v12:
time: 52 us; the launch traced here: 51.9 us
  Pallas kernels  51.2 us (98%)
  between operations  0.64 us (1%)
    pallas_call x1, Pallas kernels, layer_shard(): pl.pallas_call(functools.partial(step_kernel, ny, nx, dl * ntx), out_shap...  47.8 us
    pallas_call x1, Pallas kernels, layer_shard(): pl.pallas_call(store_kernel, out_shape=(jax.ShapeDtypeStruct((rows, dl),...  3.4 us

profile of v12, /device:TPU:97, one launch (start us, length us, event | category | flops | bytes accessed | tf_op | source)
XLA Modules:
  0.0 51.9 jit_solution(9871163235565883312)
XLA Ops:
  0.6 47.8 %step.1 = (bf16[128,768]{1,0:T(8,128)(2,1)S(1)}, bf16[4,4096,128]{2,1,0:T(8,128)(2,1)S(1)}, bf16[4,4096,128]{2,1,0:T(8,128)(2,1)S(1)}) custom-call(s32[128]{0:T(128)} %lens_ref.1, bf16[128,768]{1,0:T(8,128)(2,1)} %x_h.1, f32[768]{0:T(1024)} %gamma_h.1, bf16[128,128]{1,0:T(8,128)(2,1)} %constant.6.clone.perm_h, bf16[64,64]{1,0:T(8,128)(2,1)} %constant.7.clone.back_h, ...), custom_call_target="tpu_custom_call" | custom-call | tf_op jit(solution)/shard_map/step/pallas_call | solution.py:549
  48.5 3.4 %store.1 = (bf16[128,768]{1,0:T(8,128)(2,1)}, bf16[4,4096,128]{2,1,0:T(8,128)(2,1)}, bf16[4,4096,128]{2,1,0:T(8,128)(2,1)}) custom-call(bf16[128,768]{1,0:T(8,128)(2,1)S(1)} %get-tuple-element.6.y_v, bf16[4,4096,128]{2,1,0:T(8,128)(2,1)S(1)} %get-tuple-element.7.k_v, bf16[4,4096,128]{2,1,0:T(8,128)(2,1)S(1)} %get-tuple-element.8.v_v), custom_call_target="tpu_custom_call" | custom-call | tf_op jit(solution)/shard_map/store/pallas_call | solution.py:582

commit v13 on v12

--- a/solution.py
+++ b/solution.py
@@ -18,7 +18,7 @@
 DMA = pltpu.SemaphoreType.DMA
 SUBS = 8
 CHUNK = 1024
-EVEN = 4
+EVEN = 6
 scope = jax.named_scope
 
 

time: 52 us -> 51.5 us (level)
  no operation moved by 1% of the time
where the time goes in v13:
time: 51.5 us; the launch traced here: 51.4 us
  Pallas kernels  50.7 us (98%)
  between operations  0.64 us (1%)
    pallas_call x1, Pallas kernels, layer_shard(): pl.pallas_call(functools.partial(step_kernel, ny, nx, dl * ntx), out_shap...  47.3 us
    pallas_call x1, Pallas kernels, layer_shard(): pl.pallas_call(store_kernel, out_shape=(jax.ShapeDtypeStruct((rows, dl),...  3.4 us

profile of v13, /device:TPU:97, one launch (start us, length us, event | category | flops | bytes accessed | tf_op | source)
XLA Modules:
  0.0 51.4 jit_solution(12992133496816369740)
XLA Ops:
  0.6 47.3 %step.1 = (bf16[128,768]{1,0:T(8,128)(2,1)S(1)}, bf16[4,4096,128]{2,1,0:T(8,128)(2,1)S(1)}, bf16[4,4096,128]{2,1,0:T(8,128)(2,1)S(1)}) custom-call(s32[128]{0:T(128)} %lens_ref.1, bf16[128,768]{1,0:T(8,128)(2,1)} %x_h.1, f32[768]{0:T(1024)} %gamma_h.1, bf16[128,128]{1,0:T(8,128)(2,1)} %constant.6.clone.perm_h, bf16[64,64]{1,0:T(8,128)(2,1)} %constant.7.clone.back_h, ...), custom_call_target="tpu_custom_call" | custom-call | tf_op jit(solution)/shard_map/step/pallas_call | solution.py:549
  48.0 3.4 %store.1 = (bf16[128,768]{1,0:T(8,128)(2,1)}, bf16[4,4096,128]{2,1,0:T(8,128)(2,1)}, bf16[4,4096,128]{2,1,0:T(8,128)(2,1)}) custom-call(bf16[128,768]{1,0:T(8,128)(2,1)S(1)} %get-tuple-element.6.y_v, bf16[4,4096,128]{2,1,0:T(8,128)(2,1)S(1)} %get-tuple-element.7.k_v, bf16[4,4096,128]{2,1,0:T(8,128)(2,1)S(1)} %get-tuple-element.8.v_v), custom_call_target="tpu_custom_call" | custom-call | tf_op jit(solution)/shard_map/store/pallas_call | solution.py:582
